TPU v7x, 512 devices: a whole 4x4x16 slice. The times are simulated.
512 devices in a mesh: dp: 64 (over z, x), vocab: 8 (over y, core).
Axes of the slice: x: 4, y: 4, z: 16, core: 2. Of those that a mesh axis runs over, the one named last changes fastest.
Arguments:
- tokens: int32 [576, 512], P('dp'), may hold values from 0 to 32127
- span_bounds: int32 [576, 16, 2], P('dp'), may hold values from 1 to 512, as said below
- owner: int32 [576, 80, 1], P('dp'), may hold values from 0 to 63; in each aligned block of 720 rows (0 to 719, 720 to 1439, ..., all dimensions but the last counted through in order) at most 12 rows name the same one
- decoder_states: bfloat16 [576, 80, 1024], P('dp', None, 'vocab'), may hold values from -1024 to 1024
- norm_gain: bfloat16 [1024], replicated, may hold values from 0.25 to 1.75
- embedding: bfloat16 [32128, 1024], P('vocab', 'dp'), may hold values from -64 to 64
Outputs:
- losses: float32 [49152], P('dp')
Inputs may be any that keep to these rules, and one draw needn't show every extreme that they name: `span_bounds`: within a sequence the 16 spans are disjoint and in increasing order, each with span_end - span_start from 1 to 5; every sequence has a span of exactly 5. Among the slots of one dp device no owner is named more than 12 times; in some of those blocks an owner is named exactly 12 times.
All inputs are finite; a program needn't handle non-finite values.
Results may differ from a plain program's by a relative error of at most 0.00047.
Values may be sent and summed in bfloat16 or wider, within the bound.
No kernel may reach another device: no remote copies, remote signals or barrier semaphores. Data moves between devices by JAX's collectives and lax.ppermute only.
A program may use at most 64 MiB of HBM per device.

v0:
```python
import jax
import jax.numpy as jnp
from jax import lax
from jax.sharding import Mesh
from jax.sharding import PartitionSpec as P

MAXSPAN = 5
OWN_ROWS = 768
DP = ("dp_0", "dp_1")


epsilon = 1e-06


def from_everyone(value, axis):
    copies = jnp.broadcast_to(value, (lax.axis_size(axis), *value.shape))
    return lax.all_to_all(copies, axis, split_axis=0, concat_axis=0, tiled=True)


def laid_out(tiles, dim):
    tiles = jnp.moveaxis(tiles, 0, dim)
    shape = tiles.shape
    return tiles.reshape(*shape[:dim], shape[dim] * shape[dim + 1], *shape[dim + 2 :])


def gathered_copies(value, axis, dim):
    tiles = from_everyone(value, axis)
    return laid_out(tiles, dim)


def gathered_by_axis(value, axes, dim):
    result = value
    for number in range(len(axes) - 1, -1, -1):
        result = lax.all_gather(result, axes[number], axis=dim, tiled=True)
    return result


def collected_together(value, axis):
    leaves = jax.tree.leaves(value)
    order = sorted(range(len(leaves)), key=lambda k: -leaves[k].size)
    width = (1, *leaves[order[0]].shape)[-1]
    lines = [
        jnp.pad(leaves[k].reshape(-1), (0, -leaves[k].size % width)).reshape(-1, width)
        for k in order
    ]
    both, at, found = (from_everyone(jnp.concatenate(lines), axis), 0, {})
    for k, line in zip(order, lines):
        share = both[:, at : at + len(line)].reshape(len(both), -1)
        found[k] = share[:, : leaves[k].size].reshape(-1, *leaves[k].shape)
        at += len(line)
    numbers = iter(range(len(leaves)))
    return jax.tree.map(lambda _: found[next(numbers)], value)


def combined_pairwise(pieces, combine):
    while len(jax.tree.leaves(pieces)[0]) > 1:
        pieces = jax.vmap(combine)(
            *(jax.tree.map(lambda part: part[side::2], pieces) for side in (0, 1))
        )
    return jax.tree.map(lambda part: part[0], pieces)


def joined_all(value, axis, combine):
    pieces = collected_together(value, axis)
    return combined_pairwise(pieces, combine)


def normalize(rows, norm_gain):
    values = rows.astype(jnp.float32)
    mean_square = jnp.mean(values * values, axis=1, keepdims=True)
    scaled = (
        values
        * lax.rsqrt(mean_square + epsilon)
        * norm_gain.astype(jnp.float32)
        * values.shape[1] ** (-0.5)
    )
    return scaled.astype(jnp.bfloat16)


def combine_stats(left_stats, right_stats):
    row_top = jnp.maximum(left_stats[0], right_stats[0])
    exp_total = left_stats[1] * jnp.exp(left_stats[0] - row_top) + right_stats[1] * jnp.exp(
        right_stats[0] - row_top
    )
    return (row_top, exp_total, left_stats[2] + right_stats[2])


def on_device(tokens, span_bounds, owner, decoder_states, norm_gain, embedding):
    seq_count, slot_count, local_width = decoder_states.shape
    owner_total = lax.axis_size(DP)
    capacity = OWN_ROWS // owner_total
    slot_ids = jnp.arange(slot_count, dtype=jnp.int32)
    offsets = slot_ids % MAXSPAN
    starts = jnp.repeat(span_bounds[:, :, 0], MAXSPAN, axis=1)
    span_ends = jnp.repeat(span_bounds[:, :, 1], MAXSPAN, axis=1)
    is_live = (offsets[None, :] < span_ends - starts).reshape(-1)
    positions = jnp.minimum(starts + offsets[None, :], tokens.shape[1] - 1)
    labels = jnp.take_along_axis(tokens, positions, axis=1).reshape(-1)
    targets = owner.reshape(-1)
    slot_total = targets.shape[0]
    owner_hits = (targets[:, None] == jnp.arange(owner_total, dtype=jnp.int32)[None, :]).astype(
        jnp.bfloat16
    )
    device_slots = jnp.arange(slot_total, dtype=jnp.int32)
    earlier = (device_slots[:, None] > device_slots[None, :]).astype(jnp.bfloat16)
    running = jnp.dot(earlier, owner_hits, preferred_element_type=jnp.float32)
    slot_rank = jnp.sum(running * owner_hits.astype(jnp.float32), axis=1).astype(jnp.int32)
    target_row = targets * capacity + slot_rank
    placing = (target_row[None, :] == jnp.arange(OWN_ROWS, dtype=jnp.int32)[:, None]) & is_live[
        None, :
    ]
    sent_labels = jnp.sum(jnp.where(placing, labels[None, :] + 1, 0), axis=1) - 1
    onehot = placing.astype(jnp.bfloat16)
    states = decoder_states.reshape(slot_total, local_width)
    packed = jnp.dot(onehot, states, preferred_element_type=jnp.float32).astype(jnp.bfloat16)
    arrived, row_labels = (
        lax.all_to_all(
            packed.reshape(owner_total, capacity, local_width),
            DP,
            split_axis=0,
            concat_axis=0,
            tiled=True,
        ),
        lax.all_to_all(
            sent_labels.reshape(owner_total, capacity), DP, split_axis=0, concat_axis=0, tiled=True
        ),
    )
    full_rows = gathered_copies(arrived.reshape(OWN_ROWS, local_width), "vocab", 1)
    normed = normalize(full_rows, norm_gain)
    row_labels = row_labels.reshape(OWN_ROWS)
    vocab_rows = gathered_by_axis(embedding, DP, 1)
    logits = lax.dot_general(
        normed, vocab_rows, (((1,), (1,)), ((), ())), preferred_element_type=jnp.float32
    )
    shard_rows = vocab_rows.shape[0]
    local_label = row_labels - lax.axis_index("vocab") * shard_rows
    picked = jnp.sum(
        jnp.where(
            jnp.arange(shard_rows, dtype=jnp.int32)[None, :] == local_label[:, None], logits, 0.0
        ),
        axis=1,
    )
    local_top = jnp.max(logits, axis=1)
    local_total = jnp.sum(jnp.exp(logits - local_top[:, None]), axis=1)
    row_top, exp_total, label_logit = joined_all(
        (local_top, local_total, picked), "vocab", combine_stats
    )
    row_loss = row_top + jnp.log(exp_total) - label_logit
    return jnp.where(row_labels >= 0, row_loss, 0.0).astype(jnp.float32)


def solution(mesh):
    torus = Mesh(mesh.devices.reshape(16, 4, mesh.shape["vocab"]), ("dp_0", "dp_1", "vocab"))
    in_specs = (
        P(DP, None),
        P(DP, None, None),
        P(DP, None, None),
        P(DP, None, "vocab"),
        P(),
        P("vocab", DP),
    )
    out_specs = P(DP)
    return jax.shard_map(
        on_device, mesh=torus, in_specs=in_specs, out_specs=out_specs, check_vma=False
    )
```

profile of v0, /device:TPU:1, one launch (start us, length us, event | category | flops | bytes accessed | tf_op | source)
XLA Modules:
  0.0 174.0 jit_solution(15740770812736156887)
XLA Ops:
  6.5 0.0 copy-start
  6.5 0.0 copy-start.1
  6.5 0.0 all-gather.2.cloned.1.call-start
  6.5 13.4 %all_gather.6 = bf16[4016,64]{0,1:T(8,128)(2,1)} all-gather(bf16[4016,16]{0,1:T(8,128)(2,1)} %param.11), channel_id=1, replica_groups=mesh['dp_0'=16,'dp_1'=4,'vocab'=8] {'dp_1'}, dimensions={1}, use_global_device_ids=true | all-gather | bytes 642560 | tf_op jit(solution)/shard_map/all_gather | solution.py:34
  20.0 0.0 all-gather.2.cloned.1.call-update
  20.0 0.1 lt.58
  20.1 0.7 reduce.2
  20.8 0.1 reshape.199
  20.9 0.8 fusion.24
  21.7 0.1 broadcast_in_dim.49
  21.7 0.2 reshape.201
  22.0 0.1 broadcast_in_dim.48
  22.0 0.2 reshape.200
  22.2 0.4 fusion.11
  22.7 0.0 copy-done
  22.7 1.0 fusion.7
  23.7 0.8 reshape.204
  24.5 16.5 %all-to-all-start.1 = ((bf16[64,12,128]{2,1,0:T(8,128)(2,1)}), bf16[64,12,128]{2,1,0:T(8,128)(2,1)S(1)}, u32[]{:S(2)}, u32[]{:S(2)}) async-start(bf16[64,12,128]{2,1,0:T(8,128)(2,1)} %reshape.204), calls=%async_computation.1 | async-start | bytes 524288 | tf_op jit(solution)/shard_map/all_to_all | solution.py:117
  40.9 0.1 reshape.202
  41.1 0.1 lt.61
  41.1 0.1 reshape.213
  41.2 0.0 copy-done.1
  41.2 9.9 %gather_fusion = s32[720]{0:T(1024)S(1)} fusion(s32[9,512]{1,0:T(8,128)S(1)} %copy-done.1, s32[720]{0:T(1024)S(1)} %reshape.213), kind=kCustom, calls=%fused_computation | custom fusion | bytes 11520 | tf_op jit(solution)/shard_map/jit(take_along_axis)/gather | solution.py:98
  51.2 0.0 copy-start.2
  51.2 0.7 select_reduce_fusion.1
  51.9 0.7 sub.60
  52.6 8.6 %all-to-all-done.1 = bf16[64,12,128]{2,1,0:T(8,128)(2,1)S(1)} async-done(((bf16[64,12,128]{2,1,0:T(8,128)(2,1)}), bf16[64,12,128]{2,1,0:T(8,128)(2,1)S(1)}, u32[]{:S(2)}, u32[]{:S(2)}) %all-to-all-start.1) | async-done | bytes 196640 | tf_op jit(solution)/shard_map/all_to_all | solution.py:117
  61.1 7.5 %all-to-all-start = ((s32[64,1,12]{2,1,0:T(1,128)}), s32[64,1,12]{2,1,0:T(1,128)S(1)}, u32[]{:S(2)}, u32[]{:S(2)}) async-start(s32[64,1,12]{2,1,0:T(1,128)} %bitcast.2), calls=%async_computation | async-start | bytes 65536 | tf_op jit(solution)/shard_map/all_to_all | solution.py:124
  68.7 0.1 copy.23
  68.9 13.9 %all-to-all-done = s32[64,1,12]{2,1,0:T(1,128)S(1)} async-done(((s32[64,1,12]{2,1,0:T(1,128)}), s32[64,1,12]{2,1,0:T(1,128)S(1)}, u32[]{:S(2)}, u32[]{:S(2)}) %all-to-all-start) | async-done | bytes 3104 | tf_op jit(solution)/shard_map/all_to_all | solution.py:124
  82.8 1.3 broadcast_in_dim.53
  84.1 9.7 %all-to-all-start.2 = ((bf16[8,768,128]{1,2,0:T(8,128)(2,1)}), bf16[8,768,128]{1,2,0:T(8,128)(2,1)S(1)}, u32[]{:S(2)}, u32[]{:S(2)}) async-start(bf16[8,768,128]{1,2,0:T(8,128)(2,1)} %broadcast_in_dim.53), calls=%async_computation.2 | async-start | bytes 3145728 | tf_op jit(solution)/shard_map/all_to_all | solution.py:17
  93.8 0.0 copy-done.2
  93.8 0.1 subtract_reduce_fusion
  93.9 0.1 sub.65
  94.0 20.4 %all-to-all-done.2 = bf16[8,768,128]{1,2,0:T(8,128)(2,1)S(1)} async-done(((bf16[8,768,128]{1,2,0:T(8,128)(2,1)}), bf16[8,768,128]{1,2,0:T(8,128)(2,1)S(1)}, u32[]{:S(2)}, u32[]{:S(2)}) %all-to-all-start.2) | async-done | bytes 1572896 | tf_op jit(solution)/shard_map/all_to_all | solution.py:17
  114.4 0.4 multiply_reduce_fusion
  114.8 0.5 fusion.2
  115.3 27.0 %all-gather.2.cloned.1.call-done = bf16[4016,1024]{0,1:T(8,128)(2,1)} async-done(((bf16[4016,64]{0,1:T(8,128)(2,1)}), bf16[4016,1024]{0,1:T(8,128)(2,1)}) %all-gather.2.cloned.1.call-update) | async-done | bytes 8224784 | tf_op jit(solution)/shard_map/all_gather | solution.py:34
  142.2 9.9 %fusion.25 = (f32[768]{0:T(1024)S(1)}, f32[768,4016]{0,1:T(8,128)S(1)}) fusion(bf16[768,1024]{0,1:T(8,128)(2,1)S(1)} %fusion.2, bf16[4016,1024]{0,1:T(8,128)(2,1)} %all-gather.2.cloned.1.call-done), kind=kOutput, calls=%fused_computation.56 | convolution fusion | flops 6319705088 | bytes 22137856 | tf_op jit(solution)/shard_map/dot_general | solution.py:132
  152.1 3.3 %exponential_reduce_fusion = (f32[768]{0:T(1024)S(1)}, f32[768]{0:T(1024)S(1)}) fusion(f32[768,4016]{0,1:T(8,128)S(1)} %get-tuple-element.17, f32[768]{0:T(1024)S(1)} %get-tuple-element.16, s32[768]{0:T(1024)S(1)} %sub.65), kind=kLoop, calls=%fused_computation.3 | loop fusion | flops 15419904 | bytes 12349440 | tf_op jit(solution)/shard_map/reduce_sum | solution.py:144
  155.5 0.6 broadcast_in_dim.55
  156.1 5.0 %all-to-all-start.3 = ((f32[8,3,768]{2,1,0:T(4,128)}), f32[8,3,768]{2,1,0:T(4,128)S(1)}, u32[]{:S(2)}, u32[]{:S(2)}) async-start(f32[8,3,768]{2,1,0:T(4,128)} %broadcast_in_dim.55), calls=%async_computation.3 | async-start | bytes 196608 | tf_op jit(solution)/shard_map/all_to_all | solution.py:17
  161.1 0.1 compare_reduce_fusion
  161.2 0.1 ge.26
  161.3 4.8 %all-to-all-done.3 = f32[8,3,768]{2,1,0:T(4,128)S(1)} async-done(((f32[8,3,768]{2,1,0:T(4,128)}), f32[8,3,768]{2,1,0:T(4,128)S(1)}, u32[]{:S(2)}, u32[]{:S(2)}) %all-to-all-start.3) | async-done | bytes 73760 | tf_op jit(solution)/shard_map/all_to_all | solution.py:17
  166.1 0.1 fusion.23
  166.6 0.6 broadcast_select_fusion
  (36 shorter events, 0.6 us)
Async XLA Ops:
  6.5 16.1 %copy-start = (bf16[9,80,128]{2,1,0:T(8,128)(2,1)S(1)}, bf16[9,80,128]{2,1,0:T(8,128)(2,1)}, u32[]{:S(2)}) copy-start(bf16[9,80,128]{2,1,0:T(8,128)(2,1)} %param.9) | copy-start | bytes 552964
  6.5 34.7 %copy-start.1 = (s32[9,512]{1,0:T(8,128)S(1)}, s32[9,512]{1,0:T(8,128)}, u32[]{:S(2)}) copy-start(s32[9,512]{1,0:T(8,128)} %param.6) | copy-start | bytes 55300
  6.5 135.7 %all-gather.2.cloned.1.call-start = ((), (), s32[]{:S(2)}) async-start(), calls=%async_computation.4 | async-start | bytes 8912896 | tf_op jit(solution)/shard_map/all_gather | solution.py:34
  24.5 36.7 %all-to-all-start.1 = ((bf16[64,12,128]{2,1,0:T(8,128)(2,1)}), bf16[64,12,128]{2,1,0:T(8,128)(2,1)S(1)}, u32[]{:S(2)}, u32[]{:S(2)}) async-start(bf16[64,12,128]{2,1,0:T(8,128)(2,1)} %reshape.204), calls=%async_computation.1 | async-start | bytes 524288 | tf_op jit(solution)/shard_map/all_to_all | solution.py:117
  51.2 42.6 %copy-start.2 = (bf16[1024]{0:T(1024)(128)(2,1)S(1)}, bf16[1024]{0:T(1024)(128)(2,1)}, u32[]{:S(2)}) copy-start(bf16[1024]{0:T(1024)(128)(2,1)} %param.10) | copy-start | bytes 6148
  61.1 21.6 %all-to-all-start = ((s32[64,1,12]{2,1,0:T(1,128)}), s32[64,1,12]{2,1,0:T(1,128)S(1)}, u32[]{:S(2)}, u32[]{:S(2)}) async-start(s32[64,1,12]{2,1,0:T(1,128)} %bitcast.2), calls=%async_computation | async-start | bytes 65536 | tf_op jit(solution)/shard_map/all_to_all | solution.py:124
  84.1 30.3 %all-to-all-start.2 = ((bf16[8,768,128]{1,2,0:T(8,128)(2,1)}), bf16[8,768,128]{1,2,0:T(8,128)(2,1)S(1)}, u32[]{:S(2)}, u32[]{:S(2)}) async-start(bf16[8,768,128]{1,2,0:T(8,128)(2,1)} %broadcast_in_dim.53), calls=%async_computation.2 | async-start | bytes 3145728 | tf_op jit(solution)/shard_map/all_to_all | solution.py:17
  156.1 10.0 %all-to-all-start.3 = ((f32[8,3,768]{2,1,0:T(4,128)}), f32[8,3,768]{2,1,0:T(4,128)S(1)}, u32[]{:S(2)}, u32[]{:S(2)}) async-start(f32[8,3,768]{2,1,0:T(4,128)} %broadcast_in_dim.55), calls=%async_computation.3 | async-start | bytes 196608 | tf_op jit(solution)/shard_map/all_to_all | solution.py:17
Sparse Core Ops, SparseCore 0:
  20.1 122.1 all-gather.1
where the time goes:
time: 175 us; the launch traced here: 174 us
  waiting for transfers between devices  74.6 us (43%)
  starting transfers between devices  38.6 us (22%)
  local copies, waits for them, and re-layouts  15.9 us (9%)
  between operations  13.7 us (8%)
  blocking collectives  13.4 us (8%)
  matrix products  11.3 us (6%)
  other arithmetic  6.47 us (4%)
    all_gather x1, waiting for transfers between devices, gathered_by_axis(): result = lax.all_gather(result, axes[number], axis=dim, tiled=True)  27 us
    all_to_all x2, waiting for transfers between devices, from_everyone(): return lax.all_to_all(copies, axis, split_axis=0, concat_axis=0, tiled=True)  25.1 us
    all_to_all x1, starting transfers between devices, on_device(): lax.all_to_all(packed.reshape(owner_total, capacity, local_width), DP, sp...  16.5 us
    all_to_all x2, starting transfers between devices, from_everyone(): return lax.all_to_all(copies, axis, split_axis=0, concat_axis=0, tiled=True)  14.7 us
    all_to_all x1, waiting for transfers between devices, on_device(): lax.all_to_all(sent_labels.reshape(owner_total, capacity), DP, split_axis...  13.9 us
    all_gather x1, blocking collectives, gathered_by_axis(): result = lax.all_gather(result, axes[number], axis=dim, tiled=True)  13.4 us
    gather x2, local copies, waits for them, and re-layouts, on_device(): labels = jnp.take_along_axis(tokens, positions, axis=1).reshape(-1)  10 us
    dot_general x1, matrix products, on_device(): lax.dot_general(normed, vocab_rows, (((1,), (1,)), ((), ())), preferred_e...  9.88 us
  transfers between devices with their start and end apart: 5, of which 5 were waited for; matrix products, arithmetic and copies ran while one was open for 11% of the time, Pallas kernels for 0%

commit v1 on v0

v1 whole, which is shorter than its diff:
```python
import jax
import jax.numpy as jnp
from jax import lax
from jax.experimental import pallas as pl
from jax.experimental.pallas import tpu as pltpu
from jax.sharding import Mesh
from jax.sharding import PartitionSpec as P

MAXSPAN = 5
OWN_ROWS = 768
DP = ("z", "x")
VOC = ("y", "c")
PLANE = ("x", "y", "c")

epsilon = 1e-06


ROW_BLOCK = 256
MATMUL_ROWS = 512
LANES = 128


def broadcast_all(value, axis):
    copies = jnp.broadcast_to(value, (lax.axis_size(axis), *value.shape))
    return lax.all_to_all(copies, axis, split_axis=0, concat_axis=0, tiled=True)


def swap_cores(value):
    return lax.ppermute(value, "c", [(0, 1), (1, 0)])


def part_width(rows, parts):
    return -(-rows // (parts * LANES)) * LANES


def exchanged_embedding(embedding):
    parts = lax.axis_size("x")
    local = embedding.T
    width, rows = local.shape
    part = part_width(rows, parts)
    local = jnp.pad(local, ((0, 0), (0, part * parts - rows)))
    split = jnp.stack([local[:, k * part : (k + 1) * part] for k in range(parts)])
    mixed = lax.all_to_all(split, "x", split_axis=0, concat_axis=0, tiled=True)
    return mixed.reshape(parts * width, part)


def packed_rows(tokens, span_bounds, owner, decoder_states):
    seq_count, slot_count, local_width = decoder_states.shape
    planes, columns = lax.axis_size("z"), lax.axis_size("x")
    owner_total = planes * columns
    capacity = OWN_ROWS // owner_total
    slot_ids = jnp.arange(slot_count, dtype=jnp.int32)
    offsets = slot_ids % MAXSPAN
    starts = jnp.repeat(span_bounds[:, :, 0], MAXSPAN, axis=1)
    span_ends = jnp.repeat(span_bounds[:, :, 1], MAXSPAN, axis=1)
    is_live = (offsets[None, :] < span_ends - starts).reshape(-1)
    length = tokens.shape[1]
    positions = jnp.minimum(starts + offsets[None, :], length - 1)
    places = jnp.arange(length, dtype=jnp.int32)
    labels = jnp.sum(
        jnp.where(places[None, None, :] == positions[:, :, None], tokens[:, None, :], 0), axis=2
    ).reshape(-1)
    targets = owner.reshape(-1)
    slot_total = targets.shape[0]
    owner_hits = (targets[:, None] == jnp.arange(owner_total, dtype=jnp.int32)[None, :]).astype(
        jnp.bfloat16
    )
    device_slots = jnp.arange(slot_total, dtype=jnp.int32)
    earlier = (device_slots[:, None] > device_slots[None, :]).astype(jnp.bfloat16)
    running = jnp.dot(earlier, owner_hits, preferred_element_type=jnp.float32)
    slot_rank = jnp.sum(running * owner_hits.astype(jnp.float32), axis=1).astype(jnp.int32)
    place = (targets % columns) * planes + targets // columns
    target_row = place * capacity + slot_rank
    placing = (target_row[None, :] == jnp.arange(OWN_ROWS, dtype=jnp.int32)[:, None]) & is_live[
        None, :
    ]
    sent_labels = jnp.sum(jnp.where(placing, labels[None, :] + 1, 0), axis=1)
    onehot = placing.astype(jnp.bfloat16)
    states = decoder_states.reshape(slot_total, local_width)
    packed = jnp.dot(onehot, states, preferred_element_type=jnp.float32).astype(jnp.bfloat16)
    return packed, sent_labels


def normalize_block(core_ref, near_ref, far_ref, gain_ref, out_ref):
    first = core_ref[0] == 0
    pieces = []
    for k in range(near_ref.shape[1]):
        near = near_ref[0, k].astype(jnp.float32)
        far = far_ref[0, k].astype(jnp.float32)
        pieces += [jnp.where(first, near, far), jnp.where(first, far, near)]
    squares = pieces[0] * pieces[0]
    for piece in pieces[1:]:
        squares = squares + piece * piece
    width = len(pieces) * LANES
    mean_square = jnp.sum(squares, axis=1, keepdims=True) / width
    scale = lax.rsqrt(mean_square + epsilon)
    for k, piece in enumerate(pieces):
        gain = gain_ref[0:1, k * LANES : (k + 1) * LANES]
        out_ref[:, k * LANES : (k + 1) * LANES] = (
            piece * scale * gain * width ** (-0.5)
        ).astype(jnp.bfloat16)


def normalized(near, far, norm_gain):
    columns, slices = near.shape[:2]
    blocks = OWN_ROWS // ROW_BLOCK
    width = slices * 2 * LANES
    core = lax.axis_index("c").reshape(1)
    gain = norm_gain.astype(jnp.float32).reshape(1, width)
    spec = pl.BlockSpec((1, slices, ROW_BLOCK, LANES), lambda x, i, core: (x, 0, i, 0))
    return pl.pallas_call(
        normalize_block,
        grid_spec=pltpu.PrefetchScalarGridSpec(
            num_scalar_prefetch=1,
            grid=(columns, blocks),
            in_specs=[spec, spec, pl.BlockSpec((1, width), lambda x, i, core: (0, 0))],
            out_specs=pl.BlockSpec((ROW_BLOCK, width), lambda x, i, core: (x * blocks + i, 0)),
        ),
        out_shape=jax.ShapeDtypeStruct((columns * OWN_ROWS, width), jnp.bfloat16),
        name="normalized",
    )(core, near, far, gain)


def stats_block(valid_ref, rows_ref, weights_ref, labels_ref, out_ref):
    rows = rows_ref.shape[0]
    logits = jnp.dot(rows_ref[...], weights_ref[...], preferred_element_type=jnp.float32)
    columns = lax.broadcasted_iota(jnp.int32, logits.shape, 1)
    logits = jnp.where(columns < valid_ref[0], logits, -jnp.inf)
    top = jnp.max(logits, axis=1, keepdims=True)
    total = jnp.sum(jnp.exp(logits - top), axis=1, keepdims=True)
    label = jnp.broadcast_to(labels_ref[0:1, :], (LANES, rows)).T[:, 0:1]
    picked = jnp.sum(jnp.where(columns == label, logits, 0.0), axis=1, keepdims=True)
    lane = lax.broadcasted_iota(jnp.int32, (rows, LANES), 1)
    both = jnp.where(lane == 0, top + jnp.log(total), picked)
    out_ref[...] = both.T[0:8]


def row_stats(rows, weights, labels, valid):
    total, width = rows.shape
    part = weights.shape[1]
    stats = pl.pallas_call(
        stats_block,
        grid_spec=pltpu.PrefetchScalarGridSpec(
            num_scalar_prefetch=1,
            grid=(total // MATMUL_ROWS,),
            in_specs=[
                pl.BlockSpec((MATMUL_ROWS, width), lambda i, valid: (i, 0)),
                pl.BlockSpec((width, part), lambda i, valid: (0, 0)),
                pl.BlockSpec((1, MATMUL_ROWS), lambda i, valid: (0, i)),
            ],
            out_specs=pl.BlockSpec((8, MATMUL_ROWS), lambda i, valid: (0, i)),
        ),
        out_shape=jax.ShapeDtypeStruct((8, total), jnp.float32),
        name="row_stats",
    )(valid.reshape(1), rows, weights, labels.reshape(1, total))
    return stats[:2]


def on_device(tokens, span_bounds, owner, decoder_states, norm_gain, embedding):
    planes, columns = lax.axis_size("z"), lax.axis_size("x")
    capacity = OWN_ROWS // (planes * columns)
    shard_rows = embedding.shape[0]
    mixed = exchanged_embedding(embedding)
    mixed, tokens, span_bounds, owner, decoder_states = lax.optimization_barrier(
        (mixed, tokens, span_bounds, owner, decoder_states)
    )
    weights = lax.all_gather(mixed, "z", axis=0, tiled=True)
    packed, sent_labels = packed_rows(tokens, span_bounds, owner, decoder_states)
    digits = jnp.stack([sent_labels // 256, sent_labels % 256]).astype(jnp.bfloat16)
    digits = digits.reshape(-1, LANES)
    digits = jnp.pad(digits, ((0, -digits.shape[0] % 16), (0, 0)))
    bundle = jnp.concatenate([packed, digits], axis=0)
    near = broadcast_all(bundle, ("x", "y"))
    far = swap_cores(near)
    near = near.reshape(columns, -1, *bundle.shape)
    far = far.reshape(near.shape)
    tags = near[:, 0, OWN_ROWS : OWN_ROWS + 2 * OWN_ROWS // LANES].astype(jnp.int32)
    tags = tags.reshape(columns, 2, OWN_ROWS)
    row_labels = tags[:, 0] * 256 + tags[:, 1] - 1
    part = mixed.shape[1]
    here = lax.axis_index("x")
    valid = jnp.minimum(shard_rows - here * part, part)
    local_label = row_labels - (lax.axis_index(VOC) * shard_rows + here * part)
    local_label = jnp.where((local_label >= 0) & (local_label < valid), local_label, -1)
    rows = normalized(near, far, norm_gain)
    stats = row_stats(rows, weights, local_label.reshape(-1), valid)
    group = planes * capacity
    stats = stats.reshape(2, columns, columns, group).transpose(2, 0, 1, 3)
    stats = stats.reshape(columns, 1, 2, OWN_ROWS)
    copies = jnp.broadcast_to(stats, (columns, lax.axis_size(VOC), 2, OWN_ROWS))
    copies = copies.reshape(-1, 2, OWN_ROWS)
    parts = lax.all_to_all(copies, PLANE, split_axis=0, concat_axis=0, tiled=True)
    row_top = jnp.max(parts[:, 0], axis=0)
    row_loss = row_top + jnp.log(jnp.sum(jnp.exp(parts[:, 0] - row_top[None]), axis=0))
    row_loss = row_loss - jnp.sum(parts[:, 1], axis=0)
    mine = row_labels.reshape(columns, columns, group)
    mine = lax.dynamic_index_in_dim(mine, here, axis=1, keepdims=False).reshape(-1)
    sent = jnp.where(mine >= 0, row_loss, 0.0).astype(jnp.float32)
    sent = sent.reshape(columns, planes, capacity).swapaxes(0, 1).reshape(planes, -1)
    return lax.all_to_all(sent, "z", split_axis=0, concat_axis=0, tiled=True).reshape(-1)


def solution(mesh):
    dp, vocab = mesh.shape["dp"], mesh.shape["vocab"]
    torus = Mesh(mesh.devices.reshape(dp // 4, 4, vocab // 2, 2), ("z", "x", "y", "c"))
    in_specs = (
        P(DP, None),
        P(DP, None, None),
        P(DP, None, None),
        P(DP, None, VOC),
        P(),
        P(VOC, DP),
    )
    return jax.shard_map(
        on_device, mesh=torus, in_specs=in_specs, out_specs=P(DP), check_vma=False
    )
```

time: 175 us -> 172 us (0.983)
  Pallas kernels: 0 us -> 24.4 us
  matrix products: 11.3 us -> 1.41 us
  waiting for transfers between devices: 74.6 us -> 65.4 us
  local copies, waits for them, and re-layouts: 15.9 us -> 7.79 us
  blocking collectives: 13.4 us -> 18.5 us
  starting transfers between devices: 38.6 us -> 34.9 us
    pallas_call x0 -> x2, Pallas kernels: none -> 24.4 us  [the longest x1 13.8 us: row_stats(): pl.pallas_call(stats_block, grid_spec=pltpu.PrefetchScalarGridSpec(num_sc...]
    all_to_all x0 -> x1, blocking collectives: none -> 18.5 us  [on_device(): lax.all_to_all(sent, 'z', split_axis=0, concat_axis=0, tiled=True)]
    all_gather x1, waiting for transfers between devices: 27 us -> 12.1 us  [on_device(): weights = lax.all_gather(mixed, 'z', axis=0, tiled=True)]
    all_gather x1 -> x0, blocking collectives: 13.4 us -> none  [gathered_by_axis(): result = lax.all_gather(result, axes[number], axis=dim, tiled=True)]
    all_to_all x4 -> x3, starting transfers between devices: 38.6 us -> 26.3 us  [the longest x1 16.5 us: on_device(): lax.all_to_all(copies, PLANE, split_axis=0, concat_axis=0, tiled=True)]
    gather x2 -> x0, local copies, waits for them, and re-layouts: 10 us -> none  [on_device(): labels = jnp.take_along_axis(tokens, positions, axis=1).reshape(-1)]
    dot_general x3 -> x2, matrix products: 11.3 us -> 1.41 us  [the longest x1 1.03 us: packed_rows(): jnp.dot(onehot, states, preferred_element_type=jnp.float32)]
    ppermute x0 -> x1, starting transfers between devices: none -> 8.48 us  [swap_cores(): return lax.ppermute(value, 'c', [(0, 1), (1, 0)])]
  transfers between devices with their start and end apart: 5 -> 5, of which waited for: 5 -> 5; matrix products, arithmetic and copies ran while one was open for 11% -> 1% of each run, Pallas kernels for 0% -> 6%
where the time goes in v1:
time: 172 us; the launch traced here: 171 us
  waiting for transfers between devices  65.4 us (38%)
  starting transfers between devices  34.9 us (20%)
  Pallas kernels  24.4 us (14%)
  blocking collectives  18.5 us (11%)
  between operations  13.6 us (8%)
  local copies, waits for them, and re-layouts  7.79 us (5%)
  other arithmetic  5.51 us (3%)
    all_to_all x1, waiting for transfers between devices, broadcast_all(): return lax.all_to_all(copies, axis, split_axis=0, concat_axis=0, tiled=True)  35.6 us
    all_to_all x1, blocking collectives, on_device(): lax.all_to_all(sent, 'z', split_axis=0, concat_axis=0, tiled=True)  18.5 us
    all_to_all x1, starting transfers between devices, on_device(): lax.all_to_all(copies, PLANE, split_axis=0, concat_axis=0, tiled=True)  16.5 us
    pallas_call x1, Pallas kernels, row_stats(): pl.pallas_call(stats_block, grid_spec=pltpu.PrefetchScalarGridSpec(num_sc...  13.8 us
    all_gather x1, waiting for transfers between devices, on_device(): weights = lax.all_gather(mixed, 'z', axis=0, tiled=True)  12.1 us
    pallas_call x1, Pallas kernels, normalized(): pl.pallas_call(normalize_block, grid_spec=pltpu.PrefetchScalarGridSpec(nu...  10.6 us
    ppermute x1, starting transfers between devices, swap_cores(): return lax.ppermute(value, 'c', [(0, 1), (1, 0)])  8.48 us
    all_to_all x1, waiting for transfers between devices, on_device(): lax.all_to_all(copies, PLANE, split_axis=0, concat_axis=0, tiled=True)  8.19 us
  transfers between devices with their start and end apart: 5, of which 5 were waited for; matrix products, arithmetic and copies ran while one was open for 1% of the time, Pallas kernels for 6%

profile of v1, /device:TPU:1, one launch (start us, length us, event | category | flops | bytes accessed | tf_op | source)
XLA Modules:
  0.0 171.5 jit_solution(16747976667465230051)
XLA Ops:
  6.5 0.0 copy-start
  6.5 0.9 slice_bitcast_fusion.2
  7.4 0.7 pad_maximum_fusion
  8.1 4.8 %all-to-all-start = ((bf16[4,16,1024]{2,1,0:T(8,128)(2,1)}), bf16[4,16,1024]{2,1,0:T(8,128)(2,1)S(1)}, u32[]{:S(2)}, u32[]{:S(2)}) async-start(bf16[4,16,1024]{2,1,0:T(8,128)(2,1)} %pad_maximum_fusion), calls=%async_computation | async-start | bytes 262144 | tf_op jit(solution)/shard_map/all_to_all | solution.py:43
  12.9 0.1 lt.56
  13.0 4.7 %all-to-all-done = bf16[4,16,1024]{2,1,0:T(8,128)(2,1)S(1)} async-done(((bf16[4,16,1024]{2,1,0:T(8,128)(2,1)}), bf16[4,16,1024]{2,1,0:T(8,128)(2,1)S(1)}, u32[]{:S(2)}, u32[]{:S(2)}) %all-to-all-start) | async-done | bytes 131104 | tf_op jit(solution)/shard_map/all_to_all | solution.py:43
  17.7 0.0 copy-start.2
  17.7 0.7 copy.28
  18.4 0.7 reduce.2
  19.1 0.1 reshape.302
  19.2 0.4 fusion.8
  19.6 0.1 broadcast_in_dim.58
  19.7 0.1 reshape.304
  19.8 1.2 select_reduce_fusion.1
  21.0 0.1 add.133
  21.1 0.1 broadcast_in_dim.57
  21.1 0.2 sub.65
  21.4 0.7 select_reduce_fusion
  22.1 0.0 copy-done
  22.1 1.0 fusion.4
  23.2 2.1 %broadcast_in_dim.63 = bf16[16,784,128]{2,1,0:T(8,128)(2,1)} broadcast(bf16[784,128]{1,0:T(8,128)(2,1)S(1)} %fusion.12), dimensions={1,2} | broadcast | bytes 3411968 | tf_op jit(solution)/shard_map/broadcast_in_dim | solution.py:24
  25.3 0.0 copy-done.2
  25.3 0.0 copy-start.3
  25.3 5.0 %all-to-all-start.1 = ((bf16[16,784,128]{2,1,0:T(8,128)(2,1)}), bf16[16,784,128]{2,1,0:T(8,128)(2,1)S(1)}, u32[]{:S(2)}, u32[]{:S(2)}) async-start(bf16[16,784,128]{2,1,0:T(8,128)(2,1)} %broadcast_in_dim.63), calls=%async_computation.1 | async-start | bytes 6422528 | tf_op jit(solution)/shard_map/all_to_all | solution.py:25
  30.3 0.0 all-gather.2.cloned.1.call-start
  30.4 0.7 all-gather.2.cloned.1.call-update
  31.1 35.6 %all-to-all-done.1 = bf16[16,784,128]{2,1,0:T(8,128)(2,1)S(1)} async-done(((bf16[16,784,128]{2,1,0:T(8,128)(2,1)}), bf16[16,784,128]{2,1,0:T(8,128)(2,1)S(1)}, u32[]{:S(2)}, u32[]{:S(2)}) %all-to-all-start.1) | async-done | bytes 3211296 | tf_op jit(solution)/shard_map/all_to_all | solution.py:25
  66.7 0.0 copy-start.1
  66.7 8.5 %collective-permute-start = (bf16[16,784,128]{2,1,0:T(8,128)(2,1)S(1)}, bf16[16,784,128]{2,1,0:T(8,128)(2,1)}, u32[]{:S(2)}, u32[]{:S(2)}) collective-permute-start(bf16[16,784,128]{2,1,0:T(8,128)(2,1)S(1)} %all-to-all-done.1), channel_id=1, source_target_pairs={{0,1},{1,0},{2,3},{3,2},{4,5},{5,4},{6,7},{7,6},{8,9},{9,8},{10,11... | collective-permute-start | bytes 9633800 | tf_op jit(solution)/shard_map/ppermute | solution.py:29
  75.2 0.0 copy-done.3
  75.2 0.6 reshape.315
  75.9 0.1 sub.68
  76.0 0.6 and_select_fusion.labels_ref
  76.6 4.1 %collective-permute-done = bf16[16,784,128]{2,1,0:T(8,128)(2,1)} collective-permute-done((bf16[16,784,128]{2,1,0:T(8,128)(2,1)S(1)}, bf16[16,784,128]{2,1,0:T(8,128)(2,1)}, u32[]{:S(2)}, u32[]{:S(2)}) %collective-permute-start) | collective-permute-done | bytes 3211296 | tf_op jit(solution)/shard_map/ppermute | solution.py:29
  80.7 0.0 copy-done.1
  80.7 10.6 %normalized.1.rows_ref = bf16[3072,1024]{1,0:T(8,128)(2,1)} custom-call(s32[1]{0:T(128)} %bitcast.11.core_ref, bf16[4,4,784,128]{3,2,1,0:T(8,128)(2,1)} %bitcast.43, bf16[4,4,784,128]{3,2,1,0:T(8,128)(2,1)} %bitcast.12.far_ref, f32[1,1024]{1,0:T(1,128)} %bitcast.49), custom_call_target="tpu_custom_call" | custom-call | tf_op jit(solution)/shard_map/normalized/pallas_call | solution.py:111
  91.3 12.1 %all-gather.2.cloned.1.call-done.weights_ref = bf16[1024,1024]{1,0:T(8,128)(2,1)} async-done(((bf16[64,1024]{1,0:T(8,128)(2,1)}), bf16[1024,1024]{1,0:T(8,128)(2,1)}) %all-gather.2.cloned.1.call-update) | async-done | bytes 2097168 | tf_op jit(solution)/shard_map/all_gather | solution.py:167
  103.4 13.8 %row_stats.1 = f32[8,3072]{1,0:T(8,128)} custom-call(s32[1]{0:T(128)} %bitcast.10.valid_ref, bf16[3072,1024]{1,0:T(8,128)(2,1)} %normalized.1.rows_ref, bf16[1024,1024]{1,0:T(8,128)(2,1)} %all-gather.2.cloned.1.call-done.weights_ref, s32[1,3072]{1,0:T(1,128)} %and_select_fusion.labels_ref), custom_call_target="tpu_custom_call" | custom-call | tf_op jit(solution)/shard_map/row_stats/pallas_call | solution.py:141
  117.2 0.9 slice.60
  118.1 0.1 reshape.311
  118.2 0.1 broadcast_in_dim.64
  118.3 0.7 broadcast_in_dim.65
  119.0 16.5 %all-to-all-start.2 = ((f32[32,2,768]{2,1,0:T(2,128)}), f32[32,2,768]{2,1,0:T(2,128)S(1)}, u32[]{:S(2)}, u32[]{:S(2)}) async-start(f32[32,2,768]{2,1,0:T(2,128)} %bitcast.16), calls=%async_computation.2 | async-start | bytes 393216 | tf_op jit(solution)/shard_map/all_to_all | solution.py:192
  135.5 0.1 ge.22
  135.6 8.2 %all-to-all-done.2 = f32[32,2,768]{2,1,0:T(2,128)S(1)} async-done(((f32[32,2,768]{2,1,0:T(2,128)}), f32[32,2,768]{2,1,0:T(2,128)S(1)}, u32[]{:S(2)}, u32[]{:S(2)}) %all-to-all-start.2) | async-done | bytes 196640 | tf_op jit(solution)/shard_map/all_to_all | solution.py:192
  143.8 0.2 slice_reduce_fusion.1
  144.1 0.1 sub.76
  144.2 0.1 all_to_all.18
  144.3 18.5 %all_to_all.24 = f32[16,1,48]{2,1,0:T(1,128)S(1)} all-to-all(f32[16,1,48]{2,1,0:T(1,128)S(1)} %bitcast.48), channel_id=1, replica_groups=mesh['z'=16,'x'=4,'y'=4,'c'=2] {'z'}, dimensions={0} | all-to-all | bytes 6144 | tf_op jit(solution)/shard_map/all_to_all | solution.py:200
  162.8 0.5 broadcast.284
  163.3 0.7 reduce.7
  163.9 0.7 reshape.313
  (23 shorter events, 0.3 us)
Async XLA Ops:
  6.5 15.6 %copy-start = (bf16[9,80,128]{2,1,0:T(8,128)(2,1)S(1)}, bf16[9,80,128]{2,1,0:T(8,128)(2,1)}, u32[]{:S(2)}) copy-start(bf16[9,80,128]{2,1,0:T(8,128)(2,1)} %param.9) | copy-start | bytes 552964
  8.1 9.7 %all-to-all-start = ((bf16[4,16,1024]{2,1,0:T(8,128)(2,1)}), bf16[4,16,1024]{2,1,0:T(8,128)(2,1)S(1)}, u32[]{:S(2)}, u32[]{:S(2)}) async-start(bf16[4,16,1024]{2,1,0:T(8,128)(2,1)} %pad_maximum_fusion), calls=%async_computation | async-start | bytes 262144 | tf_op jit(solution)/shard_map/all_to_all | solution.py:43
  17.7 7.6 %copy-start.2 = (bf16[4,16,1024]{2,1,0:T(8,128)(2,1)}, bf16[4,16,1024]{2,1,0:T(8,128)(2,1)S(1)}, u32[]{:S(2)}) copy-start(bf16[4,16,1024]{2,1,0:T(8,128)(2,1)S(1)} %all-to-all-done) | copy-start | bytes 393220
  25.3 49.9 %copy-start.3 = (bf16[1024]{0:T(1024)(128)(2,1)S(1)}, bf16[1024]{0:T(1024)(128)(2,1)}, u32[]{:S(2)}) copy-start(bf16[1024]{0:T(1024)(128)(2,1)} %param.10) | copy-start | bytes 6148
  25.3 41.4 %all-to-all-start.1 = ((bf16[16,784,128]{2,1,0:T(8,128)(2,1)}), bf16[16,784,128]{2,1,0:T(8,128)(2,1)S(1)}, u32[]{:S(2)}, u32[]{:S(2)}) async-start(bf16[16,784,128]{2,1,0:T(8,128)(2,1)} %broadcast_in_dim.63), calls=%async_computation.1 | async-start | bytes 6422528 | tf_op jit(solution)/shard_map/all_to_all | solution.py:25
  30.3 73.0 %all-gather.2.cloned.1.call-start = ((), (), s32[]{:S(2)}) async-start(), calls=%async_computation.4 | async-start | bytes 2228224 | tf_op jit(solution)/shard_map/all_gather | solution.py:167
  66.7 14.0 %copy-start.1 = (bf16[16,784,128]{2,1,0:T(8,128)(2,1)}, bf16[16,784,128]{2,1,0:T(8,128)(2,1)S(1)}, u32[]{:S(2)}) copy-start(bf16[16,784,128]{2,1,0:T(8,128)(2,1)S(1)} %all-to-all-done.1) | copy-start | bytes 9633796
  66.7 14.0 %collective-permute-start = (bf16[16,784,128]{2,1,0:T(8,128)(2,1)S(1)}, bf16[16,784,128]{2,1,0:T(8,128)(2,1)}, u32[]{:S(2)}, u32[]{:S(2)}) collective-permute-start(bf16[16,784,128]{2,1,0:T(8,128)(2,1)S(1)} %all-to-all-done.1), channel_id=1, source_target_pairs={{0,1},{1,0},{2,3},{3,2},{4,5},{5,4},{6,7},{7,6},{8,9},{9,8},{10,11... | collective-permute-start | bytes 9633800 | tf_op jit(solution)/shard_map/ppermute | solution.py:29
  119.0 24.8 %all-to-all-start.2 = ((f32[32,2,768]{2,1,0:T(2,128)}), f32[32,2,768]{2,1,0:T(2,128)S(1)}, u32[]{:S(2)}, u32[]{:S(2)}) async-start(f32[32,2,768]{2,1,0:T(2,128)} %bitcast.16), calls=%async_computation.2 | async-start | bytes 393216 | tf_op jit(solution)/shard_map/all_to_all | solution.py:192
Sparse Core Ops, SparseCore 0:
  33.2 70.0 all-gather.1

commit v2 on v1

--- a/solution.py
+++ b/solution.py
@@ -1,3 +1,5 @@
+import functools
+
 import jax
 import jax.numpy as jnp
 from jax import lax
@@ -6,11 +8,13 @@
 from jax.sharding import Mesh
 from jax.sharding import PartitionSpec as P
 
+
 MAXSPAN = 5
 OWN_ROWS = 768
 DP = ("z", "x")
 VOC = ("y", "c")
 PLANE = ("x", "y", "c")
+
 
 epsilon = 1e-06
 
@@ -45,7 +49,7 @@
 
 
 def packed_rows(tokens, span_bounds, owner, decoder_states):
-    seq_count, slot_count, local_width = decoder_states.shape
+    _, slot_count, local_width = decoder_states.shape
     planes, columns = lax.axis_size("z"), lax.axis_size("x")
     owner_total = planes * columns
     capacity = OWN_ROWS // owner_total
@@ -121,11 +125,47 @@
     )(core, near, far, gain)
 
 
-def stats_block(valid_ref, rows_ref, weights_ref, labels_ref, out_ref):
+def gathered_blocks(mixed):
+    planes = lax.axis_size("z")
+
+    def shifted(value, step):
+        return lax.ppermute(value, "z", [(k, (k + step) % planes) for k in range(planes)])
+
+    below = shifted(mixed, 5)
+    above = shifted(mixed, -5)
+    three = jnp.concatenate([mixed, below, above], axis=0)
+    half = mixed.shape[0] // 2
+    found = [(three, (0, -5, 5))]
+    for step in (1, -1, 2, -2):
+        found.append((shifted(three, step), (-step, -step - 5, -step + 5)))
+    low = shifted(above[:half], -3)
+    high = shifted(below[half:], 3)
+    return found, (low, high)
+
+
+def stats_block(scalars_ref, rows_ref, labels_ref, *refs, offsets):
+    block_refs, (low_ref, high_ref, out_ref, weights_ref) = refs[: len(offsets)], refs[len(offsets) :]
     rows = rows_ref.shape[0]
+
+    @pl.when(pl.program_id(0) == 0)
+    def _():
+        size = 2 * low_ref.shape[0]
+        planes = weights_ref.shape[0] // size
+
+        def place(offset):
+            plane = (scalars_ref[1] + offset + planes) % planes
+            return pl.multiple_of(plane * size, size)
+
+        for ref, around in zip(block_refs, offsets):
+            for k, offset in enumerate(around):
+                weights_ref[pl.ds(place(offset), size), :] = ref[k * size : (k + 1) * size, :]
+        middle = place(planes // 2)
+        weights_ref[pl.ds(middle, size // 2), :] = low_ref[...]
+        weights_ref[pl.ds(pl.multiple_of(middle + size // 2, size // 2), size // 2), :] = high_ref[...]
+
     logits = jnp.dot(rows_ref[...], weights_ref[...], preferred_element_type=jnp.float32)
     columns = lax.broadcasted_iota(jnp.int32, logits.shape, 1)
-    logits = jnp.where(columns < valid_ref[0], logits, -jnp.inf)
+    logits = jnp.where(columns < scalars_ref[0], logits, -jnp.inf)
     top = jnp.max(logits, axis=1, keepdims=True)
     total = jnp.sum(jnp.exp(logits - top), axis=1, keepdims=True)
     label = jnp.broadcast_to(labels_ref[0:1, :], (LANES, rows)).T[:, 0:1]
@@ -135,28 +175,33 @@
     out_ref[...] = both.T[0:8]
 
 
-def row_stats(rows, weights, labels, valid):
+def row_stats(rows, blocks, labels, valid):
     total, width = rows.shape
-    part = weights.shape[1]
+    found, halves = blocks
+    arrays = [array for array, _ in found] + list(halves)
+    part = arrays[0].shape[1]
+    scalars = jnp.stack([valid, lax.axis_index("z")]).astype(jnp.int32)
+    whole = [pl.BlockSpec(array.shape, lambda i, scalars: (0, 0)) for array in arrays]
     stats = pl.pallas_call(
-        stats_block,
+        functools.partial(stats_block, offsets=tuple(around for _, around in found)),
         grid_spec=pltpu.PrefetchScalarGridSpec(
             num_scalar_prefetch=1,
             grid=(total // MATMUL_ROWS,),
             in_specs=[
-                pl.BlockSpec((MATMUL_ROWS, width), lambda i, valid: (i, 0)),
-                pl.BlockSpec((width, part), lambda i, valid: (0, 0)),
-                pl.BlockSpec((1, MATMUL_ROWS), lambda i, valid: (0, i)),
+                pl.BlockSpec((MATMUL_ROWS, width), lambda i, scalars: (i, 0)),
+                pl.BlockSpec((1, MATMUL_ROWS), lambda i, scalars: (0, i)),
+                *whole,
             ],
-            out_specs=pl.BlockSpec((8, MATMUL_ROWS), lambda i, valid: (0, i)),
+            out_specs=pl.BlockSpec((8, MATMUL_ROWS), lambda i, scalars: (0, i)),
+            scratch_shapes=[pltpu.VMEM((width, part), jnp.bfloat16)],
         ),
         out_shape=jax.ShapeDtypeStruct((8, total), jnp.float32),
         name="row_stats",
-    )(valid.reshape(1), rows, weights, labels.reshape(1, total))
+    )(scalars, rows, labels.reshape(1, total), *arrays)
     return stats[:2]
 
 
-def on_device(tokens, span_bounds, owner, decoder_states, norm_gain, embedding):
+def on_device_body(tokens, span_bounds, owner, decoder_states, norm_gain, embedding):
     planes, columns = lax.axis_size("z"), lax.axis_size("x")
     capacity = OWN_ROWS // (planes * columns)
     shard_rows = embedding.shape[0]
@@ -164,7 +209,7 @@
     mixed, tokens, span_bounds, owner, decoder_states = lax.optimization_barrier(
         (mixed, tokens, span_bounds, owner, decoder_states)
     )
-    weights = lax.all_gather(mixed, "z", axis=0, tiled=True)
+    blocks = gathered_blocks(mixed)
     packed, sent_labels = packed_rows(tokens, span_bounds, owner, decoder_states)
     digits = jnp.stack([sent_labels // 256, sent_labels % 256]).astype(jnp.bfloat16)
     digits = digits.reshape(-1, LANES)
@@ -183,7 +228,7 @@
     local_label = row_labels - (lax.axis_index(VOC) * shard_rows + here * part)
     local_label = jnp.where((local_label >= 0) & (local_label < valid), local_label, -1)
     rows = normalized(near, far, norm_gain)
-    stats = row_stats(rows, weights, local_label.reshape(-1), valid)
+    stats = row_stats(rows, blocks, local_label.reshape(-1), valid)
     group = planes * capacity
     stats = stats.reshape(2, columns, columns, group).transpose(2, 0, 1, 3)
     stats = stats.reshape(columns, 1, 2, OWN_ROWS)
@@ -212,5 +257,5 @@
         P(VOC, DP),
     )
     return jax.shard_map(
-        on_device, mesh=torus, in_specs=in_specs, out_specs=P(DP), check_vma=False
-    )
+        on_device_body, mesh=torus, in_specs=in_specs, out_specs=P(DP), check_vma=False
+    )

time: 172 us -> 197 us (1.15)
  blocking collectives: 18.5 us -> 61.2 us
  waiting for transfers between devices: 65.4 us -> 33.5 us
  starting transfers between devices: 34.9 us -> 57 us
  between operations: 13.6 us -> 0.34 us
  local copies, waits for them, and re-layouts: 7.79 us -> 11.1 us
    all_to_all x1 -> x2, blocking collectives: 18.5 us -> 61.2 us  [the longest x1 40.5 us: broadcast_all(): return lax.all_to_all(copies, axis, split_axis=0, concat_axis=0, tiled=True)]
    ppermute x0 -> x8, starting transfers between devices: none -> 40.8 us  [shifted(): lax.ppermute(value, 'z', [(k, (k + step) % planes) for k in range(planes)])]
    all_to_all x2 -> x1, waiting for transfers between devices: 43.8 us -> 8.3 us  [on_device_body(): lax.all_to_all(copies, PLANE, split_axis=0, concat_axis=0, tiled=True)]
    ppermute x0 -> x8, waiting for transfers between devices: none -> 20.4 us  [shifted(): lax.ppermute(value, 'z', [(k, (k + step) % planes) for k in range(planes)])]
    all_to_all x2 -> x1, starting transfers between devices: 21.5 us -> 4.01 us  [on_device_body(): lax.all_to_all(copies, PLANE, split_axis=0, concat_axis=0, tiled=True)]
    all_gather x1 -> x0, waiting for transfers between devices: 12.1 us -> none  [on_device(): weights = lax.all_gather(mixed, 'z', axis=0, tiled=True)]
    ppermute x1, waiting for transfers between devices: 4.06 us -> 0.01 us  [swap_cores(): return lax.ppermute(value, 'c', [(0, 1), (1, 0)])]
    unnamed x8 -> x10, local copies, waits for them, and re-layouts: 0.02 us -> 2.23 us
  transfers between devices with their start and end apart: 5 -> 11, of which waited for: 5 -> 6; matrix products, arithmetic and copies ran while one was open for 1% -> 4% of each run, Pallas kernels for 6% -> 5%
where the time goes in v2:
time: 197 us; the launch traced here: 196 us
  blocking collectives  61.2 us (31%)
  starting transfers between devices  57 us (29%)
  waiting for transfers between devices  33.5 us (17%)
  Pallas kernels  25.2 us (13%)
  local copies, waits for them, and re-layouts  11.1 us (6%)
  other arithmetic  6.17 us (3%)
    ppermute x8, starting transfers between devices, shifted(): lax.ppermute(value, 'z', [(k, (k + step) % planes) for k in range(planes)])  40.8 us
    all_to_all x1, blocking collectives, broadcast_all(): return lax.all_to_all(copies, axis, split_axis=0, concat_axis=0, tiled=True)  40.5 us
    all_to_all x1, blocking collectives, on_device_body(): lax.all_to_all(sent, 'z', split_axis=0, concat_axis=0, tiled=True)  20.7 us
    ppermute x8, waiting for transfers between devices, shifted(): lax.ppermute(value, 'z', [(k, (k + step) % planes) for k in range(planes)])  20.4 us
    pallas_call x1, Pallas kernels, row_stats(): pl.pallas_call(functools.partial(stats_block, offsets=tuple((around for _...  14.6 us
    pallas_call x1, Pallas kernels, normalized(): pl.pallas_call(normalize_block, grid_spec=pltpu.PrefetchScalarGridSpec(nu...  10.6 us
    all_to_all x1, waiting for transfers between devices, on_device_body(): lax.all_to_all(copies, PLANE, split_axis=0, concat_axis=0, tiled=True)  8.3 us
    ppermute x1, starting transfers between devices, swap_cores(): return lax.ppermute(value, 'c', [(0, 1), (1, 0)])  7.37 us
  transfers between devices with their start and end apart: 11, of which 6 were waited for; matrix products, arithmetic and copies ran while one was open for 4% of the time, Pallas kernels for 5%

profile of v2, /device:TPU:1, one launch (start us, length us, event | category | flops | bytes accessed | tf_op | source)
XLA Modules:
  0.0 195.9 jit_solution(18374048787226230772)
XLA Ops:
  0.0 0.0 copy-start
  0.0 0.9 slice_bitcast_fusion.2
  0.9 0.7 pad_maximum_fusion
  1.5 4.8 %all-to-all-start = ((bf16[4,16,1024]{2,1,0:T(8,128)(2,1)}), bf16[4,16,1024]{2,1,0:T(8,128)(2,1)S(1)}, u32[]{:S(2)}, u32[]{:S(2)}) async-start(bf16[4,16,1024]{2,1,0:T(8,128)(2,1)} %pad_maximum_fusion), calls=%async_computation | async-start | bytes 262144 | tf_op jit(solution)/shard_map/all_to_all | solution.py:47
  6.4 0.1 lt.56
  6.4 4.7 %all-to-all-done = bf16[4,16,1024]{2,1,0:T(8,128)(2,1)S(1)} async-done(((bf16[4,16,1024]{2,1,0:T(8,128)(2,1)}), bf16[4,16,1024]{2,1,0:T(8,128)(2,1)S(1)}, u32[]{:S(2)}, u32[]{:S(2)}) %all-to-all-start) | async-done | bytes 131104 | tf_op jit(solution)/shard_map/all_to_all | solution.py:47
  11.2 0.7 copy.28
  11.9 0.7 reduce.2
  12.6 0.1 reshape.299
  12.7 0.4 fusion.8
  13.1 0.1 broadcast_in_dim.58
  13.2 0.1 reshape.301
  13.3 1.2 select_reduce_fusion.1
  14.5 0.1 add.133
  14.5 0.1 broadcast_in_dim.57
  14.6 0.2 sub.65
  14.8 0.7 select_reduce_fusion
  15.6 1.0 fusion.4
  16.7 0.4 broadcast_in_dim.63
  17.1 0.0 copy-start.3
  17.1 40.5 %all_to_all.24 = bf16[16,784,128]{2,1,0:T(8,128)(2,1)S(1)} all-to-all(bf16[16,784,128]{2,1,0:T(8,128)(2,1)S(1)} %broadcast_in_dim.63), channel_id=1, replica_groups=mesh['z'=16,'x'=4,'y'=4,'c'=2] {'x','y'}, dimensions={0} | all-to-all | bytes 6422528 | tf_op jit(solution)/shard_map/all_to_all | solution.py:29
  57.6 7.4 %collective-permute-start = (bf16[16,784,128]{2,1,0:T(8,128)(2,1)S(1)}, bf16[16,784,128]{2,1,0:T(8,128)(2,1)}, u32[]{:S(2)}, u32[]{:S(2)}) collective-permute-start(bf16[16,784,128]{2,1,0:T(8,128)(2,1)S(1)} %all_to_all.24), channel_id=1, source_target_pairs={{0,1},{1,0},{2,3},{3,2},{4,5},{5,4},{6,7},{7,6},{8,9},{9,8},{10,11... | collective-permute-start | bytes 9633800 | tf_op jit(solution)/shard_map/ppermute | solution.py:33
  65.0 10.6 %collective-permute-start.1 = (bf16[64,1024]{1,0:T(8,128)(2,1)S(1)}, bf16[64,1024]{1,0:T(8,128)(2,1)}, u32[]{:S(2)}, u32[]{:S(2)}) collective-permute-start(bf16[64,1024]{1,0:T(8,128)(2,1)S(1)} %bitcast.45), channel_id=1, source_target_pairs={{0,160},{32,192},{64,224},{96,256},{128,288},{160,320},{192,352},{... | collective-permute-start | bytes 393224 | tf_op jit(solution)/shard_map/ppermute | solution.py:132
  75.6 0.7 pad_add_fusion.scalars_ref
  76.2 0.6 reshape.311
  76.8 5.8 %collective-permute-start.2 = (bf16[64,1024]{1,0:T(8,128)(2,1)S(1)}, bf16[64,1024]{1,0:T(8,128)(2,1)S(1)}, u32[]{:S(2)}, u32[]{:S(2)}) collective-permute-start(bf16[64,1024]{1,0:T(8,128)(2,1)S(1)} %bitcast.46), channel_id=1, source_target_pairs={{0,352},{32,384},{64,416},{96,448},{128,480},{160,0},{192,32},{224... | collective-permute-start | bytes 393224 | tf_op jit(solution)/shard_map/ppermute | solution.py:132
  82.7 0.7 constant_dynamic-update-slice_fusion.2
  83.3 0.2 collective-permute-done.1
  83.5 1.6 constant_dynamic-update-slice_fusion.1
  85.1 12.2 %collective-permute-done.2 = bf16[64,1024]{1,0:T(8,128)(2,1)S(1)} collective-permute-done((bf16[64,1024]{1,0:T(8,128)(2,1)S(1)}, bf16[64,1024]{1,0:T(8,128)(2,1)S(1)}, u32[]{:S(2)}, u32[]{:S(2)}) %collective-permute-start.2) | collective-permute-done | bytes 131104 | tf_op jit(solution)/shard_map/ppermute | solution.py:132
  97.3 0.7 constant_dynamic-update-slice_fusion.refs_0_
  97.9 1.9 collective-permute-start.3
  99.9 5.6 %collective-permute-start.4 = (bf16[192,1024]{1,0:T(8,128)(2,1)}, bf16[192,1024]{1,0:T(8,128)(2,1)}, u32[]{:S(2)}, u32[]{:S(2)}) collective-permute-start(bf16[192,1024]{1,0:T(8,128)(2,1)} %constant_dynamic-update-slice_fusion.refs_0_), channel_id=1, source_target_pairs={{0,480},{32,0},{64,32},{96,64},{128,96},{160,128},{192,160},{224,1... | collective-permute-start | bytes 1179656 | tf_op jit(solution)/shard_map/ppermute | solution.py:132
  105.5 2.3 %collective-permute-start.5 = (bf16[192,1024]{1,0:T(8,128)(2,1)}, bf16[192,1024]{1,0:T(8,128)(2,1)}, u32[]{:S(2)}, u32[]{:S(2)}) collective-permute-start(bf16[192,1024]{1,0:T(8,128)(2,1)} %constant_dynamic-update-slice_fusion.refs_0_), channel_id=1, source_target_pairs={{0,64},{32,96},{64,128},{96,160},{128,192},{160,224},{192,256},{22... | collective-permute-start | bytes 1179656 | tf_op jit(solution)/shard_map/ppermute | solution.py:132
  107.7 0.6 slice.68
  108.4 5.4 %collective-permute-start.7 = (bf16[32,1024]{1,0:T(8,128)(2,1)}, bf16[32,1024]{1,0:T(8,128)(2,1)S(1)}, u32[]{:S(2)}, u32[]{:S(2)}) collective-permute-start(bf16[32,1024]{1,0:T(8,128)(2,1)} %slice.68), channel_id=1, source_target_pairs={{0,416},{32,448},{64,480},{96,0},{128,32},{160,64},{192,96},{224,1... | collective-permute-start | bytes 196616 | tf_op jit(solution)/shard_map/ppermute | solution.py:132
  113.8 1.5 slice.69
  115.3 3.1 %collective-permute-done.7.refs_5_ = bf16[32,1024]{1,0:T(8,128)(2,1)S(1)} collective-permute-done((bf16[32,1024]{1,0:T(8,128)(2,1)}, bf16[32,1024]{1,0:T(8,128)(2,1)S(1)}, u32[]{:S(2)}, u32[]{:S(2)}) %collective-permute-start.7) | collective-permute-done | bytes 65568 | tf_op jit(solution)/shard_map/ppermute | solution.py:132
  118.4 4.6 %collective-permute-start.6 = (bf16[192,1024]{1,0:T(8,128)(2,1)}, bf16[192,1024]{1,0:T(8,128)(2,1)}, u32[]{:S(2)}, u32[]{:S(2)}) collective-permute-start(bf16[192,1024]{1,0:T(8,128)(2,1)} %constant_dynamic-update-slice_fusion.refs_0_), channel_id=1, source_target_pairs={{0,448},{32,480},{64,0},{96,32},{128,64},{160,96},{192,128},{224,1... | collective-permute-start | bytes 1179656 | tf_op jit(solution)/shard_map/ppermute | solution.py:132
  123.0 0.6 and_select_fusion.labels_ref
  123.7 0.1 sub.68
  123.8 0.0 collective-permute-done
  123.8 4.5 %collective-permute-start.8 = (bf16[32,1024]{1,0:T(8,128)(2,1)}, bf16[32,1024]{1,0:T(8,128)(2,1)}, u32[]{:S(2)}, u32[]{:S(2)}) collective-permute-start(bf16[32,1024]{1,0:T(8,128)(2,1)} %slice.69), channel_id=1, source_target_pairs={{0,96},{32,128},{64,160},{96,192},{128,224},{160,256},{192,288},{2... | collective-permute-start | bytes 196616 | tf_op jit(solution)/shard_map/ppermute | solution.py:132
  128.4 10.6 %normalized.1.rows_ref = bf16[3072,1024]{1,0:T(8,128)(2,1)} custom-call(s32[1]{0:T(128)} %bitcast.12.core_ref, bf16[4,4,784,128]{3,2,1,0:T(8,128)(2,1)} %bitcast.44, bf16[4,4,784,128]{3,2,1,0:T(8,128)(2,1)} %bitcast.13.far_ref, f32[1,1024]{1,0:T(1,128)} %bitcast.52), custom_call_target="tpu_custom_call" | custom-call | tf_op jit(solution)/shard_map/normalized/pallas_call | solution.py:115
  139.0 0.0 collective-permute-done.8.refs_6_
  139.0 0.0 collective-permute-done.3.refs_1_
  139.0 0.0 collective-permute-done.4.refs_2_
  139.0 0.0 collective-permute-done.5.refs_3_
  139.0 5.0 %collective-permute-done.6.refs_4_ = bf16[192,1024]{1,0:T(8,128)(2,1)} collective-permute-done((bf16[192,1024]{1,0:T(8,128)(2,1)}, bf16[192,1024]{1,0:T(8,128)(2,1)}, u32[]{:S(2)}, u32[]{:S(2)}) %collective-permute-start.6) | collective-permute-done | bytes 393248 | tf_op jit(solution)/shard_map/ppermute | solution.py:132
  144.0 14.6 %row_stats.1 = f32[8,3072]{1,0:T(8,128)} custom-call(s32[2]{0:T(128)} %pad_add_fusion.scalars_ref, bf16[3072,1024]{1,0:T(8,128)(2,1)} %normalized.1.rows_ref, s32[1,3072]{1,0:T(1,128)} %and_select_fusion.labels_ref, bf16[192,1024]{1,0:T(8,128)(2,1)} %constant_dynamic-update-slice_fusion.refs_0_, bf16[192,1024]{1,0:T(8,128)(2,1)} %collective-permute-done.3.refs_1_, ...), custom_call_target="tpu_custom_call" | custom-call | tf_op jit(solution)/shard_map/row_stats/pallas_call | solution.py:185
  158.5 0.9 slice.70
  159.4 0.1 reshape.307
  159.6 0.1 broadcast_in_dim.64
  159.7 0.7 broadcast_in_dim.65
  160.4 4.0 %all-to-all-start.2 = ((f32[32,2,768]{2,1,0:T(2,128)}), f32[32,2,768]{2,1,0:T(2,128)S(1)}, u32[]{:S(2)}, u32[]{:S(2)}) async-start(f32[32,2,768]{2,1,0:T(2,128)} %bitcast.17), calls=%async_computation.2 | async-start | bytes 393216 | tf_op jit(solution)/shard_map/all_to_all | solution.py:237
  164.4 0.1 ge.22
  164.5 8.3 %all-to-all-done.2 = f32[32,2,768]{2,1,0:T(2,128)S(1)} async-done(((f32[32,2,768]{2,1,0:T(2,128)}), f32[32,2,768]{2,1,0:T(2,128)S(1)}, u32[]{:S(2)}, u32[]{:S(2)}) %all-to-all-start.2) | async-done | bytes 196640 | tf_op jit(solution)/shard_map/all_to_all | solution.py:237
  172.8 0.2 slice_reduce_fusion.1
  173.1 0.1 sub.76
  173.2 0.1 all_to_all.18
  173.3 20.7 %all_to_all.25 = f32[16,1,48]{2,1,0:T(1,128)S(1)} all-to-all(f32[16,1,48]{2,1,0:T(1,128)S(1)} %bitcast.51), channel_id=1, replica_groups=mesh['z'=16,'x'=4,'y'=4,'c'=2] {'z'}, dimensions={0} | all-to-all | bytes 6144 | tf_op jit(solution)/shard_map/all_to_all | solution.py:245
  194.0 0.5 broadcast.284
  194.6 0.7 reduce.7
  195.2 0.7 reshape.309
  (29 shorter events, 0.3 us)
Async XLA Ops:
  0.0 15.6 %copy-start = (bf16[9,80,128]{2,1,0:T(8,128)(2,1)S(1)}, bf16[9,80,128]{2,1,0:T(8,128)(2,1)}, u32[]{:S(2)}) copy-start(bf16[9,80,128]{2,1,0:T(8,128)(2,1)} %param.9) | copy-start | bytes 552964
  1.5 9.7 %all-to-all-start = ((bf16[4,16,1024]{2,1,0:T(8,128)(2,1)}), bf16[4,16,1024]{2,1,0:T(8,128)(2,1)S(1)}, u32[]{:S(2)}, u32[]{:S(2)}) async-start(bf16[4,16,1024]{2,1,0:T(8,128)(2,1)} %pad_maximum_fusion), calls=%async_computation | async-start | bytes 262144 | tf_op jit(solution)/shard_map/all_to_all | solution.py:47
  17.1 59.1 %copy-start.3 = (bf16[1024]{0:T(1024)(128)(2,1)S(1)}, bf16[1024]{0:T(1024)(128)(2,1)}, u32[]{:S(2)}) copy-start(bf16[1024]{0:T(1024)(128)(2,1)} %param.10) | copy-start | bytes 6148
  57.6 70.8 %copy-start.1 = (bf16[16,784,128]{2,1,0:T(8,128)(2,1)}, bf16[16,784,128]{2,1,0:T(8,128)(2,1)S(1)}, u32[]{:S(2)}) copy-start(bf16[16,784,128]{2,1,0:T(8,128)(2,1)S(1)} %all_to_all.24) | copy-start | bytes 9633796
  57.6 66.2 %collective-permute-start = (bf16[16,784,128]{2,1,0:T(8,128)(2,1)S(1)}, bf16[16,784,128]{2,1,0:T(8,128)(2,1)}, u32[]{:S(2)}, u32[]{:S(2)}) collective-permute-start(bf16[16,784,128]{2,1,0:T(8,128)(2,1)S(1)} %all_to_all.24), channel_id=1, source_target_pairs={{0,1},{1,0},{2,3},{3,2},{4,5},{5,4},{6,7},{7,6},{8,9},{9,8},{10,11... | collective-permute-start | bytes 9633800 | tf_op jit(solution)/shard_map/ppermute | solution.py:33
  65.0 18.6 %collective-permute-start.1 = (bf16[64,1024]{1,0:T(8,128)(2,1)S(1)}, bf16[64,1024]{1,0:T(8,128)(2,1)}, u32[]{:S(2)}, u32[]{:S(2)}) collective-permute-start(bf16[64,1024]{1,0:T(8,128)(2,1)S(1)} %bitcast.45), channel_id=1, source_target_pairs={{0,160},{32,192},{64,224},{96,256},{128,288},{160,320},{192,352},{... | collective-permute-start | bytes 393224 | tf_op jit(solution)/shard_map/ppermute | solution.py:132
  76.8 20.4 %collective-permute-start.2 = (bf16[64,1024]{1,0:T(8,128)(2,1)S(1)}, bf16[64,1024]{1,0:T(8,128)(2,1)S(1)}, u32[]{:S(2)}, u32[]{:S(2)}) collective-permute-start(bf16[64,1024]{1,0:T(8,128)(2,1)S(1)} %bitcast.46), channel_id=1, source_target_pairs={{0,352},{32,384},{64,416},{96,448},{128,480},{160,0},{192,32},{224... | collective-permute-start | bytes 393224 | tf_op jit(solution)/shard_map/ppermute | solution.py:132
  97.9 41.0 %collective-permute-start.3 = (bf16[192,1024]{1,0:T(8,128)(2,1)}, bf16[192,1024]{1,0:T(8,128)(2,1)}, u32[]{:S(2)}, u32[]{:S(2)}) collective-permute-start(bf16[192,1024]{1,0:T(8,128)(2,1)} %constant_dynamic-update-slice_fusion.refs_0_), channel_id=1, source_target_pairs={{0,32},{32,64},{64,96},{96,128},{128,160},{160,192},{192,224},{224... | collective-permute-start | bytes 1179656 | tf_op jit(solution)/shard_map/ppermute | solution.py:132
  99.9 39.1 %collective-permute-start.4 = (bf16[192,1024]{1,0:T(8,128)(2,1)}, bf16[192,1024]{1,0:T(8,128)(2,1)}, u32[]{:S(2)}, u32[]{:S(2)}) collective-permute-start(bf16[192,1024]{1,0:T(8,128)(2,1)} %constant_dynamic-update-slice_fusion.refs_0_), channel_id=1, source_target_pairs={{0,480},{32,0},{64,32},{96,64},{128,96},{160,128},{192,160},{224,1... | collective-permute-start | bytes 1179656 | tf_op jit(solution)/shard_map/ppermute | solution.py:132
  105.5 33.5 %collective-permute-start.5 = (bf16[192,1024]{1,0:T(8,128)(2,1)}, bf16[192,1024]{1,0:T(8,128)(2,1)}, u32[]{:S(2)}, u32[]{:S(2)}) collective-permute-start(bf16[192,1024]{1,0:T(8,128)(2,1)} %constant_dynamic-update-slice_fusion.refs_0_), channel_id=1, source_target_pairs={{0,64},{32,96},{64,128},{96,160},{128,192},{160,224},{192,256},{22... | collective-permute-start | bytes 1179656 | tf_op jit(solution)/shard_map/ppermute | solution.py:132
  108.4 10.0 %collective-permute-start.7 = (bf16[32,1024]{1,0:T(8,128)(2,1)}, bf16[32,1024]{1,0:T(8,128)(2,1)S(1)}, u32[]{:S(2)}, u32[]{:S(2)}) collective-permute-start(bf16[32,1024]{1,0:T(8,128)(2,1)} %slice.68), channel_id=1, source_target_pairs={{0,416},{32,448},{64,480},{96,0},{128,32},{160,64},{192,96},{224,1... | collective-permute-start | bytes 196616 | tf_op jit(solution)/shard_map/ppermute | solution.py:132
  118.4 20.6 %copy-start.2 = (bf16[32,1024]{1,0:T(8,128)(2,1)}, bf16[32,1024]{1,0:T(8,128)(2,1)S(1)}, u32[]{:S(2)}) copy-start(bf16[32,1024]{1,0:T(8,128)(2,1)S(1)} %collective-permute-done.7.refs_5_) | copy-start | bytes 196612
  118.4 25.6 %collective-permute-start.6 = (bf16[192,1024]{1,0:T(8,128)(2,1)}, bf16[192,1024]{1,0:T(8,128)(2,1)}, u32[]{:S(2)}, u32[]{:S(2)}) collective-permute-start(bf16[192,1024]{1,0:T(8,128)(2,1)} %constant_dynamic-update-slice_fusion.refs_0_), channel_id=1, source_target_pairs={{0,448},{32,480},{64,0},{96,32},{128,64},{160,96},{192,128},{224,1... | collective-permute-start | bytes 1179656 | tf_op jit(solution)/shard_map/ppermute | solution.py:132
  123.8 15.2 %collective-permute-start.8 = (bf16[32,1024]{1,0:T(8,128)(2,1)}, bf16[32,1024]{1,0:T(8,128)(2,1)}, u32[]{:S(2)}, u32[]{:S(2)}) collective-permute-start(bf16[32,1024]{1,0:T(8,128)(2,1)} %slice.69), channel_id=1, source_target_pairs={{0,96},{32,128},{64,160},{96,192},{128,224},{160,256},{192,288},{2... | collective-permute-start | bytes 196616 | tf_op jit(solution)/shard_map/ppermute | solution.py:132
  160.4 12.4 %all-to-all-start.2 = ((f32[32,2,768]{2,1,0:T(2,128)}), f32[32,2,768]{2,1,0:T(2,128)S(1)}, u32[]{:S(2)}, u32[]{:S(2)}) async-start(f32[32,2,768]{2,1,0:T(2,128)} %bitcast.17), calls=%async_computation.2 | async-start | bytes 393216 | tf_op jit(solution)/shard_map/all_to_all | solution.py:237

commit v3 on v2

--- a/solution.py
+++ b/solution.py
@@ -20,7 +20,9 @@
 
 
 ROW_BLOCK = 256
-MATMUL_ROWS = 512
+HALF_ROWS = 384
+CHUNK = 32
+DEAD = -1e30
 LANES = 128
 
 
@@ -73,8 +75,7 @@
     earlier = (device_slots[:, None] > device_slots[None, :]).astype(jnp.bfloat16)
     running = jnp.dot(earlier, owner_hits, preferred_element_type=jnp.float32)
     slot_rank = jnp.sum(running * owner_hits.astype(jnp.float32), axis=1).astype(jnp.int32)
-    place = (targets % columns) * planes + targets // columns
-    target_row = place * capacity + slot_rank
+    target_row = targets * capacity + slot_rank
     placing = (target_row[None, :] == jnp.arange(OWN_ROWS, dtype=jnp.int32)[:, None]) & is_live[
         None, :
     ]
@@ -87,22 +88,23 @@
 
 def normalize_block(core_ref, near_ref, far_ref, gain_ref, out_ref):
     first = core_ref[0] == 0
-    pieces = []
-    for k in range(near_ref.shape[1]):
-        near = near_ref[0, k].astype(jnp.float32)
-        far = far_ref[0, k].astype(jnp.float32)
-        pieces += [jnp.where(first, near, far), jnp.where(first, far, near)]
-    squares = pieces[0] * pieces[0]
-    for piece in pieces[1:]:
-        squares = squares + piece * piece
-    width = len(pieces) * LANES
-    mean_square = jnp.sum(squares, axis=1, keepdims=True) / width
-    scale = lax.rsqrt(mean_square + epsilon)
-    for k, piece in enumerate(pieces):
-        gain = gain_ref[0:1, k * LANES : (k + 1) * LANES]
-        out_ref[:, k * LANES : (k + 1) * LANES] = (
-            piece * scale * gain * width ** (-0.5)
-        ).astype(jnp.bfloat16)
+    width = out_ref.shape[1]
+    for start in range(0, out_ref.shape[0], CHUNK):
+        pieces = []
+        for k in range(near_ref.shape[1]):
+            near = near_ref[0, k, start : start + CHUNK, :].astype(jnp.float32)
+            far = far_ref[0, k, start : start + CHUNK, :].astype(jnp.float32)
+            pieces += [jnp.where(first, near, far), jnp.where(first, far, near)]
+        squares = pieces[0] * pieces[0]
+        for piece in pieces[1:]:
+            squares = squares + piece * piece
+        mean_square = jnp.sum(squares, axis=1, keepdims=True) / width
+        scale = lax.rsqrt(mean_square + epsilon)
+        for k, piece in enumerate(pieces):
+            gain = gain_ref[0:1, k * LANES : (k + 1) * LANES]
+            out_ref[start : start + CHUNK, k * LANES : (k + 1) * LANES] = (
+                piece * scale * gain
+            ).astype(jnp.bfloat16)
 
 
 def normalized(near, far, norm_gain):
@@ -110,7 +112,7 @@
     blocks = OWN_ROWS // ROW_BLOCK
     width = slices * 2 * LANES
     core = lax.axis_index("c").reshape(1)
-    gain = norm_gain.astype(jnp.float32).reshape(1, width)
+    gain = (norm_gain.astype(jnp.float32) * width ** (-0.5)).reshape(1, width)
     spec = pl.BlockSpec((1, slices, ROW_BLOCK, LANES), lambda x, i, core: (x, 0, i, 0))
     return pl.pallas_call(
         normalize_block,
@@ -133,21 +135,45 @@
 
     below = shifted(mixed, 5)
     above = shifted(mixed, -5)
-    three = jnp.concatenate([mixed, below, above], axis=0)
-    half = mixed.shape[0] // 2
+    three, low, high = joined(mixed, below, above)
     found = [(three, (0, -5, 5))]
     for step in (1, -1, 2, -2):
         found.append((shifted(three, step), (-step, -step - 5, -step + 5)))
-    low = shifted(above[:half], -3)
-    high = shifted(below[half:], 3)
+    low = shifted(low, -3)
+    high = shifted(high, 3)
     return found, (low, high)
 
 
+def joined_block(own_ref, below_ref, above_ref, three_ref, low_ref, high_ref):
+    size = own_ref.shape[0]
+    half = size // 2
+    three_ref[0:size, :] = own_ref[...]
+    three_ref[size : 2 * size, :] = below_ref[...]
+    three_ref[2 * size : 3 * size, :] = above_ref[...]
+    low_ref[...] = above_ref[0:half, :]
+    high_ref[...] = below_ref[half:size, :]
+
+
+def joined(own, below, above):
+    size, part = own.shape
+    return pl.pallas_call(
+        joined_block,
+        out_shape=tuple(
+            jax.ShapeDtypeStruct((rows, part), own.dtype)
+            for rows in (3 * size, size // 2, size // 2)
+        ),
+        name="joined",
+    )(own, below, above)
+
+
 def stats_block(scalars_ref, rows_ref, labels_ref, *refs, offsets):
-    block_refs, (low_ref, high_ref, out_ref, weights_ref) = refs[: len(offsets)], refs[len(offsets) :]
-    rows = rows_ref.shape[0]
-
-    @pl.when(pl.program_id(0) == 0)
+    count = len(offsets)
+    block_refs = refs[:count]
+    low_ref, high_ref, out_ref, weights_ref, even_ref, odd_ref = refs[count:]
+    step = pl.program_id(0)
+    half = even_ref.shape[0]
+
+    @pl.when(step == 0)
     def _():
         size = 2 * low_ref.shape[0]
         planes = weights_ref.shape[0] // size
@@ -163,16 +189,45 @@
         weights_ref[pl.ds(middle, size // 2), :] = low_ref[...]
         weights_ref[pl.ds(pl.multiple_of(middle + size // 2, size // 2), size // 2), :] = high_ref[...]
 
-    logits = jnp.dot(rows_ref[...], weights_ref[...], preferred_element_type=jnp.float32)
-    columns = lax.broadcasted_iota(jnp.int32, logits.shape, 1)
-    logits = jnp.where(columns < scalars_ref[0], logits, -jnp.inf)
-    top = jnp.max(logits, axis=1, keepdims=True)
-    total = jnp.sum(jnp.exp(logits - top), axis=1, keepdims=True)
-    label = jnp.broadcast_to(labels_ref[0:1, :], (LANES, rows)).T[:, 0:1]
-    picked = jnp.sum(jnp.where(columns == label, logits, 0.0), axis=1, keepdims=True)
-    lane = lax.broadcasted_iota(jnp.int32, (rows, LANES), 1)
-    both = jnp.where(lane == 0, top + jnp.log(total), picked)
-    out_ref[...] = both.T[0:8]
+    def product(first):
+        return jnp.dot(
+            rows_ref[first : first + half, :], weights_ref[...], preferred_element_type=jnp.float32
+        )
+
+    def reduced(logits_ref, start):
+        start = pl.multiple_of(start, LANES)
+        part = logits_ref.shape[1]
+        columns = lax.broadcasted_iota(jnp.int32, (CHUNK, part), 1)
+        inside = columns < scalars_ref[0]
+        lane = lax.broadcasted_iota(jnp.int32, (CHUNK, LANES), 1)
+        for group in range(0, half, LANES):
+            label_row = labels_ref[0:1, pl.ds(start + group, LANES)]
+            label_all = jnp.broadcast_to(label_row, (LANES, LANES)).T
+            pieces = []
+            for chunk in range(0, LANES, CHUNK):
+                label = label_all[chunk : chunk + CHUNK, 0:1]
+                logits = logits_ref[group + chunk : group + chunk + CHUNK, :]
+                logits = jnp.where(inside, logits, -jnp.inf)
+                top = jnp.max(logits, axis=1, keepdims=True)
+                total = jnp.sum(jnp.exp(logits - top), axis=1, keepdims=True)
+                picked = jnp.sum(jnp.where(columns == label, logits, 0.0), axis=1, keepdims=True)
+                value = jnp.where(label == -2, DEAD, top + jnp.log(total))
+                pieces.append(jnp.where(lane == 0, value, picked))
+            both = jnp.concatenate(pieces, axis=0).T
+            out_ref[:, pl.ds(pl.multiple_of(start + group, LANES), LANES)] = both[0:8]
+
+    total_rows = out_ref.shape[1]
+
+    @pl.when(step < total_rows // (2 * half))
+    def _():
+        even_ref[...] = product(0)
+        reduced(odd_ref, jnp.maximum(step * 2 - 1, 0) * half)
+        odd_ref[...] = product(half)
+        reduced(even_ref, step * 2 * half)
+
+    @pl.when(step == total_rows // (2 * half))
+    def _():
+        reduced(odd_ref, total_rows - half)
 
 
 def row_stats(rows, blocks, labels, valid):
@@ -182,18 +237,25 @@
     part = arrays[0].shape[1]
     scalars = jnp.stack([valid, lax.axis_index("z")]).astype(jnp.int32)
     whole = [pl.BlockSpec(array.shape, lambda i, scalars: (0, 0)) for array in arrays]
+    steps = total // (2 * HALF_ROWS)
     stats = pl.pallas_call(
         functools.partial(stats_block, offsets=tuple(around for _, around in found)),
         grid_spec=pltpu.PrefetchScalarGridSpec(
             num_scalar_prefetch=1,
-            grid=(total // MATMUL_ROWS,),
+            grid=(steps + 1,),
             in_specs=[
-                pl.BlockSpec((MATMUL_ROWS, width), lambda i, scalars: (i, 0)),
-                pl.BlockSpec((1, MATMUL_ROWS), lambda i, scalars: (0, i)),
+                pl.BlockSpec(
+                    (2 * HALF_ROWS, width), lambda i, scalars: (jnp.minimum(i, steps - 1), 0)
+                ),
+                pl.BlockSpec((1, total), lambda i, scalars: (0, 0)),
                 *whole,
             ],
-            out_specs=pl.BlockSpec((8, MATMUL_ROWS), lambda i, scalars: (0, i)),
-            scratch_shapes=[pltpu.VMEM((width, part), jnp.bfloat16)],
+            out_specs=pl.BlockSpec((8, total), lambda i, scalars: (0, 0)),
+            scratch_shapes=[
+                pltpu.VMEM((width, part), jnp.bfloat16),
+                pltpu.VMEM((HALF_ROWS, part), jnp.float32),
+                pltpu.VMEM((HALF_ROWS, part), jnp.float32),
+            ],
         ),
         out_shape=jax.ShapeDtypeStruct((8, total), jnp.float32),
         name="row_stats",
@@ -206,9 +268,6 @@
     capacity = OWN_ROWS // (planes * columns)
     shard_rows = embedding.shape[0]
     mixed = exchanged_embedding(embedding)
-    mixed, tokens, span_bounds, owner, decoder_states = lax.optimization_barrier(
-        (mixed, tokens, span_bounds, owner, decoder_states)
-    )
     blocks = gathered_blocks(mixed)
     packed, sent_labels = packed_rows(tokens, span_bounds, owner, decoder_states)
     digits = jnp.stack([sent_labels // 256, sent_labels % 256]).astype(jnp.bfloat16)
@@ -227,22 +286,20 @@
     valid = jnp.minimum(shard_rows - here * part, part)
     local_label = row_labels - (lax.axis_index(VOC) * shard_rows + here * part)
     local_label = jnp.where((local_label >= 0) & (local_label < valid), local_label, -1)
+    local_label = jnp.where(row_labels < 0, -2, local_label)
     rows = normalized(near, far, norm_gain)
     stats = row_stats(rows, blocks, local_label.reshape(-1), valid)
-    group = planes * capacity
-    stats = stats.reshape(2, columns, columns, group).transpose(2, 0, 1, 3)
-    stats = stats.reshape(columns, 1, 2, OWN_ROWS)
-    copies = jnp.broadcast_to(stats, (columns, lax.axis_size(VOC), 2, OWN_ROWS))
-    copies = copies.reshape(-1, 2, OWN_ROWS)
-    parts = lax.all_to_all(copies, PLANE, split_axis=0, concat_axis=0, tiled=True)
-    row_top = jnp.max(parts[:, 0], axis=0)
-    row_loss = row_top + jnp.log(jnp.sum(jnp.exp(parts[:, 0] - row_top[None]), axis=0))
-    row_loss = row_loss - jnp.sum(parts[:, 1], axis=0)
-    mine = row_labels.reshape(columns, columns, group)
-    mine = lax.dynamic_index_in_dim(mine, here, axis=1, keepdims=False).reshape(-1)
-    sent = jnp.where(mine >= 0, row_loss, 0.0).astype(jnp.float32)
-    sent = sent.reshape(columns, planes, capacity).swapaxes(0, 1).reshape(planes, -1)
-    return lax.all_to_all(sent, "z", split_axis=0, concat_axis=0, tiled=True).reshape(-1)
+    share = 2 * columns * capacity
+    owners = planes * columns
+    stats = stats.reshape(2 * columns, owners, capacity).swapaxes(0, 1).reshape(owners, 1, share)
+    copies = jnp.broadcast_to(stats, (owners, lax.axis_size(VOC), share)).reshape(-1, share)
+    parts = lax.all_to_all(copies, ("z", *PLANE), split_axis=0, concat_axis=0, tiled=True)
+    parts = parts.reshape(planes, -1, share)
+    values, picked = parts[:, :, : share // 2], parts[:, :, share // 2 :]
+    row_top = jnp.max(values, axis=1)
+    row_loss = row_top + jnp.log(jnp.sum(jnp.exp(values - row_top[:, None]), axis=1))
+    row_loss = row_loss - jnp.sum(picked, axis=1)
+    return jnp.where(row_top > 0.5 * DEAD, row_loss, 0.0).reshape(-1).astype(jnp.float32)
 
 
 def solution(mesh):

time: 197 us -> 209 us (1.061)
  blocking collectives: 61.2 us -> 90.8 us
  waiting for transfers between devices: 33.5 us -> 21.2 us
  Pallas kernels: 25.2 us -> 37.2 us
  starting transfers between devices: 57 us -> 48.6 us
  local copies, waits for them, and re-layouts: 11.1 us -> 4.08 us
    all_to_all x1 -> x2, blocking collectives: 20.7 us -> 45.1 us  [the longest x1 37.7 us: on_device_body(): lax.all_to_all(copies, ('z', *PLANE), split_axis=0, concat_axis=0, tiled=...]
    all_to_all x2 -> x0, waiting for transfers between devices: 13 us -> none  [the longest x1 8.3 us: on_device_body(): lax.all_to_all(copies, PLANE, split_axis=0, concat_axis=0, tiled=True)]
    pallas_call x1, Pallas kernels: 14.6 us -> 24.9 us  [row_stats(): pl.pallas_call(functools.partial(stats_block, offsets=tuple((around for _...]
    all_to_all x2 -> x0, starting transfers between devices: 8.84 us -> none  [the longest x1 4.83 us: exchanged_embedding(): mixed = lax.all_to_all(split, 'x', split_axis=0, concat_axis=0, tiled=True)]
    all_to_all x1, blocking collectives: 40.5 us -> 45.7 us  [broadcast_all(): return lax.all_to_all(copies, axis, split_axis=0, concat_axis=0, tiled=True)]
    ppermute x8, starting transfers between devices: 40.8 us -> 43.6 us  [shifted(): lax.ppermute(value, 'z', [(k, (k + step) % planes) for k in range(planes)])]
    ppermute x1, starting transfers between devices: 7.37 us -> 5.02 us  [swap_cores(): return lax.ppermute(value, 'c', [(0, 1), (1, 0)])]
    unnamed x10 -> x13, local copies, waits for them, and re-layouts: 2.23 us -> 0.03 us
  transfers between devices with their start and end apart: 11 -> 9, of which waited for: 6 -> 3; matrix products, arithmetic and copies ran while one was open for 4% -> 1% of each run, Pallas kernels for 5% -> 6%
where the time goes in v3:
time: 209 us; the launch traced here: 208 us
  blocking collectives  90.8 us (43%)
  starting transfers between devices  48.6 us (23%)
  Pallas kernels  37.2 us (18%)
  waiting for transfers between devices  21.2 us (10%)
  other arithmetic  4.79 us (2%)
  local copies, waits for them, and re-layouts  4.08 us (2%)
    all_to_all x1, blocking collectives, broadcast_all(): return lax.all_to_all(copies, axis, split_axis=0, concat_axis=0, tiled=True)  45.7 us
    ppermute x8, starting transfers between devices, shifted(): lax.ppermute(value, 'z', [(k, (k + step) % planes) for k in range(planes)])  43.6 us
    all_to_all x1, blocking collectives, on_device_body(): lax.all_to_all(copies, ('z', *PLANE), split_axis=0, concat_axis=0, tiled=...  37.7 us
    pallas_call x1, Pallas kernels, row_stats(): pl.pallas_call(functools.partial(stats_block, offsets=tuple((around for _...  24.9 us
    ppermute x8, waiting for transfers between devices, shifted(): lax.ppermute(value, 'z', [(k, (k + step) % planes) for k in range(planes)])  21.2 us
    pallas_call x1, Pallas kernels, normalized(): pl.pallas_call(normalize_block, grid_spec=pltpu.PrefetchScalarGridSpec(nu...  10.5 us
    all_to_all x1, blocking collectives, exchanged_embedding(): mixed = lax.all_to_all(split, 'x', split_axis=0, concat_axis=0, tiled=True)  7.44 us
    ppermute x1, starting transfers between devices, swap_cores(): return lax.ppermute(value, 'c', [(0, 1), (1, 0)])  5.02 us
  transfers between devices with their start and end apart: 9, of which 3 were waited for; matrix products, arithmetic and copies ran while one was open for 1% of the time, Pallas kernels for 6%

profile of v3, /device:TPU:1, one launch (start us, length us, event | category | flops | bytes accessed | tf_op | source)
XLA Modules:
  0.0 208.4 jit_solution(907855253598591164)
XLA Ops:
  0.0 0.0 copy-start
  0.0 0.8 fusion.22
  0.8 0.1 broadcast_in_dim.62
  0.9 0.1 reshape.249
  1.0 1.2 select_reduce_fusion.1
  2.2 0.1 add.104
  2.3 0.7 reduce
  3.0 0.1 reshape.247
  3.1 0.4 fusion.8
  3.5 0.1 lt.58
  3.5 0.1 broadcast_in_dim.61
  3.6 0.2 sub.55
  3.9 0.7 select_reduce_fusion
  4.6 0.0 copy-done
  4.6 1.0 fusion.4
  5.7 0.4 broadcast_in_dim.67
  6.1 0.0 copy-start.3
  6.1 0.0 copy-start.5
  6.1 45.7 %all_to_all.19 = bf16[16,784,128]{2,1,0:T(8,128)(2,1)S(1)} all-to-all(bf16[16,784,128]{2,1,0:T(8,128)(2,1)S(1)} %broadcast_in_dim.67), channel_id=1, replica_groups=mesh['z'=16,'x'=4,'y'=4,'c'=2] {'x','y'}, dimensions={0} | all-to-all | bytes 6422528 | tf_op jit(solution)/shard_map/all_to_all | solution.py:31
  51.8 0.0 copy-start.1
  51.8 5.0 %collective-permute-start = (bf16[16,784,128]{2,1,0:T(8,128)(2,1)S(1)}, bf16[16,784,128]{2,1,0:T(8,128)(2,1)}, u32[]{:S(2)}, u32[]{:S(2)}) collective-permute-start(bf16[16,784,128]{2,1,0:T(8,128)(2,1)S(1)} %all_to_all.19), channel_id=1, source_target_pairs={{0,1},{1,0},{2,3},{3,2},{4,5},{5,4},{6,7},{7,6},{8,9},{9,8},{10,11... | collective-permute-start | bytes 9633800 | tf_op jit(solution)/shard_map/ppermute | solution.py:35
  56.8 0.0 copy-done.3
  56.9 7.4 %all_to_all.20 = bf16[4,16,1024]{2,1,0:T(8,128)(2,1)S(1)} all-to-all(bf16[4,16,1024]{2,1,0:T(8,128)(2,1)S(1)} %pad_maximum_fusion), channel_id=1, replica_groups=mesh['z'=16,'x'=4,'y'=4,'c'=2] {'x'}, dimensions={0} | all-to-all | bytes 262144 | tf_op jit(solution)/shard_map/all_to_all | solution.py:49
  64.3 0.0 copy-start.2
  64.3 10.6 %collective-permute-start.1 = (bf16[64,1024]{1,0:T(8,128)(2,1)S(1)}, bf16[64,1024]{1,0:T(8,128)(2,1)}, u32[]{:S(2)}, u32[]{:S(2)}) collective-permute-start(bf16[64,1024]{1,0:T(8,128)(2,1)S(1)} %bitcast.41), channel_id=1, source_target_pairs={{0,160},{32,192},{64,224},{96,256},{128,288},{160,320},{192,352},{... | collective-permute-start | bytes 393224 | tf_op jit(solution)/shard_map/ppermute | solution.py:134
  74.9 5.9 %collective-permute-start.2 = (bf16[64,1024]{1,0:T(8,128)(2,1)S(1)}, bf16[64,1024]{1,0:T(8,128)(2,1)}, u32[]{:S(2)}, u32[]{:S(2)}) collective-permute-start(bf16[64,1024]{1,0:T(8,128)(2,1)S(1)} %bitcast.42), channel_id=1, source_target_pairs={{0,352},{32,384},{64,416},{96,448},{128,480},{160,0},{192,32},{224... | collective-permute-start | bytes 393224 | tf_op jit(solution)/shard_map/ppermute | solution.py:134
  80.8 0.0 copy-done.5
  80.8 0.6 convert_multiply_fusion
  81.4 0.6 pad_add_fusion.scalars_ref
  82.0 0.0 collective-permute-done.1.below_ref
  82.0 9.2 %collective-permute-done.2.above_ref = bf16[64,1024]{1,0:T(8,128)(2,1)} collective-permute-done((bf16[64,1024]{1,0:T(8,128)(2,1)S(1)}, bf16[64,1024]{1,0:T(8,128)(2,1)}, u32[]{:S(2)}, u32[]{:S(2)}) %collective-permute-start.2) | collective-permute-done | bytes 131104 | tf_op jit(solution)/shard_map/ppermute | solution.py:134
  91.3 0.0 copy-done.2
  91.3 1.9 joined.1
  93.1 1.9 collective-permute-start.3
  95.1 9.5 %collective-permute-start.4 = (bf16[192,1024]{1,0:T(8,128)(2,1)}, bf16[192,1024]{1,0:T(8,128)(2,1)}, u32[]{:S(2)}, u32[]{:S(2)}) collective-permute-start(bf16[192,1024]{1,0:T(8,128)(2,1)} %get-tuple-element.8.refs_0_), channel_id=1, source_target_pairs={{0,480},{32,0},{64,32},{96,64},{128,96},{160,128},{192,160},{224,1... | collective-permute-start | bytes 1179656 | tf_op jit(solution)/shard_map/ppermute | solution.py:134
  104.6 1.9 collective-permute-start.5
  106.5 5.8 %collective-permute-start.7 = (bf16[32,1024]{1,0:T(8,128)(2,1)}, bf16[32,1024]{1,0:T(8,128)(2,1)S(1)}, u32[]{:S(2)}, u32[]{:S(2)}) collective-permute-start(bf16[32,1024]{1,0:T(8,128)(2,1)} %get-tuple-element.9), channel_id=1, source_target_pairs={{0,416},{32,448},{64,480},{96,0},{128,32},{160,64},{192,96},{224,1... | collective-permute-start | bytes 196616 | tf_op jit(solution)/shard_map/ppermute | solution.py:134
  112.4 6.7 %collective-permute-done.7.refs_5_ = bf16[32,1024]{1,0:T(8,128)(2,1)S(1)} collective-permute-done((bf16[32,1024]{1,0:T(8,128)(2,1)}, bf16[32,1024]{1,0:T(8,128)(2,1)S(1)}, u32[]{:S(2)}, u32[]{:S(2)}) %collective-permute-start.7) | collective-permute-done | bytes 65568 | tf_op jit(solution)/shard_map/ppermute | solution.py:134
  119.1 0.0 copy-start.4
  119.1 1.9 collective-permute-start.6
  121.0 0.0 collective-permute-done
  121.1 6.0 %collective-permute-start.8 = (bf16[32,1024]{1,0:T(8,128)(2,1)}, bf16[32,1024]{1,0:T(8,128)(2,1)}, u32[]{:S(2)}, u32[]{:S(2)}) collective-permute-start(bf16[32,1024]{1,0:T(8,128)(2,1)} %get-tuple-element.10), channel_id=1, source_target_pairs={{0,96},{32,128},{64,160},{96,192},{128,224},{160,256},{192,288},{2... | collective-permute-start | bytes 196616 | tf_op jit(solution)/shard_map/ppermute | solution.py:134
  127.1 0.6 fusion.16.labels_ref
  127.7 0.0 copy-done.1
  127.7 10.5 %normalized.1.rows_ref = bf16[3072,1024]{1,0:T(8,128)(2,1)} custom-call(s32[1]{0:T(128)} %bitcast.2.core_ref, bf16[4,4,784,128]{3,2,1,0:T(8,128)(2,1)} %bitcast.36, bf16[4,4,784,128]{3,2,1,0:T(8,128)(2,1)} %bitcast.7.far_ref, f32[1,1024]{1,0:T(1,128)} %bitcast.48), custom_call_target="tpu_custom_call" | custom-call | tf_op jit(solution)/shard_map/normalized/pallas_call | solution.py:117
  138.2 0.0 copy-done.4
  138.2 0.0 collective-permute-done.8.refs_6_
  138.2 0.0 collective-permute-done.3.refs_1_
  138.2 0.0 collective-permute-done.4.refs_2_
  138.2 0.0 collective-permute-done.5.refs_3_
  138.2 5.3 %collective-permute-done.6.refs_4_ = bf16[192,1024]{1,0:T(8,128)(2,1)} collective-permute-done((bf16[192,1024]{1,0:T(8,128)(2,1)}, bf16[192,1024]{1,0:T(8,128)(2,1)}, u32[]{:S(2)}, u32[]{:S(2)}) %collective-permute-start.6) | collective-permute-done | bytes 393248 | tf_op jit(solution)/shard_map/ppermute | solution.py:134
  143.5 24.9 %row_stats.1 = f32[8,3072]{1,0:T(8,128)} custom-call(s32[2]{0:T(128)} %pad_add_fusion.scalars_ref, bf16[3072,1024]{1,0:T(8,128)(2,1)} %normalized.1.rows_ref, s32[1,3072]{1,0:T(1,128)} %fusion.16.labels_ref, bf16[192,1024]{1,0:T(8,128)(2,1)} %get-tuple-element.8.refs_0_, bf16[192,1024]{1,0:T(8,128)(2,1)} %collective-permute-done.3.refs_1_, ...), custom_call_target="tpu_custom_call" | custom-call | tf_op jit(solution)/shard_map/row_stats/pallas_call | solution.py:241
  168.4 0.9 slice.57
  169.3 0.3 reshape.254
  169.6 0.1 copy.20
  169.7 0.1 copy.21
  169.8 37.7 %all_to_all.21 = f32[512,1,96]{2,1,0:T(1,128)S(1)} all-to-all(f32[512,1,96]{2,1,0:T(1,128)S(1)} %bitcast.40), channel_id=1, replica_groups=mesh['z'=16,'x'=4,'y'=4,'c'=2] {'z','x','y','c'}, dimensions={0} | all-to-all | bytes 393216 | tf_op jit(solution)/shard_map/all_to_all | solution.py:296
  207.6 0.2 exponential_reduce_fusion
  207.7 0.7 select_n.84
  (22 shorter events, 0.3 us)
Async XLA Ops:
  0.0 4.6 %copy-start = (bf16[9,80,128]{2,1,0:T(8,128)(2,1)S(1)}, bf16[9,80,128]{2,1,0:T(8,128)(2,1)}, u32[]{:S(2)}) copy-start(bf16[9,80,128]{2,1,0:T(8,128)(2,1)} %param.9) | copy-start | bytes 552964
  6.1 50.7 %copy-start.3 = (bf16[4016,16]{0,1:T(8,128)(2,1)S(1)}, bf16[4016,16]{0,1:T(8,128)(2,1)}, u32[]{:S(2)}) copy-start(bf16[4016,16]{0,1:T(8,128)(2,1)} %param.11) | copy-start | bytes 385540
  6.1 74.7 %copy-start.5 = (bf16[1024]{0:T(1024)(128)(2,1)S(1)}, bf16[1024]{0:T(1024)(128)(2,1)}, u32[]{:S(2)}) copy-start(bf16[1024]{0:T(1024)(128)(2,1)} %param.10) | copy-start | bytes 6148
  51.8 75.9 %copy-start.1 = (bf16[16,784,128]{2,1,0:T(8,128)(2,1)}, bf16[16,784,128]{2,1,0:T(8,128)(2,1)S(1)}, u32[]{:S(2)}) copy-start(bf16[16,784,128]{2,1,0:T(8,128)(2,1)S(1)} %all_to_all.19) | copy-start | bytes 9633796
  51.8 69.3 %collective-permute-start = (bf16[16,784,128]{2,1,0:T(8,128)(2,1)S(1)}, bf16[16,784,128]{2,1,0:T(8,128)(2,1)}, u32[]{:S(2)}, u32[]{:S(2)}) collective-permute-start(bf16[16,784,128]{2,1,0:T(8,128)(2,1)S(1)} %all_to_all.19), channel_id=1, source_target_pairs={{0,1},{1,0},{2,3},{3,2},{4,5},{5,4},{6,7},{7,6},{8,9},{9,8},{10,11... | collective-permute-start | bytes 9633800 | tf_op jit(solution)/shard_map/ppermute | solution.py:35
  64.3 27.0 %copy-start.2 = (bf16[4,16,1024]{2,1,0:T(8,128)(2,1)}, bf16[4,16,1024]{2,1,0:T(8,128)(2,1)S(1)}, u32[]{:S(2)}) copy-start(bf16[4,16,1024]{2,1,0:T(8,128)(2,1)S(1)} %all_to_all.20) | copy-start | bytes 393220
  64.3 17.7 %collective-permute-start.1 = (bf16[64,1024]{1,0:T(8,128)(2,1)S(1)}, bf16[64,1024]{1,0:T(8,128)(2,1)}, u32[]{:S(2)}, u32[]{:S(2)}) collective-permute-start(bf16[64,1024]{1,0:T(8,128)(2,1)S(1)} %bitcast.41), channel_id=1, source_target_pairs={{0,160},{32,192},{64,224},{96,256},{128,288},{160,320},{192,352},{... | collective-permute-start | bytes 393224 | tf_op jit(solution)/shard_map/ppermute | solution.py:134
  74.9 16.4 %collective-permute-start.2 = (bf16[64,1024]{1,0:T(8,128)(2,1)S(1)}, bf16[64,1024]{1,0:T(8,128)(2,1)}, u32[]{:S(2)}, u32[]{:S(2)}) collective-permute-start(bf16[64,1024]{1,0:T(8,128)(2,1)S(1)} %bitcast.42), channel_id=1, source_target_pairs={{0,352},{32,384},{64,416},{96,448},{128,480},{160,0},{192,32},{224... | collective-permute-start | bytes 393224 | tf_op jit(solution)/shard_map/ppermute | solution.py:134
  93.1 45.1 %collective-permute-start.3 = (bf16[192,1024]{1,0:T(8,128)(2,1)}, bf16[192,1024]{1,0:T(8,128)(2,1)}, u32[]{:S(2)}, u32[]{:S(2)}) collective-permute-start(bf16[192,1024]{1,0:T(8,128)(2,1)} %get-tuple-element.8.refs_0_), channel_id=1, source_target_pairs={{0,32},{32,64},{64,96},{96,128},{128,160},{160,192},{192,224},{224... | collective-permute-start | bytes 1179656 | tf_op jit(solution)/shard_map/ppermute | solution.py:134
  95.1 43.1 %collective-permute-start.4 = (bf16[192,1024]{1,0:T(8,128)(2,1)}, bf16[192,1024]{1,0:T(8,128)(2,1)}, u32[]{:S(2)}, u32[]{:S(2)}) collective-permute-start(bf16[192,1024]{1,0:T(8,128)(2,1)} %get-tuple-element.8.refs_0_), channel_id=1, source_target_pairs={{0,480},{32,0},{64,32},{96,64},{128,96},{160,128},{192,160},{224,1... | collective-permute-start | bytes 1179656 | tf_op jit(solution)/shard_map/ppermute | solution.py:134
  104.6 33.6 %collective-permute-start.5 = (bf16[192,1024]{1,0:T(8,128)(2,1)}, bf16[192,1024]{1,0:T(8,128)(2,1)}, u32[]{:S(2)}, u32[]{:S(2)}) collective-permute-start(bf16[192,1024]{1,0:T(8,128)(2,1)} %get-tuple-element.8.refs_0_), channel_id=1, source_target_pairs={{0,64},{32,96},{64,128},{96,160},{128,192},{160,224},{192,256},{22... | collective-permute-start | bytes 1179656 | tf_op jit(solution)/shard_map/ppermute | solution.py:134
  106.5 12.6 %collective-permute-start.7 = (bf16[32,1024]{1,0:T(8,128)(2,1)}, bf16[32,1024]{1,0:T(8,128)(2,1)S(1)}, u32[]{:S(2)}, u32[]{:S(2)}) collective-permute-start(bf16[32,1024]{1,0:T(8,128)(2,1)} %get-tuple-element.9), channel_id=1, source_target_pairs={{0,416},{32,448},{64,480},{96,0},{128,32},{160,64},{192,96},{224,1... | collective-permute-start | bytes 196616 | tf_op jit(solution)/shard_map/ppermute | solution.py:134
  119.1 19.1 %copy-start.4 = (bf16[32,1024]{1,0:T(8,128)(2,1)}, bf16[32,1024]{1,0:T(8,128)(2,1)S(1)}, u32[]{:S(2)}) copy-start(bf16[32,1024]{1,0:T(8,128)(2,1)S(1)} %collective-permute-done.7.refs_5_) | copy-start | bytes 196612
  119.1 24.4 %collective-permute-start.6 = (bf16[192,1024]{1,0:T(8,128)(2,1)}, bf16[192,1024]{1,0:T(8,128)(2,1)}, u32[]{:S(2)}, u32[]{:S(2)}) collective-permute-start(bf16[192,1024]{1,0:T(8,128)(2,1)} %get-tuple-element.8.refs_0_), channel_id=1, source_target_pairs={{0,448},{32,480},{64,0},{96,32},{128,64},{160,96},{192,128},{224,1... | collective-permute-start | bytes 1179656 | tf_op jit(solution)/shard_map/ppermute | solution.py:134
  121.1 17.1 %collective-permute-start.8 = (bf16[32,1024]{1,0:T(8,128)(2,1)}, bf16[32,1024]{1,0:T(8,128)(2,1)}, u32[]{:S(2)}, u32[]{:S(2)}) collective-permute-start(bf16[32,1024]{1,0:T(8,128)(2,1)} %get-tuple-element.10), channel_id=1, source_target_pairs={{0,96},{32,128},{64,160},{96,192},{128,224},{160,256},{192,288},{2... | collective-permute-start | bytes 196616 | tf_op jit(solution)/shard_map/ppermute | solution.py:134

commit v4 on v2

v4 whole, which is shorter than its diff:
```python
import functools

import jax
import jax.numpy as jnp
from jax import lax
from jax.experimental import pallas as pl
from jax.experimental.pallas import tpu as pltpu
from jax.sharding import Mesh
from jax.sharding import PartitionSpec as P


MAXSPAN = 5
OWN_ROWS = 768
DP = ("z", "x")
VOC = ("y", "c")
PLANE = ("x", "y", "c")


epsilon = 1e-06


ROW_BLOCK = 384
LANES = 128


def broadcast_all(value, axis):
    copies = jnp.broadcast_to(value, (lax.axis_size(axis), *value.shape))
    return lax.all_to_all(copies, axis, split_axis=0, concat_axis=0, tiled=True)


def swap_cores(value):
    return lax.ppermute(value, "c", [(0, 1), (1, 0)])


def part_width(rows, parts):
    return -(-rows // (parts * LANES)) * LANES


def exchanged_embedding(embedding):
    parts = lax.axis_size("x")
    local = embedding.T
    width, rows = local.shape
    part = part_width(rows, parts)
    local = jnp.pad(local, ((0, 0), (0, part * parts - rows)))
    split = jnp.stack([local[:, k * part : (k + 1) * part] for k in range(parts)])
    mixed = lax.all_to_all(split, "x", split_axis=0, concat_axis=0, tiled=True)
    return mixed.reshape(parts * width, part)


def packed_rows(tokens, span_bounds, owner, decoder_states):
    _, slot_count, local_width = decoder_states.shape
    planes, columns = lax.axis_size("z"), lax.axis_size("x")
    owner_total = planes * columns
    capacity = OWN_ROWS // owner_total
    slot_ids = jnp.arange(slot_count, dtype=jnp.int32)
    offsets = slot_ids % MAXSPAN
    starts = jnp.repeat(span_bounds[:, :, 0], MAXSPAN, axis=1)
    span_ends = jnp.repeat(span_bounds[:, :, 1], MAXSPAN, axis=1)
    is_live = (offsets[None, :] < span_ends - starts).reshape(-1)
    length = tokens.shape[1]
    positions = jnp.minimum(starts + offsets[None, :], length - 1)
    places = jnp.arange(length, dtype=jnp.int32)
    labels = jnp.sum(
        jnp.where(places[None, None, :] == positions[:, :, None], tokens[:, None, :], 0), axis=2
    ).reshape(-1)
    targets = owner.reshape(-1)
    slot_total = targets.shape[0]
    owner_hits = (targets[:, None] == jnp.arange(owner_total, dtype=jnp.int32)[None, :]).astype(
        jnp.bfloat16
    )
    device_slots = jnp.arange(slot_total, dtype=jnp.int32)
    earlier = (device_slots[:, None] > device_slots[None, :]).astype(jnp.bfloat16)
    running = jnp.dot(earlier, owner_hits, preferred_element_type=jnp.float32)
    slot_rank = jnp.sum(running * owner_hits.astype(jnp.float32), axis=1).astype(jnp.int32)
    target_row = targets * capacity + slot_rank
    placing = (target_row[None, :] == jnp.arange(OWN_ROWS, dtype=jnp.int32)[:, None]) & is_live[
        None, :
    ]
    sent_labels = jnp.sum(jnp.where(placing, labels[None, :] + 1, 0), axis=1)
    onehot = placing.astype(jnp.bfloat16)
    states = decoder_states.reshape(slot_total, local_width)
    packed = jnp.dot(onehot, states, preferred_element_type=jnp.float32).astype(jnp.bfloat16)
    return packed, sent_labels


def gathered_blocks(mixed):
    planes = lax.axis_size("z")

    def shifted(value, step):
        return lax.ppermute(value, "z", [(k, (k + step) % planes) for k in range(planes)])

    below = shifted(mixed, 5)
    above = shifted(mixed, -5)
    three, low, high = joined(mixed, below, above)
    found = [(three, (0, -5, 5))]
    for step in (1, -1, 2, -2):
        found.append((shifted(three, step), (-step, -step - 5, -step + 5)))
    low = shifted(low, -3)
    high = shifted(high, 3)
    return found, (low, high)


def joined_block(own_ref, below_ref, above_ref, three_ref, low_ref, high_ref):
    size = own_ref.shape[0]
    half = size // 2
    three_ref[0:size, :] = own_ref[...]
    three_ref[size : 2 * size, :] = below_ref[...]
    three_ref[2 * size : 3 * size, :] = above_ref[...]
    low_ref[...] = above_ref[0:half, :]
    high_ref[...] = below_ref[half:size, :]


def joined(own, below, above):
    size, part = own.shape
    return pl.pallas_call(
        joined_block,
        out_shape=tuple(
            jax.ShapeDtypeStruct((rows, part), own.dtype)
            for rows in (3 * size, size // 2, size // 2)
        ),
        name="joined",
    )(own, below, above)


def stats_block(scalars_ref, near_ref, far_ref, gain_ref, labels_ref, *refs, offsets):
    count = len(offsets)
    block_refs, (low_ref, high_ref, out_ref, weights_ref) = refs[:count], refs[count:]
    rows, width = near_ref.shape[2], weights_ref.shape[0]
    part = weights_ref.shape[1]

    @pl.when((pl.program_id(0) == 0) & (pl.program_id(1) == 0))
    def _():
        size = 2 * low_ref.shape[0]
        planes = width // size

        def place(offset):
            plane = (scalars_ref[1] + offset + planes) % planes
            return pl.multiple_of(plane * size, size)

        for ref, around in zip(block_refs, offsets):
            for k, offset in enumerate(around):
                weights_ref[pl.ds(place(offset), size), :] = ref[k * size : (k + 1) * size, :]
        middle = place(planes // 2)
        weights_ref[pl.ds(middle, size // 2), :] = low_ref[...]
        middle = pl.multiple_of(middle + size // 2, size // 2)
        weights_ref[pl.ds(middle, size // 2), :] = high_ref[...]

    north = scalars_ref[2] == 0
    pieces = []
    for k in range(near_ref.shape[1]):
        near = near_ref[0, k].astype(jnp.float32)
        far = far_ref[0, k].astype(jnp.float32)
        pieces += [jnp.where(north, near, far), jnp.where(north, far, near)]
    squares = pieces[0] * pieces[0]
    for piece in pieces[1:]:
        squares = squares + piece * piece
    mean_square = jnp.sum(squares, axis=1, keepdims=True) / width
    scale = lax.rsqrt(mean_square + epsilon)
    normed = jnp.concatenate(
        [
            (piece * scale * gain_ref[0:1, k * LANES : (k + 1) * LANES]).astype(jnp.bfloat16)
            for k, piece in enumerate(pieces)
        ],
        axis=1,
    )
    logits = jnp.dot(normed, weights_ref[...], preferred_element_type=jnp.float32)
    columns = lax.broadcasted_iota(jnp.int32, (rows, part), 1)
    logits = jnp.where(columns < scalars_ref[0], logits, -jnp.inf)
    top = jnp.max(logits, axis=1, keepdims=True)
    total = jnp.sum(jnp.exp(logits - top), axis=1, keepdims=True)
    label = jnp.broadcast_to(labels_ref[0:1, :], (LANES, rows)).T[:, 0:1]
    picked = jnp.sum(jnp.where(columns == label, logits, 0.0), axis=1, keepdims=True)
    lane = lax.broadcasted_iota(jnp.int32, (rows, LANES), 1)
    both = jnp.where(lane == 0, top + jnp.log(total), picked)
    out_ref[...] = both.T[0:8]


def row_stats(near, far, gain, blocks, labels, valid):
    sources, slices = near.shape[:2]
    steps = OWN_ROWS // ROW_BLOCK
    width = slices * 2 * LANES
    found, halves = blocks
    arrays = [array for array, _ in found] + list(halves)
    part = arrays[0].shape[1]
    plane, core = lax.axis_index("z"), lax.axis_index("c")
    scalars = jnp.stack([valid, plane, core]).astype(jnp.int32)
    rows = pl.BlockSpec((1, slices, ROW_BLOCK, LANES), lambda x, i, scalars: (x, 0, i, 0))
    whole = [
        pl.BlockSpec(array.shape, lambda x, i, scalars: (0, 0)) for array in (gain, *arrays)
    ]
    stats = pl.pallas_call(
        functools.partial(stats_block, offsets=tuple(around for _, around in found)),
        grid_spec=pltpu.PrefetchScalarGridSpec(
            num_scalar_prefetch=1,
            grid=(sources, steps),
            in_specs=[
                rows,
                rows,
                whole[0],
                pl.BlockSpec((1, ROW_BLOCK), lambda x, i, scalars: (0, x * steps + i)),
                *whole[1:],
            ],
            out_specs=pl.BlockSpec((8, ROW_BLOCK), lambda x, i, scalars: (0, x * steps + i)),
            scratch_shapes=[pltpu.VMEM((width, part), jnp.bfloat16)],
        ),
        out_shape=jax.ShapeDtypeStruct((8, sources * OWN_ROWS), jnp.float32),
        name="row_stats",
    )(scalars, near, far, gain, labels.reshape(1, -1), *arrays)
    return stats[:2]


def on_device_body(tokens, span_bounds, owner, decoder_states, norm_gain, embedding):
    planes, columns = lax.axis_size("z"), lax.axis_size("x")
    capacity = OWN_ROWS // (planes * columns)
    shard_rows = embedding.shape[0]
    mixed = exchanged_embedding(embedding)
    blocks = gathered_blocks(mixed)
    packed, sent_labels = packed_rows(tokens, span_bounds, owner, decoder_states)
    group = columns * capacity
    width = packed.shape[1]
    digits = jnp.stack([sent_labels // 256, sent_labels % 256]).astype(jnp.bfloat16)
    digits = digits.reshape(2, planes, group).swapaxes(0, 1)
    digits = jnp.pad(digits, ((0, 0), (0, 6), (0, width - group)))
    sent = jnp.concatenate([packed.reshape(planes, group, width), digits], axis=1)
    arrived = lax.all_to_all(sent, "z", split_axis=0, concat_axis=0, tiled=True)
    bundle = jnp.concatenate(
        [
            arrived[:, :group].reshape(OWN_ROWS, width),
            arrived[:, group],
            arrived[:, group + 1],
        ],
        axis=0,
    )
    near = broadcast_all(bundle, ("x", "y"))
    far = swap_cores(near)
    near = near.reshape(columns, -1, *bundle.shape)
    far = far.reshape(near.shape)
    tags = near[:, 0, OWN_ROWS : OWN_ROWS + 2 * planes].astype(jnp.int32)
    tags = tags.reshape(columns, 2, planes, width)[..., :group]
    row_labels = tags[:, 0] * 256 + tags[:, 1] - 1
    part = mixed.shape[1]
    here = lax.axis_index("x")
    valid = jnp.minimum(shard_rows - here * part, part)
    local_label = row_labels - (lax.axis_index(VOC) * shard_rows + here * part)
    local_label = jnp.where((local_label >= 0) & (local_label < valid), local_label, -1)
    gain = (norm_gain.astype(jnp.float32) * norm_gain.shape[0] ** (-0.5)).reshape(1, -1)
    stats = row_stats(near, far, gain, blocks, local_label.reshape(-1), valid)
    stats = stats.reshape(2, columns, planes, columns, capacity).transpose(3, 0, 2, 1, 4)
    stats = stats.reshape(columns, 1, 2, OWN_ROWS)
    copies = jnp.broadcast_to(stats, (columns, lax.axis_size(VOC), 2, OWN_ROWS))
    copies = copies.reshape(-1, 2, OWN_ROWS)
    parts = lax.all_to_all(copies, PLANE, split_axis=0, concat_axis=0, tiled=True)
    row_top = jnp.max(parts[:, 0], axis=0)
    row_loss = row_top + jnp.log(jnp.sum(jnp.exp(parts[:, 0] - row_top[None]), axis=0))
    row_loss = row_loss - jnp.sum(parts[:, 1], axis=0)
    mine = row_labels.reshape(columns, planes, columns, capacity)
    mine = lax.dynamic_index_in_dim(mine, here, axis=2, keepdims=False)
    live = mine.swapaxes(0, 1).reshape(-1) >= 0
    return jnp.where(live, row_loss, 0.0).astype(jnp.float32)


def solution(mesh):
    dp, vocab = mesh.shape["dp"], mesh.shape["vocab"]
    torus = Mesh(mesh.devices.reshape(dp // 4, 4, vocab // 2, 2), ("z", "x", "y", "c"))
    in_specs = (
        P(DP, None),
        P(DP, None, None),
        P(DP, None, None),
        P(DP, None, VOC),
        P(),
        P(VOC, DP),
    )
    return jax.shard_map(
        on_device_body, mesh=torus, in_specs=in_specs, out_specs=P(DP), check_vma=False
    )
```

time: 197 us -> 203 us (1.030)
  blocking collectives: 61.2 us -> 78 us
  Pallas kernels: 25.2 us -> 18.8 us
  local copies, waits for them, and re-layouts: 11.1 us -> 5.68 us
  waiting for transfers between devices: 33.5 us -> 36.3 us
    all_to_all x1 -> x2, blocking collectives: 20.7 us -> 36.3 us  [the longest x1 28.2 us: on_device_body(): arrived = lax.all_to_all(sent, 'z', split_axis=0, concat_axis=0, tiled=True)]
    pallas_call x1, Pallas kernels: 10.6 us -> 1.84 us  [joined(): pl.pallas_call(joined_block, out_shape=tuple((jax.ShapeDtypeStruct((rows,...]
    ppermute x8, waiting for transfers between devices: 20.4 us -> 28.3 us  [shifted(): lax.ppermute(value, 'z', [(k, (k + step) % planes) for k in range(planes)])]
    all_to_all x1 -> x0, starting transfers between devices: 4.83 us -> none  [exchanged_embedding(): mixed = lax.all_to_all(split, 'x', split_axis=0, concat_axis=0, tiled=True)]
    all_to_all x1 -> x0, waiting for transfers between devices: 4.73 us -> none  [exchanged_embedding(): mixed = lax.all_to_all(split, 'x', split_axis=0, concat_axis=0, tiled=True)]
    pallas_call x1, Pallas kernels: 14.6 us -> 16.9 us  [row_stats(): pl.pallas_call(functools.partial(stats_block, offsets=tuple((around for _...]
  transfers between devices with their start and end apart: 11 -> 10, of which waited for: 6 -> 5; matrix products, arithmetic and copies ran while one was open for 4% -> 1% of each run, Pallas kernels for 5% -> 1%
where the time goes in v4:
time: 203 us; the launch traced here: 202 us
  blocking collectives  78 us (38%)
  starting transfers between devices  56.5 us (28%)
  waiting for transfers between devices  36.3 us (18%)
  Pallas kernels  18.8 us (9%)
  local copies, waits for them, and re-layouts  5.68 us (3%)
  other arithmetic  5.48 us (3%)
    ppermute x8, starting transfers between devices, shifted(): lax.ppermute(value, 'z', [(k, (k + step) % planes) for k in range(planes)])  42.6 us
    all_to_all x1, blocking collectives, broadcast_all(): return lax.all_to_all(copies, axis, split_axis=0, concat_axis=0, tiled=True)  41.7 us
    ppermute x8, waiting for transfers between devices, shifted(): lax.ppermute(value, 'z', [(k, (k + step) % planes) for k in range(planes)])  28.3 us
    all_to_all x1, blocking collectives, on_device_body(): arrived = lax.all_to_all(sent, 'z', split_axis=0, concat_axis=0, tiled=True)  28.2 us
    pallas_call x1, Pallas kernels, row_stats(): pl.pallas_call(functools.partial(stats_block, offsets=tuple((around for _...  16.9 us
    ppermute x1, starting transfers between devices, swap_cores(): return lax.ppermute(value, 'c', [(0, 1), (1, 0)])  8.7 us
    all_to_all x1, blocking collectives, exchanged_embedding(): mixed = lax.all_to_all(split, 'x', split_axis=0, concat_axis=0, tiled=True)  8.09 us
    all_to_all x1, waiting for transfers between devices, on_device_body(): lax.all_to_all(copies, PLANE, split_axis=0, concat_axis=0, tiled=True)  8 us
  transfers between devices with their start and end apart: 10, of which 5 were waited for; matrix products, arithmetic and copies ran while one was open for 1% of the time, Pallas kernels for 1%

profile of v4, /device:TPU:1, one launch (start us, length us, event | category | flops | bytes accessed | tf_op | source)
XLA Modules:
  0.0 202.5 jit_solution(2373185726600893415)
XLA Ops:
  0.0 0.0 copy-start
  0.0 0.1 lt.49
  0.1 0.7 reduce.2
  0.8 0.1 reshape.258
  0.9 0.4 fusion.8
  1.3 0.8 fusion.27
  2.1 0.1 broadcast_in_dim.58
  2.2 0.1 reshape.261
  2.3 1.2 select_reduce_fusion.1
  3.5 0.1 add.112
  3.5 0.1 broadcast_in_dim.57
  3.6 0.2 sub.54
  3.9 0.7 select_reduce_fusion
  4.5 0.1 reduce_sum.50
  4.7 0.0 copy-done
  4.7 1.0 fusion.4
  5.8 28.2 %all_to_all.20 = bf16[16,56,128]{2,1,0:T(8,128)(2,1)S(1)} all-to-all(bf16[16,56,128]{2,1,0:T(8,128)(2,1)S(1)} %fusion.12), channel_id=1, replica_groups=mesh['z'=16,'x'=4,'y'=4,'c'=2] {'z'}, dimensions={0} | all-to-all | bytes 458752 | tf_op jit(solution)/shard_map/all_to_all | solution.py:225
  34.1 0.4 broadcast_in_dim.63
  34.5 0.0 copy-start.2
  34.5 0.0 copy-start.5
  34.5 41.7 %all_to_all.21 = bf16[16,800,128]{2,1,0:T(8,128)(2,1)S(1)} all-to-all(bf16[16,800,128]{2,1,0:T(8,128)(2,1)S(1)} %broadcast_in_dim.63), channel_id=1, replica_groups=mesh['z'=16,'x'=4,'y'=4,'c'=2] {'x','y'}, dimensions={0} | all-to-all | bytes 6553600 | tf_op jit(solution)/shard_map/all_to_all | solution.py:28
  76.2 0.0 copy-start.1
  76.2 8.7 %collective-permute-start = (bf16[16,800,128]{2,1,0:T(8,128)(2,1)S(1)}, bf16[16,800,128]{2,1,0:T(8,128)(2,1)}, u32[]{:S(2)}, u32[]{:S(2)}) collective-permute-start(bf16[16,800,128]{2,1,0:T(8,128)(2,1)S(1)} %all_to_all.21), channel_id=1, source_target_pairs={{0,1},{1,0},{2,3},{3,2},{4,5},{5,4},{6,7},{7,6},{8,9},{9,8},{10,11... | collective-permute-start | bytes 9830408 | tf_op jit(solution)/shard_map/ppermute | solution.py:32
  84.9 0.0 copy-done.2
  85.0 8.1 %all_to_all.22 = bf16[4,16,1024]{2,1,0:T(8,128)(2,1)} all-to-all(bf16[4,16,1024]{2,1,0:T(8,128)(2,1)S(1)} %pad_maximum_fusion.1), channel_id=1, replica_groups=mesh['z'=16,'x'=4,'y'=4,'c'=2] {'x'}, dimensions={0} | all-to-all | bytes 262144 | tf_op jit(solution)/shard_map/all_to_all | solution.py:46
  93.1 9.4 %collective-permute-start.2 = (bf16[64,1024]{1,0:T(8,128)(2,1)}, bf16[64,1024]{1,0:T(8,128)(2,1)}, u32[]{:S(2)}, u32[]{:S(2)}) collective-permute-start(bf16[64,1024]{1,0:T(8,128)(2,1)} %bitcast.22.own_ref), channel_id=1, source_target_pairs={{0,352},{32,384},{64,416},{96,448},{128,480},{160,0},{192,32},{224... | collective-permute-start | bytes 393224 | tf_op jit(solution)/shard_map/ppermute | solution.py:90
  102.5 2.4 %collective-permute-start.1 = (bf16[64,1024]{1,0:T(8,128)(2,1)}, bf16[64,1024]{1,0:T(8,128)(2,1)}, u32[]{:S(2)}, u32[]{:S(2)}) collective-permute-start(bf16[64,1024]{1,0:T(8,128)(2,1)} %bitcast.22.own_ref), channel_id=1, source_target_pairs={{0,160},{32,192},{64,224},{96,256},{128,288},{160,320},{192,352},{... | collective-permute-start | bytes 393224 | tf_op jit(solution)/shard_map/ppermute | solution.py:90
  104.8 0.0 copy-done.5
  104.8 0.6 convert_multiply_fusion
  105.4 0.7 pad_add_fusion.scalars_ref
  106.1 0.0 collective-permute-done.2.above_ref
  106.1 14.2 %collective-permute-done.1.below_ref = bf16[64,1024]{1,0:T(8,128)(2,1)} collective-permute-done((bf16[64,1024]{1,0:T(8,128)(2,1)}, bf16[64,1024]{1,0:T(8,128)(2,1)}, u32[]{:S(2)}, u32[]{:S(2)}) %collective-permute-start.1) | collective-permute-done | bytes 131104 | tf_op jit(solution)/shard_map/ppermute | solution.py:90
  120.2 1.8 joined.1
  122.1 3.5 %collective-permute-start.6 = (bf16[192,1024]{1,0:T(8,128)(2,1)}, bf16[192,1024]{1,0:T(8,128)(2,1)}, u32[]{:S(2)}, u32[]{:S(2)}) collective-permute-start(bf16[192,1024]{1,0:T(8,128)(2,1)} %get-tuple-element.8.refs_0_), channel_id=1, source_target_pairs={{0,448},{32,480},{64,0},{96,32},{128,64},{160,96},{192,128},{224,1... | collective-permute-start | bytes 1179656 | tf_op jit(solution)/shard_map/ppermute | solution.py:90
  125.6 6.1 %collective-permute-start.5 = (bf16[192,1024]{1,0:T(8,128)(2,1)}, bf16[192,1024]{1,0:T(8,128)(2,1)}, u32[]{:S(2)}, u32[]{:S(2)}) collective-permute-start(bf16[192,1024]{1,0:T(8,128)(2,1)} %get-tuple-element.8.refs_0_), channel_id=1, source_target_pairs={{0,64},{32,96},{64,128},{96,160},{128,192},{160,224},{192,256},{22... | collective-permute-start | bytes 1179656 | tf_op jit(solution)/shard_map/ppermute | solution.py:90
  131.7 1.9 collective-permute-start.7
  133.6 5.2 %collective-permute-start.8 = (bf16[32,1024]{1,0:T(8,128)(2,1)}, bf16[32,1024]{1,0:T(8,128)(2,1)}, u32[]{:S(2)}, u32[]{:S(2)}) collective-permute-start(bf16[32,1024]{1,0:T(8,128)(2,1)} %get-tuple-element.10), channel_id=1, source_target_pairs={{0,96},{32,128},{64,160},{96,192},{128,224},{160,256},{192,288},{2... | collective-permute-start | bytes 196616 | tf_op jit(solution)/shard_map/ppermute | solution.py:90
  138.9 0.1 sub.61
  139.0 5.5 %collective-permute-done.7.refs_5_ = bf16[32,1024]{1,0:T(8,128)(2,1)} collective-permute-done((bf16[32,1024]{1,0:T(8,128)(2,1)}, bf16[32,1024]{1,0:T(8,128)(2,1)}, u32[]{:S(2)}, u32[]{:S(2)}) %collective-permute-start.7) | collective-permute-done | bytes 65568 | tf_op jit(solution)/shard_map/ppermute | solution.py:90
  144.4 10.2 %collective-permute-start.4 = (bf16[192,1024]{1,0:T(8,128)(2,1)}, bf16[192,1024]{1,0:T(8,128)(2,1)S(1)}, u32[]{:S(2)}, u32[]{:S(2)}) collective-permute-start(bf16[192,1024]{1,0:T(8,128)(2,1)} %get-tuple-element.8.refs_0_), channel_id=1, source_target_pairs={{0,480},{32,0},{64,32},{96,64},{128,96},{160,128},{192,160},{224,1... | collective-permute-start | bytes 1179656 | tf_op jit(solution)/shard_map/ppermute | solution.py:90
  154.7 0.0 collective-permute-done.8.refs_6_
  154.7 3.9 %collective-permute-start.3 = (bf16[192,1024]{1,0:T(8,128)(2,1)}, bf16[192,1024]{1,0:T(8,128)(2,1)S(1)}, u32[]{:S(2)}, u32[]{:S(2)}) collective-permute-start(bf16[192,1024]{1,0:T(8,128)(2,1)} %get-tuple-element.8.refs_0_), channel_id=1, source_target_pairs={{0,32},{32,64},{64,96},{96,128},{128,160},{160,192},{192,224},{224... | collective-permute-start | bytes 1179656 | tf_op jit(solution)/shard_map/ppermute | solution.py:90
  158.6 0.6 and_select_fusion.labels_ref
  159.3 0.0 collective-permute-done.6.refs_4_
  159.3 0.0 collective-permute-done.5.refs_3_
  159.3 6.6 %collective-permute-done.4.refs_2_ = bf16[192,1024]{1,0:T(8,128)(2,1)S(1)} collective-permute-done((bf16[192,1024]{1,0:T(8,128)(2,1)}, bf16[192,1024]{1,0:T(8,128)(2,1)S(1)}, u32[]{:S(2)}, u32[]{:S(2)}) %collective-permute-start.4) | collective-permute-done | bytes 393248 | tf_op jit(solution)/shard_map/ppermute | solution.py:90
  165.9 2.1 %collective-permute-done.3.refs_1_ = bf16[192,1024]{1,0:T(8,128)(2,1)S(1)} collective-permute-done((bf16[192,1024]{1,0:T(8,128)(2,1)}, bf16[192,1024]{1,0:T(8,128)(2,1)S(1)}, u32[]{:S(2)}, u32[]{:S(2)}) %collective-permute-start.3) | collective-permute-done | bytes 393248 | tf_op jit(solution)/shard_map/ppermute | solution.py:90
  167.9 0.0 collective-permute-done
  167.9 0.0 copy-done.3
  167.9 0.7 copy-done.4
  168.7 0.0 copy-done.1
  168.7 16.9 %row_stats.1 = f32[8,3072]{1,0:T(8,128)} custom-call(s32[3]{0:T(128)} %pad_add_fusion.scalars_ref, bf16[4,4,800,128]{3,2,1,0:T(8,128)(2,1)} %bitcast.70, bf16[4,4,800,128]{3,2,1,0:T(8,128)(2,1)} %bitcast.15.far_ref, f32[1,1024]{1,0:T(1,128)} %bitcast.78, s32[1,3072]{1,0:T(1,128)} %and_select_fusion.labels_ref, bf16[192,1024]{1,0:T(8,128)(2,1)} %get-tuple-element.8.refs_0_, ...), custom_call_target="tpu_custom_call" | custom-call | tf_op jit(solution)/shard_map/row_stats/pallas_call | solution.py:191
  185.6 0.9 slice.76
  186.5 0.4 reshape.267
  186.9 0.2 copy.48
  187.1 0.3 broadcast_in_dim.64
  187.3 0.7 broadcast_in_dim.65
  188.1 5.2 %all-to-all-start.3 = ((f32[32,2,768]{2,1,0:T(2,128)}), f32[32,2,768]{2,1,0:T(2,128)S(1)}, u32[]{:S(2)}, u32[]{:S(2)}) async-start(f32[32,2,768]{2,1,0:T(2,128)} %bitcast.24), calls=%async_computation.3 | async-start | bytes 393216 | tf_op jit(solution)/shard_map/all_to_all | solution.py:252
  193.3 0.1 copy.51
  193.4 0.1 copy.47
  193.5 0.1 ge.29
  193.6 8.0 %all-to-all-done.3 = f32[32,2,768]{2,1,0:T(2,128)S(1)} async-done(((f32[32,2,768]{2,1,0:T(2,128)}), f32[32,2,768]{2,1,0:T(2,128)S(1)}, u32[]{:S(2)}, u32[]{:S(2)}) %all-to-all-start.3) | async-done | bytes 196640 | tf_op jit(solution)/shard_map/all_to_all | solution.py:252
  201.6 0.2 slice_reduce_fusion.1
  201.9 0.6 subtract_select_fusion
  (25 shorter events, 0.3 us)
Async XLA Ops:
  0.0 4.7 %copy-start = (bf16[9,80,128]{2,1,0:T(8,128)(2,1)S(1)}, bf16[9,80,128]{2,1,0:T(8,128)(2,1)}, u32[]{:S(2)}) copy-start(bf16[9,80,128]{2,1,0:T(8,128)(2,1)} %param.9) | copy-start | bytes 552964
  34.5 50.4 %copy-start.2 = (bf16[4016,16]{0,1:T(8,128)(2,1)S(1)}, bf16[4016,16]{0,1:T(8,128)(2,1)}, u32[]{:S(2)}) copy-start(bf16[4016,16]{0,1:T(8,128)(2,1)} %param.11) | copy-start | bytes 385540
  34.5 70.3 %copy-start.5 = (bf16[1024]{0:T(1024)(128)(2,1)S(1)}, bf16[1024]{0:T(1024)(128)(2,1)}, u32[]{:S(2)}) copy-start(bf16[1024]{0:T(1024)(128)(2,1)} %param.10) | copy-start | bytes 6148
  76.2 92.5 %copy-start.1 = (bf16[16,800,128]{2,1,0:T(8,128)(2,1)}, bf16[16,800,128]{2,1,0:T(8,128)(2,1)S(1)}, u32[]{:S(2)}) copy-start(bf16[16,800,128]{2,1,0:T(8,128)(2,1)S(1)} %all_to_all.21) | copy-start | bytes 9830404
  76.2 91.7 %collective-permute-start = (bf16[16,800,128]{2,1,0:T(8,128)(2,1)S(1)}, bf16[16,800,128]{2,1,0:T(8,128)(2,1)}, u32[]{:S(2)}, u32[]{:S(2)}) collective-permute-start(bf16[16,800,128]{2,1,0:T(8,128)(2,1)S(1)} %all_to_all.21), channel_id=1, source_target_pairs={{0,1},{1,0},{2,3},{3,2},{4,5},{5,4},{6,7},{7,6},{8,9},{9,8},{10,11... | collective-permute-start | bytes 9830408 | tf_op jit(solution)/shard_map/ppermute | solution.py:32
  93.1 13.0 %collective-permute-start.2 = (bf16[64,1024]{1,0:T(8,128)(2,1)}, bf16[64,1024]{1,0:T(8,128)(2,1)}, u32[]{:S(2)}, u32[]{:S(2)}) collective-permute-start(bf16[64,1024]{1,0:T(8,128)(2,1)} %bitcast.22.own_ref), channel_id=1, source_target_pairs={{0,352},{32,384},{64,416},{96,448},{128,480},{160,0},{192,32},{224... | collective-permute-start | bytes 393224 | tf_op jit(solution)/shard_map/ppermute | solution.py:90
  102.5 17.8 %collective-permute-start.1 = (bf16[64,1024]{1,0:T(8,128)(2,1)}, bf16[64,1024]{1,0:T(8,128)(2,1)}, u32[]{:S(2)}, u32[]{:S(2)}) collective-permute-start(bf16[64,1024]{1,0:T(8,128)(2,1)} %bitcast.22.own_ref), channel_id=1, source_target_pairs={{0,160},{32,192},{64,224},{96,256},{128,288},{160,320},{192,352},{... | collective-permute-start | bytes 393224 | tf_op jit(solution)/shard_map/ppermute | solution.py:90
  122.1 37.2 %collective-permute-start.6 = (bf16[192,1024]{1,0:T(8,128)(2,1)}, bf16[192,1024]{1,0:T(8,128)(2,1)}, u32[]{:S(2)}, u32[]{:S(2)}) collective-permute-start(bf16[192,1024]{1,0:T(8,128)(2,1)} %get-tuple-element.8.refs_0_), channel_id=1, source_target_pairs={{0,448},{32,480},{64,0},{96,32},{128,64},{160,96},{192,128},{224,1... | collective-permute-start | bytes 1179656 | tf_op jit(solution)/shard_map/ppermute | solution.py:90
  125.6 33.7 %collective-permute-start.5 = (bf16[192,1024]{1,0:T(8,128)(2,1)}, bf16[192,1024]{1,0:T(8,128)(2,1)}, u32[]{:S(2)}, u32[]{:S(2)}) collective-permute-start(bf16[192,1024]{1,0:T(8,128)(2,1)} %get-tuple-element.8.refs_0_), channel_id=1, source_target_pairs={{0,64},{32,96},{64,128},{96,160},{128,192},{160,224},{192,256},{22... | collective-permute-start | bytes 1179656 | tf_op jit(solution)/shard_map/ppermute | solution.py:90
  131.7 12.7 %collective-permute-start.7 = (bf16[32,1024]{1,0:T(8,128)(2,1)}, bf16[32,1024]{1,0:T(8,128)(2,1)}, u32[]{:S(2)}, u32[]{:S(2)}) collective-permute-start(bf16[32,1024]{1,0:T(8,128)(2,1)} %get-tuple-element.9), channel_id=1, source_target_pairs={{0,416},{32,448},{64,480},{96,0},{128,32},{160,64},{192,96},{224,1... | collective-permute-start | bytes 196616 | tf_op jit(solution)/shard_map/ppermute | solution.py:90
  133.6 21.1 %collective-permute-start.8 = (bf16[32,1024]{1,0:T(8,128)(2,1)}, bf16[32,1024]{1,0:T(8,128)(2,1)}, u32[]{:S(2)}, u32[]{:S(2)}) collective-permute-start(bf16[32,1024]{1,0:T(8,128)(2,1)} %get-tuple-element.10), channel_id=1, source_target_pairs={{0,96},{32,128},{64,160},{96,192},{128,224},{160,256},{192,288},{2... | collective-permute-start | bytes 196616 | tf_op jit(solution)/shard_map/ppermute | solution.py:90
  144.4 21.4 %collective-permute-start.4 = (bf16[192,1024]{1,0:T(8,128)(2,1)}, bf16[192,1024]{1,0:T(8,128)(2,1)S(1)}, u32[]{:S(2)}, u32[]{:S(2)}) collective-permute-start(bf16[192,1024]{1,0:T(8,128)(2,1)} %get-tuple-element.8.refs_0_), channel_id=1, source_target_pairs={{0,480},{32,0},{64,32},{96,64},{128,96},{160,128},{192,160},{224,1... | collective-permute-start | bytes 1179656 | tf_op jit(solution)/shard_map/ppermute | solution.py:90
  154.7 13.2 %collective-permute-start.3 = (bf16[192,1024]{1,0:T(8,128)(2,1)}, bf16[192,1024]{1,0:T(8,128)(2,1)S(1)}, u32[]{:S(2)}, u32[]{:S(2)}) collective-permute-start(bf16[192,1024]{1,0:T(8,128)(2,1)} %get-tuple-element.8.refs_0_), channel_id=1, source_target_pairs={{0,32},{32,64},{64,96},{96,128},{128,160},{160,192},{192,224},{224... | collective-permute-start | bytes 1179656 | tf_op jit(solution)/shard_map/ppermute | solution.py:90
  165.9 2.1 %copy-start.3 = (bf16[192,1024]{1,0:T(8,128)(2,1)}, bf16[192,1024]{1,0:T(8,128)(2,1)S(1)}, u32[]{:S(2)}) copy-start(bf16[192,1024]{1,0:T(8,128)(2,1)S(1)} %collective-permute-done.4.refs_2_) | copy-start | bytes 1179652
  167.9 0.8 copy-start.4
  188.1 13.6 %all-to-all-start.3 = ((f32[32,2,768]{2,1,0:T(2,128)}), f32[32,2,768]{2,1,0:T(2,128)S(1)}, u32[]{:S(2)}, u32[]{:S(2)}) async-start(f32[32,2,768]{2,1,0:T(2,128)} %bitcast.24), calls=%async_computation.3 | async-start | bytes 393216 | tf_op jit(solution)/shard_map/all_to_all | solution.py:252

commit v5 on v4

--- a/solution.py
+++ b/solution.py
@@ -19,7 +19,7 @@
 epsilon = 1e-06
 
 
-ROW_BLOCK = 384
+GROUP = 128
 LANES = 128
 
 
@@ -124,11 +124,12 @@
 
 def stats_block(scalars_ref, near_ref, far_ref, gain_ref, labels_ref, *refs, offsets):
     count = len(offsets)
-    block_refs, (low_ref, high_ref, out_ref, weights_ref) = refs[:count], refs[count:]
-    rows, width = near_ref.shape[2], weights_ref.shape[0]
+    block_refs = refs[:count]
+    low_ref, high_ref, out_ref, weights_ref, even_ref, odd_ref = refs[count:]
+    rows, width = even_ref.shape[0], weights_ref.shape[0]
     part = weights_ref.shape[1]
 
-    @pl.when((pl.program_id(0) == 0) & (pl.program_id(1) == 0))
+    @pl.when(pl.program_id(0) == 0)
     def _():
         size = 2 * low_ref.shape[0]
         planes = width // size
@@ -145,68 +146,102 @@
         middle = pl.multiple_of(middle + size // 2, size // 2)
         weights_ref[pl.ds(middle, size // 2), :] = high_ref[...]
 
-    north = scalars_ref[2] == 0
-    pieces = []
-    for k in range(near_ref.shape[1]):
-        near = near_ref[0, k].astype(jnp.float32)
-        far = far_ref[0, k].astype(jnp.float32)
-        pieces += [jnp.where(north, near, far), jnp.where(north, far, near)]
-    squares = pieces[0] * pieces[0]
-    for piece in pieces[1:]:
-        squares = squares + piece * piece
-    mean_square = jnp.sum(squares, axis=1, keepdims=True) / width
-    scale = lax.rsqrt(mean_square + epsilon)
-    normed = jnp.concatenate(
-        [
-            (piece * scale * gain_ref[0:1, k * LANES : (k + 1) * LANES]).astype(jnp.bfloat16)
-            for k, piece in enumerate(pieces)
-        ],
-        axis=1,
-    )
-    logits = jnp.dot(normed, weights_ref[...], preferred_element_type=jnp.float32)
-    columns = lax.broadcasted_iota(jnp.int32, (rows, part), 1)
-    logits = jnp.where(columns < scalars_ref[0], logits, -jnp.inf)
-    top = jnp.max(logits, axis=1, keepdims=True)
-    total = jnp.sum(jnp.exp(logits - top), axis=1, keepdims=True)
-    label = jnp.broadcast_to(labels_ref[0:1, :], (LANES, rows)).T[:, 0:1]
-    picked = jnp.sum(jnp.where(columns == label, logits, 0.0), axis=1, keepdims=True)
-    lane = lax.broadcasted_iota(jnp.int32, (rows, LANES), 1)
-    both = jnp.where(lane == 0, top + jnp.log(total), picked)
-    out_ref[...] = both.T[0:8]
+    def normed(first):
+        north = scalars_ref[2] == 0
+        pieces = []
+        for k in range(near_ref.shape[1]):
+            near = near_ref[0, k, first : first + rows, :].astype(jnp.float32)
+            far = far_ref[0, k, first : first + rows, :].astype(jnp.float32)
+            pieces += [jnp.where(north, near, far), jnp.where(north, far, near)]
+        squares = pieces[0] * pieces[0]
+        for piece in pieces[1:]:
+            squares = squares + piece * piece
+        mean_square = jnp.sum(squares, axis=1, keepdims=True) / width
+        scale = lax.rsqrt(mean_square + epsilon)
+        return jnp.concatenate(
+            [
+                (piece * scale * gain_ref[0:1, k * LANES : (k + 1) * LANES]).astype(jnp.bfloat16)
+                for k, piece in enumerate(pieces)
+            ],
+            axis=1,
+        )
+
+    def product(values):
+        return jnp.dot(values, weights_ref[...], preferred_element_type=jnp.float32)
+
+    def reduced(logits_ref, start):
+        for group in range(0, rows, GROUP):
+            place = pl.ds(pl.multiple_of(start + group, LANES), GROUP)
+            lane = lax.broadcasted_iota(jnp.int32, (GROUP, LANES), 1)
+            tiles = [
+                logits_ref[group : group + GROUP, first : first + LANES]
+                for first in range(0, part, LANES)
+            ]
+            tiles[-1] = jnp.where(lane < scalars_ref[0] - (part - LANES), tiles[-1], -jnp.inf)
+            top = functools.reduce(jnp.maximum, tiles)
+            top = jnp.max(top, axis=1, keepdims=True)
+            total = functools.reduce(jnp.add, [jnp.exp(tile - top) for tile in tiles])
+            total = jnp.sum(total, axis=1, keepdims=True)
+            label = jnp.broadcast_to(labels_ref[0:1, place], (LANES, GROUP)).T
+            ahead = label - lane
+            picked = jnp.zeros((GROUP, LANES), jnp.float32)
+            for k, tile in enumerate(tiles):
+                picked = jnp.where(ahead == k * LANES, tile, picked)
+            picked = jnp.sum(picked, axis=1, keepdims=True)
+            both = jnp.where(lane == 0, top + jnp.log(total), picked)
+            out_ref[:, place] = both.T[0:2]
+
+    step = pl.program_id(0)
+    last = pl.num_programs(0) - 1
+
+    @pl.when(step < last)
+    def _():
+        even_ref[...] = product(normed(0))
+        reduced(odd_ref, jnp.maximum(2 * step - 1, 0) * rows)
+        odd_ref[...] = product(normed(rows))
+        reduced(even_ref, 2 * step * rows)
+
+    @pl.when(step == last)
+    def _():
+        reduced(odd_ref, (2 * last - 1) * rows)
 
 
 def row_stats(near, far, gain, blocks, labels, valid):
     sources, slices = near.shape[:2]
-    steps = OWN_ROWS // ROW_BLOCK
     width = slices * 2 * LANES
     found, halves = blocks
     arrays = [array for array, _ in found] + list(halves)
     part = arrays[0].shape[1]
     plane, core = lax.axis_index("z"), lax.axis_index("c")
     scalars = jnp.stack([valid, plane, core]).astype(jnp.int32)
-    rows = pl.BlockSpec((1, slices, ROW_BLOCK, LANES), lambda x, i, scalars: (x, 0, i, 0))
+    rows = pl.BlockSpec(
+        (1, slices, OWN_ROWS, LANES), lambda x, scalars: (jnp.minimum(x, sources - 1), 0, 0, 0)
+    )
     whole = [
-        pl.BlockSpec(array.shape, lambda x, i, scalars: (0, 0)) for array in (gain, *arrays)
+        pl.BlockSpec(array.shape, lambda x, scalars: (0, 0)) for array in (gain, *arrays)
     ]
-    stats = pl.pallas_call(
+    return pl.pallas_call(
         functools.partial(stats_block, offsets=tuple(around for _, around in found)),
         grid_spec=pltpu.PrefetchScalarGridSpec(
             num_scalar_prefetch=1,
-            grid=(sources, steps),
+            grid=(sources + 1,),
             in_specs=[
                 rows,
                 rows,
                 whole[0],
-                pl.BlockSpec((1, ROW_BLOCK), lambda x, i, scalars: (0, x * steps + i)),
+                pl.BlockSpec((1, sources * OWN_ROWS), lambda x, scalars: (0, 0)),
                 *whole[1:],
             ],
-            out_specs=pl.BlockSpec((8, ROW_BLOCK), lambda x, i, scalars: (0, x * steps + i)),
-            scratch_shapes=[pltpu.VMEM((width, part), jnp.bfloat16)],
+            out_specs=pl.BlockSpec((2, sources * OWN_ROWS), lambda x, scalars: (0, 0)),
+            scratch_shapes=[
+                pltpu.VMEM((width, part), jnp.bfloat16),
+                pltpu.VMEM((OWN_ROWS // 2, part), jnp.float32),
+                pltpu.VMEM((OWN_ROWS // 2, part), jnp.float32),
+            ],
         ),
-        out_shape=jax.ShapeDtypeStruct((8, sources * OWN_ROWS), jnp.float32),
+        out_shape=jax.ShapeDtypeStruct((2, sources * OWN_ROWS), jnp.float32),
         name="row_stats",
     )(scalars, near, far, gain, labels.reshape(1, -1), *arrays)
-    return stats[:2]
 
 
 def on_device_body(tokens, span_bounds, owner, decoder_states, norm_gain, embedding):
@@ -239,6 +274,7 @@
     tags = tags.reshape(columns, 2, planes, width)[..., :group]
     row_labels = tags[:, 0] * 256 + tags[:, 1] - 1
     part = mixed.shape[1]
+    assert columns * part - shard_rows < LANES
     here = lax.axis_index("x")
     valid = jnp.minimum(shard_rows - here * part, part)
     local_label = row_labels - (lax.axis_index(VOC) * shard_rows + here * part)

time: 203 us -> 200 us (0.985)
  Pallas kernels: 18.8 us -> 15.9 us
    pallas_call x1, Pallas kernels: 16.9 us -> 14.1 us  [row_stats(): pl.pallas_call(functools.partial(stats_block, offsets=tuple((around for _...]
where the time goes in v5:
time: 200 us
  blocking collectives  78 us (39%)
  starting transfers between devices  56.5 us (28%)
  waiting for transfers between devices  36.4 us (18%)
  Pallas kernels  15.9 us (8%)
  local copies, waits for them, and re-layouts  5.52 us (3%)
  other arithmetic  5.44 us (3%)
    ppermute x8, starting transfers between devices, shifted(): lax.ppermute(value, 'z', [(k, (k + step) % planes) for k in range(planes)])  42.6 us
    all_to_all x1, blocking collectives, broadcast_all(): return lax.all_to_all(copies, axis, split_axis=0, concat_axis=0, tiled=True)  41.7 us
    ppermute x8, waiting for transfers between devices, shifted(): lax.ppermute(value, 'z', [(k, (k + step) % planes) for k in range(planes)])  28.4 us
    all_to_all x1, blocking collectives, on_device_body(): arrived = lax.all_to_all(sent, 'z', split_axis=0, concat_axis=0, tiled=True)  28.2 us
    pallas_call x1, Pallas kernels, row_stats(): pl.pallas_call(functools.partial(stats_block, offsets=tuple((around for _...  14.1 us
    ppermute x1, starting transfers between devices, swap_cores(): return lax.ppermute(value, 'c', [(0, 1), (1, 0)])  8.7 us
    all_to_all x1, blocking collectives, exchanged_embedding(): mixed = lax.all_to_all(split, 'x', split_axis=0, concat_axis=0, tiled=True)  8.09 us
    all_to_all x1, waiting for transfers between devices, on_device_body(): lax.all_to_all(copies, PLANE, split_axis=0, concat_axis=0, tiled=True)  8.02 us
  transfers between devices with their start and end apart: 10, of which 5 were waited for; matrix products, arithmetic and copies ran while one was open for 1% of the time, Pallas kernels for 1%

profile of v5, /device:TPU:1, one launch (start us, length us, event | category | flops | bytes accessed | tf_op | source)
XLA Modules:
  0.0 199.5 jit_solution(13711371567627054209)
XLA Ops:
  0.0 0.0 copy-start
  0.0 0.1 lt.49
  0.1 0.7 reduce.2
  0.8 0.1 reshape.258
  0.9 0.4 fusion.8
  1.3 0.8 fusion.27
  2.1 0.1 broadcast_in_dim.58
  2.2 0.1 reshape.261
  2.3 1.2 select_reduce_fusion.1
  3.5 0.1 add.112
  3.5 0.1 broadcast_in_dim.57
  3.6 0.2 sub.54
  3.9 0.7 select_reduce_fusion
  4.5 0.1 reduce_sum.50
  4.7 0.0 copy-done
  4.7 1.0 fusion.4
  5.8 28.2 %all_to_all.20 = bf16[16,56,128]{2,1,0:T(8,128)(2,1)S(1)} all-to-all(bf16[16,56,128]{2,1,0:T(8,128)(2,1)S(1)} %fusion.12), channel_id=1, replica_groups=mesh['z'=16,'x'=4,'y'=4,'c'=2] {'z'}, dimensions={0} | all-to-all | bytes 458752 | tf_op jit(solution)/shard_map/all_to_all | solution.py:260
  34.1 0.4 broadcast_in_dim.63
  34.5 0.0 copy-start.2
  34.5 0.0 copy-start.5
  34.5 41.7 %all_to_all.21 = bf16[16,800,128]{2,1,0:T(8,128)(2,1)S(1)} all-to-all(bf16[16,800,128]{2,1,0:T(8,128)(2,1)S(1)} %broadcast_in_dim.63), channel_id=1, replica_groups=mesh['z'=16,'x'=4,'y'=4,'c'=2] {'x','y'}, dimensions={0} | all-to-all | bytes 6553600 | tf_op jit(solution)/shard_map/all_to_all | solution.py:28
  76.2 0.0 copy-start.1
  76.2 8.7 %collective-permute-start = (bf16[16,800,128]{2,1,0:T(8,128)(2,1)S(1)}, bf16[16,800,128]{2,1,0:T(8,128)(2,1)}, u32[]{:S(2)}, u32[]{:S(2)}) collective-permute-start(bf16[16,800,128]{2,1,0:T(8,128)(2,1)S(1)} %all_to_all.21), channel_id=1, source_target_pairs={{0,1},{1,0},{2,3},{3,2},{4,5},{5,4},{6,7},{7,6},{8,9},{9,8},{10,11... | collective-permute-start | bytes 9830408 | tf_op jit(solution)/shard_map/ppermute | solution.py:32
  84.9 0.0 copy-done.2
  85.0 8.1 %all_to_all.22 = bf16[4,16,1024]{2,1,0:T(8,128)(2,1)} all-to-all(bf16[4,16,1024]{2,1,0:T(8,128)(2,1)S(1)} %pad_maximum_fusion.1), channel_id=1, replica_groups=mesh['z'=16,'x'=4,'y'=4,'c'=2] {'x'}, dimensions={0} | all-to-all | bytes 262144 | tf_op jit(solution)/shard_map/all_to_all | solution.py:46
  93.1 9.4 %collective-permute-start.2 = (bf16[64,1024]{1,0:T(8,128)(2,1)}, bf16[64,1024]{1,0:T(8,128)(2,1)}, u32[]{:S(2)}, u32[]{:S(2)}) collective-permute-start(bf16[64,1024]{1,0:T(8,128)(2,1)} %bitcast.22.own_ref), channel_id=1, source_target_pairs={{0,352},{32,384},{64,416},{96,448},{128,480},{160,0},{192,32},{224... | collective-permute-start | bytes 393224 | tf_op jit(solution)/shard_map/ppermute | solution.py:90
  102.5 2.4 %collective-permute-start.1 = (bf16[64,1024]{1,0:T(8,128)(2,1)}, bf16[64,1024]{1,0:T(8,128)(2,1)}, u32[]{:S(2)}, u32[]{:S(2)}) collective-permute-start(bf16[64,1024]{1,0:T(8,128)(2,1)} %bitcast.22.own_ref), channel_id=1, source_target_pairs={{0,160},{32,192},{64,224},{96,256},{128,288},{160,320},{192,352},{... | collective-permute-start | bytes 393224 | tf_op jit(solution)/shard_map/ppermute | solution.py:90
  104.8 0.0 copy-done.5
  104.8 0.6 convert_multiply_fusion
  105.4 0.6 pad_add_fusion.scalars_ref
  106.0 0.0 collective-permute-done.2.above_ref
  106.0 14.2 %collective-permute-done.1.below_ref = bf16[64,1024]{1,0:T(8,128)(2,1)} collective-permute-done((bf16[64,1024]{1,0:T(8,128)(2,1)}, bf16[64,1024]{1,0:T(8,128)(2,1)}, u32[]{:S(2)}, u32[]{:S(2)}) %collective-permute-start.1) | collective-permute-done | bytes 131104 | tf_op jit(solution)/shard_map/ppermute | solution.py:90
  120.2 1.8 joined.1
  122.1 3.5 %collective-permute-start.6 = (bf16[192,1024]{1,0:T(8,128)(2,1)}, bf16[192,1024]{1,0:T(8,128)(2,1)}, u32[]{:S(2)}, u32[]{:S(2)}) collective-permute-start(bf16[192,1024]{1,0:T(8,128)(2,1)} %get-tuple-element.8.refs_0_), channel_id=1, source_target_pairs={{0,448},{32,480},{64,0},{96,32},{128,64},{160,96},{192,128},{224,1... | collective-permute-start | bytes 1179656 | tf_op jit(solution)/shard_map/ppermute | solution.py:90
  125.6 6.1 %collective-permute-start.5 = (bf16[192,1024]{1,0:T(8,128)(2,1)}, bf16[192,1024]{1,0:T(8,128)(2,1)}, u32[]{:S(2)}, u32[]{:S(2)}) collective-permute-start(bf16[192,1024]{1,0:T(8,128)(2,1)} %get-tuple-element.8.refs_0_), channel_id=1, source_target_pairs={{0,64},{32,96},{64,128},{96,160},{128,192},{160,224},{192,256},{22... | collective-permute-start | bytes 1179656 | tf_op jit(solution)/shard_map/ppermute | solution.py:90
  131.7 1.9 collective-permute-start.7
  133.6 5.2 %collective-permute-start.8 = (bf16[32,1024]{1,0:T(8,128)(2,1)}, bf16[32,1024]{1,0:T(8,128)(2,1)}, u32[]{:S(2)}, u32[]{:S(2)}) collective-permute-start(bf16[32,1024]{1,0:T(8,128)(2,1)} %get-tuple-element.10), channel_id=1, source_target_pairs={{0,96},{32,128},{64,160},{96,192},{128,224},{160,256},{192,288},{2... | collective-permute-start | bytes 196616 | tf_op jit(solution)/shard_map/ppermute | solution.py:90
  138.9 0.1 sub.61
  139.0 5.5 %collective-permute-done.7.refs_5_ = bf16[32,1024]{1,0:T(8,128)(2,1)} collective-permute-done((bf16[32,1024]{1,0:T(8,128)(2,1)}, bf16[32,1024]{1,0:T(8,128)(2,1)}, u32[]{:S(2)}, u32[]{:S(2)}) %collective-permute-start.7) | collective-permute-done | bytes 65568 | tf_op jit(solution)/shard_map/ppermute | solution.py:90
  144.4 10.2 %collective-permute-start.4 = (bf16[192,1024]{1,0:T(8,128)(2,1)}, bf16[192,1024]{1,0:T(8,128)(2,1)S(1)}, u32[]{:S(2)}, u32[]{:S(2)}) collective-permute-start(bf16[192,1024]{1,0:T(8,128)(2,1)} %get-tuple-element.8.refs_0_), channel_id=1, source_target_pairs={{0,480},{32,0},{64,32},{96,64},{128,96},{160,128},{192,160},{224,1... | collective-permute-start | bytes 1179656 | tf_op jit(solution)/shard_map/ppermute | solution.py:90
  154.7 0.0 collective-permute-done.8.refs_6_
  154.7 3.9 %collective-permute-start.3 = (bf16[192,1024]{1,0:T(8,128)(2,1)}, bf16[192,1024]{1,0:T(8,128)(2,1)S(1)}, u32[]{:S(2)}, u32[]{:S(2)}) collective-permute-start(bf16[192,1024]{1,0:T(8,128)(2,1)} %get-tuple-element.8.refs_0_), channel_id=1, source_target_pairs={{0,32},{32,64},{64,96},{96,128},{128,160},{160,192},{192,224},{224... | collective-permute-start | bytes 1179656 | tf_op jit(solution)/shard_map/ppermute | solution.py:90
  158.6 0.6 and_select_fusion.labels_ref
  159.3 0.0 collective-permute-done.6.refs_4_
  159.3 0.0 collective-permute-done.5.refs_3_
  159.3 6.6 %collective-permute-done.4.refs_2_ = bf16[192,1024]{1,0:T(8,128)(2,1)S(1)} collective-permute-done((bf16[192,1024]{1,0:T(8,128)(2,1)}, bf16[192,1024]{1,0:T(8,128)(2,1)S(1)}, u32[]{:S(2)}, u32[]{:S(2)}) %collective-permute-start.4) | collective-permute-done | bytes 393248 | tf_op jit(solution)/shard_map/ppermute | solution.py:90
  165.9 0.0 copy-start.3
  165.9 2.1 %collective-permute-done.3.refs_1_ = bf16[192,1024]{1,0:T(8,128)(2,1)S(1)} collective-permute-done((bf16[192,1024]{1,0:T(8,128)(2,1)}, bf16[192,1024]{1,0:T(8,128)(2,1)S(1)}, u32[]{:S(2)}, u32[]{:S(2)}) %collective-permute-start.3) | collective-permute-done | bytes 393248 | tf_op jit(solution)/shard_map/ppermute | solution.py:90
  167.9 0.0 collective-permute-done
  167.9 0.0 copy-done.3
  167.9 0.7 copy-done.4
  168.7 0.0 copy-done.1
  168.7 14.1 %row_stats.1 = f32[2,3072]{1,0:T(2,128)} custom-call(s32[3]{0:T(128)} %pad_add_fusion.scalars_ref, bf16[4,4,800,128]{3,2,1,0:T(8,128)(2,1)} %bitcast.70, bf16[4,4,800,128]{3,2,1,0:T(8,128)(2,1)} %bitcast.15.far_ref, f32[1,1024]{1,0:T(1,128)} %bitcast.78, s32[1,3072]{1,0:T(1,128)} %and_select_fusion.labels_ref, bf16[192,1024]{1,0:T(8,128)(2,1)} %get-tuple-element.8.refs_0_, ...), custom_call_target="tpu_custom_call" | custom-call | tf_op jit(solution)/shard_map/row_stats/pallas_call | solution.py:223
  182.8 1.1 reshape.267
  183.9 0.2 copy.48
  184.1 0.3 broadcast_in_dim.64
  184.4 0.7 broadcast_in_dim.65
  185.1 5.2 %all-to-all-start.3 = ((f32[32,2,768]{2,1,0:T(2,128)}), f32[32,2,768]{2,1,0:T(2,128)S(1)}, u32[]{:S(2)}, u32[]{:S(2)}) async-start(f32[32,2,768]{2,1,0:T(2,128)} %bitcast.24), calls=%async_computation.3 | async-start | bytes 393216 | tf_op jit(solution)/shard_map/all_to_all | solution.py:288
  190.3 0.1 copy.51
  190.4 0.1 copy.47
  190.5 0.1 ge.29
  190.6 8.0 %all-to-all-done.3 = f32[32,2,768]{2,1,0:T(2,128)S(1)} async-done(((f32[32,2,768]{2,1,0:T(2,128)}), f32[32,2,768]{2,1,0:T(2,128)S(1)}, u32[]{:S(2)}, u32[]{:S(2)}) %all-to-all-start.3) | async-done | bytes 196640 | tf_op jit(solution)/shard_map/all_to_all | solution.py:288
  198.7 0.2 slice_reduce_fusion.1
  198.9 0.6 subtract_select_fusion
  (24 shorter events, 0.3 us)
Async XLA Ops:
  0.0 4.7 %copy-start = (bf16[9,80,128]{2,1,0:T(8,128)(2,1)S(1)}, bf16[9,80,128]{2,1,0:T(8,128)(2,1)}, u32[]{:S(2)}) copy-start(bf16[9,80,128]{2,1,0:T(8,128)(2,1)} %param.9) | copy-start | bytes 552964
  34.5 50.4 %copy-start.2 = (bf16[4016,16]{0,1:T(8,128)(2,1)S(1)}, bf16[4016,16]{0,1:T(8,128)(2,1)}, u32[]{:S(2)}) copy-start(bf16[4016,16]{0,1:T(8,128)(2,1)} %param.11) | copy-start | bytes 385540
  34.5 70.3 %copy-start.5 = (bf16[1024]{0:T(1024)(128)(2,1)S(1)}, bf16[1024]{0:T(1024)(128)(2,1)}, u32[]{:S(2)}) copy-start(bf16[1024]{0:T(1024)(128)(2,1)} %param.10) | copy-start | bytes 6148
  76.2 92.5 %copy-start.1 = (bf16[16,800,128]{2,1,0:T(8,128)(2,1)}, bf16[16,800,128]{2,1,0:T(8,128)(2,1)S(1)}, u32[]{:S(2)}) copy-start(bf16[16,800,128]{2,1,0:T(8,128)(2,1)S(1)} %all_to_all.21) | copy-start | bytes 9830404
  76.2 91.7 %collective-permute-start = (bf16[16,800,128]{2,1,0:T(8,128)(2,1)S(1)}, bf16[16,800,128]{2,1,0:T(8,128)(2,1)}, u32[]{:S(2)}, u32[]{:S(2)}) collective-permute-start(bf16[16,800,128]{2,1,0:T(8,128)(2,1)S(1)} %all_to_all.21), channel_id=1, source_target_pairs={{0,1},{1,0},{2,3},{3,2},{4,5},{5,4},{6,7},{7,6},{8,9},{9,8},{10,11... | collective-permute-start | bytes 9830408 | tf_op jit(solution)/shard_map/ppermute | solution.py:32
  93.1 13.0 %collective-permute-start.2 = (bf16[64,1024]{1,0:T(8,128)(2,1)}, bf16[64,1024]{1,0:T(8,128)(2,1)}, u32[]{:S(2)}, u32[]{:S(2)}) collective-permute-start(bf16[64,1024]{1,0:T(8,128)(2,1)} %bitcast.22.own_ref), channel_id=1, source_target_pairs={{0,352},{32,384},{64,416},{96,448},{128,480},{160,0},{192,32},{224... | collective-permute-start | bytes 393224 | tf_op jit(solution)/shard_map/ppermute | solution.py:90
  102.5 17.8 %collective-permute-start.1 = (bf16[64,1024]{1,0:T(8,128)(2,1)}, bf16[64,1024]{1,0:T(8,128)(2,1)}, u32[]{:S(2)}, u32[]{:S(2)}) collective-permute-start(bf16[64,1024]{1,0:T(8,128)(2,1)} %bitcast.22.own_ref), channel_id=1, source_target_pairs={{0,160},{32,192},{64,224},{96,256},{128,288},{160,320},{192,352},{... | collective-permute-start | bytes 393224 | tf_op jit(solution)/shard_map/ppermute | solution.py:90
  122.1 37.2 %collective-permute-start.6 = (bf16[192,1024]{1,0:T(8,128)(2,1)}, bf16[192,1024]{1,0:T(8,128)(2,1)}, u32[]{:S(2)}, u32[]{:S(2)}) collective-permute-start(bf16[192,1024]{1,0:T(8,128)(2,1)} %get-tuple-element.8.refs_0_), channel_id=1, source_target_pairs={{0,448},{32,480},{64,0},{96,32},{128,64},{160,96},{192,128},{224,1... | collective-permute-start | bytes 1179656 | tf_op jit(solution)/shard_map/ppermute | solution.py:90
  125.6 33.7 %collective-permute-start.5 = (bf16[192,1024]{1,0:T(8,128)(2,1)}, bf16[192,1024]{1,0:T(8,128)(2,1)}, u32[]{:S(2)}, u32[]{:S(2)}) collective-permute-start(bf16[192,1024]{1,0:T(8,128)(2,1)} %get-tuple-element.8.refs_0_), channel_id=1, source_target_pairs={{0,64},{32,96},{64,128},{96,160},{128,192},{160,224},{192,256},{22... | collective-permute-start | bytes 1179656 | tf_op jit(solution)/shard_map/ppermute | solution.py:90
  131.7 12.7 %collective-permute-start.7 = (bf16[32,1024]{1,0:T(8,128)(2,1)}, bf16[32,1024]{1,0:T(8,128)(2,1)}, u32[]{:S(2)}, u32[]{:S(2)}) collective-permute-start(bf16[32,1024]{1,0:T(8,128)(2,1)} %get-tuple-element.9), channel_id=1, source_target_pairs={{0,416},{32,448},{64,480},{96,0},{128,32},{160,64},{192,96},{224,1... | collective-permute-start | bytes 196616 | tf_op jit(solution)/shard_map/ppermute | solution.py:90
  133.6 21.1 %collective-permute-start.8 = (bf16[32,1024]{1,0:T(8,128)(2,1)}, bf16[32,1024]{1,0:T(8,128)(2,1)}, u32[]{:S(2)}, u32[]{:S(2)}) collective-permute-start(bf16[32,1024]{1,0:T(8,128)(2,1)} %get-tuple-element.10), channel_id=1, source_target_pairs={{0,96},{32,128},{64,160},{96,192},{128,224},{160,256},{192,288},{2... | collective-permute-start | bytes 196616 | tf_op jit(solution)/shard_map/ppermute | solution.py:90
  144.4 21.4 %collective-permute-start.4 = (bf16[192,1024]{1,0:T(8,128)(2,1)}, bf16[192,1024]{1,0:T(8,128)(2,1)S(1)}, u32[]{:S(2)}, u32[]{:S(2)}) collective-permute-start(bf16[192,1024]{1,0:T(8,128)(2,1)} %get-tuple-element.8.refs_0_), channel_id=1, source_target_pairs={{0,480},{32,0},{64,32},{96,64},{128,96},{160,128},{192,160},{224,1... | collective-permute-start | bytes 1179656 | tf_op jit(solution)/shard_map/ppermute | solution.py:90
  154.7 13.2 %collective-permute-start.3 = (bf16[192,1024]{1,0:T(8,128)(2,1)}, bf16[192,1024]{1,0:T(8,128)(2,1)S(1)}, u32[]{:S(2)}, u32[]{:S(2)}) collective-permute-start(bf16[192,1024]{1,0:T(8,128)(2,1)} %get-tuple-element.8.refs_0_), channel_id=1, source_target_pairs={{0,32},{32,64},{64,96},{96,128},{128,160},{160,192},{192,224},{224... | collective-permute-start | bytes 1179656 | tf_op jit(solution)/shard_map/ppermute | solution.py:90
  165.9 2.1 %copy-start.3 = (bf16[192,1024]{1,0:T(8,128)(2,1)}, bf16[192,1024]{1,0:T(8,128)(2,1)S(1)}, u32[]{:S(2)}) copy-start(bf16[192,1024]{1,0:T(8,128)(2,1)S(1)} %collective-permute-done.4.refs_2_) | copy-start | bytes 1179652
  167.9 0.8 copy-start.4
  185.1 13.6 %all-to-all-start.3 = ((f32[32,2,768]{2,1,0:T(2,128)}), f32[32,2,768]{2,1,0:T(2,128)S(1)}, u32[]{:S(2)}, u32[]{:S(2)}) async-start(f32[32,2,768]{2,1,0:T(2,128)} %bitcast.24), calls=%async_computation.3 | async-start | bytes 393216 | tf_op jit(solution)/shard_map/all_to_all | solution.py:288

commit v6 on v5

--- a/solution.py
+++ b/solution.py
@@ -23,9 +23,27 @@
 LANES = 128
 
 
-def broadcast_all(value, axis):
-    copies = jnp.broadcast_to(value, (lax.axis_size(axis), *value.shape))
-    return lax.all_to_all(copies, axis, split_axis=0, concat_axis=0, tiled=True)
+def spread_block(arrived_ref, tags_ref, out_ref, *, group):
+    planes = arrived_ref.shape[0]
+    for k in range(planes):
+        out_ref[0, k * group : (k + 1) * group, :] = arrived_ref[k, 0:group, :]
+    out_ref[0, planes * group : planes * group + planes, :] = tags_ref[...]
+
+
+def spread(arrived, tags, group, copies):
+    planes, _, width = arrived.shape
+    rows = planes * (group + 1)
+    return pl.pallas_call(
+        functools.partial(spread_block, group=group),
+        grid=(copies,),
+        in_specs=[
+            pl.BlockSpec(arrived.shape, lambda i: (0, 0, 0)),
+            pl.BlockSpec(tags.shape, lambda i: (0, 0)),
+        ],
+        out_specs=pl.BlockSpec((1, rows, width), lambda i: (i, 0, 0)),
+        out_shape=jax.ShapeDtypeStruct((copies, rows, width), arrived.dtype),
+        name="spread",
+    )(arrived, tags)
 
 
 def swap_cores(value):
@@ -254,25 +272,17 @@
     group = columns * capacity
     width = packed.shape[1]
     digits = jnp.stack([sent_labels // 256, sent_labels % 256]).astype(jnp.bfloat16)
-    digits = digits.reshape(2, planes, group).swapaxes(0, 1)
-    digits = jnp.pad(digits, ((0, 0), (0, 6), (0, width - group)))
+    digits = digits.reshape(2, planes, group).swapaxes(0, 1).reshape(planes, 1, 2 * group)
+    digits = jnp.pad(digits, ((0, 0), (0, 7), (0, width - 2 * group)))
     sent = jnp.concatenate([packed.reshape(planes, group, width), digits], axis=1)
     arrived = lax.all_to_all(sent, "z", split_axis=0, concat_axis=0, tiled=True)
-    bundle = jnp.concatenate(
-        [
-            arrived[:, :group].reshape(OWN_ROWS, width),
-            arrived[:, group],
-            arrived[:, group + 1],
-        ],
-        axis=0,
-    )
-    near = broadcast_all(bundle, ("x", "y"))
+    copies = spread(arrived, arrived[:, group], group, lax.axis_size(("x", "y")))
+    near = lax.all_to_all(copies, ("x", "y"), split_axis=0, concat_axis=0, tiled=True)
     far = swap_cores(near)
-    near = near.reshape(columns, -1, *bundle.shape)
+    near = near.reshape(columns, -1, *near.shape[1:])
     far = far.reshape(near.shape)
-    tags = near[:, 0, OWN_ROWS : OWN_ROWS + 2 * planes].astype(jnp.int32)
-    tags = tags.reshape(columns, 2, planes, width)[..., :group]
-    row_labels = tags[:, 0] * 256 + tags[:, 1] - 1
+    tags = near[:, 0, OWN_ROWS : OWN_ROWS + planes].astype(jnp.int32)
+    row_labels = tags[..., :group] * 256 + tags[..., group : 2 * group] - 1
     part = mixed.shape[1]
     assert columns * part - shard_rows < LANES
     here = lax.axis_index("x")

time: 200 us -> 207 us (1.035)
  waiting for transfers between devices: 36.4 us -> 47.5 us
  blocking collectives: 78 us -> 69.5 us
  Pallas kernels: 15.9 us -> 22.6 us
  starting transfers between devices: 56.5 us -> 52.4 us
    all_to_all x2 -> x1, blocking collectives: 49.8 us -> 41.3 us  [on_device_body(): lax.all_to_all(copies, ('x', 'y'), split_axis=0, concat_axis=0, tiled=True)]
    ppermute x8, starting transfers between devices: 42.6 us -> 34.9 us  [shifted(): lax.ppermute(value, 'z', [(k, (k + step) % planes) for k in range(planes)])]
    pallas_call x0 -> x1, Pallas kernels: none -> 6.61 us  [spread(): pl.pallas_call(functools.partial(spread_block, group=group), grid=(copies...]
    ppermute x8, waiting for transfers between devices: 28.4 us -> 34.5 us  [shifted(): lax.ppermute(value, 'z', [(k, (k + step) % planes) for k in range(planes)])]
    all_to_all x0 -> x1, waiting for transfers between devices: none -> 5 us  [exchanged_embedding(): mixed = lax.all_to_all(split, 'x', split_axis=0, concat_axis=0, tiled=True)]
    all_to_all x0 -> x1, starting transfers between devices: none -> 3.32 us  [exchanged_embedding(): mixed = lax.all_to_all(split, 'x', split_axis=0, concat_axis=0, tiled=True)]
  transfers between devices with their start and end apart: 10 -> 11, of which waited for: 5 -> 8; matrix products, arithmetic and copies ran while one was open for 1% -> 1% of each run, Pallas kernels for 1% -> 1%
where the time goes in v6:
time: 207 us; the launch traced here: 206 us
  blocking collectives  69.5 us (34%)
  starting transfers between devices  52.4 us (25%)
  waiting for transfers between devices  47.5 us (23%)
  Pallas kernels  22.6 us (11%)
  local copies, waits for them, and re-layouts  6.34 us (3%)
  other arithmetic  5.48 us (3%)
    all_to_all x1, blocking collectives, on_device_body(): lax.all_to_all(copies, ('x', 'y'), split_axis=0, concat_axis=0, tiled=True)  41.3 us
    ppermute x8, starting transfers between devices, shifted(): lax.ppermute(value, 'z', [(k, (k + step) % planes) for k in range(planes)])  34.9 us
    ppermute x8, waiting for transfers between devices, shifted(): lax.ppermute(value, 'z', [(k, (k + step) % planes) for k in range(planes)])  34.5 us
    all_to_all x1, blocking collectives, on_device_body(): arrived = lax.all_to_all(sent, 'z', split_axis=0, concat_axis=0, tiled=True)  28.2 us
    pallas_call x1, Pallas kernels, row_stats(): pl.pallas_call(functools.partial(stats_block, offsets=tuple((around for _...  14.1 us
    ppermute x1, starting transfers between devices, swap_cores(): return lax.ppermute(value, 'c', [(0, 1), (1, 0)])  8.7 us
    all_to_all x1, waiting for transfers between devices, on_device_body(): lax.all_to_all(copies, PLANE, split_axis=0, concat_axis=0, tiled=True)  8.04 us
    pallas_call x1, Pallas kernels, spread(): pl.pallas_call(functools.partial(spread_block, group=group), grid=(copies...  6.61 us
  transfers between devices with their start and end apart: 11, of which 8 were waited for; matrix products, arithmetic and copies ran while one was open for 1% of the time, Pallas kernels for 1%

profile of v6, /device:TPU:1, one launch (start us, length us, event | category | flops | bytes accessed | tf_op | source)
XLA Modules:
  0.0 205.6 jit_solution(16663944459226268331)
XLA Ops:
  0.0 0.0 copy-start
  0.0 0.1 lt.42
  0.1 0.7 reduce.2
  0.8 0.1 reshape.206
  0.9 0.4 fusion.8
  1.3 0.8 fusion.25
  2.1 0.1 broadcast_in_dim.55
  2.2 0.1 reshape.209
  2.3 1.2 select_reduce_fusion.1
  3.5 0.1 add.92
  3.5 0.1 broadcast_in_dim.54
  3.6 0.2 sub.42
  3.9 0.7 select_reduce_fusion
  4.5 0.1 reduce_sum.50
  4.7 0.1 reshape.219
  4.8 0.0 copy-done
  4.8 1.0 fusion.4
  5.9 28.2 %all_to_all.20.arrived_ref = bf16[16,56,128]{2,1,0:T(8,128)(2,1)S(1)} all-to-all(bf16[16,56,128]{2,1,0:T(8,128)(2,1)S(1)} %fusion.12), channel_id=1, replica_groups=mesh['z'=16,'x'=4,'y'=4,'c'=2] {'z'}, dimensions={0} | all-to-all | bytes 458752 | tf_op jit(solution)/shard_map/all_to_all | solution.py:278
  34.1 0.6 copy.71
  34.7 0.0 copy-done.2
  34.8 6.6 %spread.1 = bf16[16,784,128]{2,1,0:T(8,128)(2,1)} custom-call(bf16[16,56,128]{2,1,0:T(8,128)(2,1)} %copy-done.2, bf16[16,128]{1,0:T(8,128)(2,1)} %bitcast.63), custom_call_target="tpu_custom_call" | custom-call | tf_op jit(solution)/shard_map/spread/pallas_call | solution.py:36
  41.4 41.3 %all_to_all.21 = bf16[16,784,128]{2,1,0:T(8,128)(2,1)S(1)} all-to-all(bf16[16,784,128]{2,1,0:T(8,128)(2,1)} %spread.1), channel_id=1, replica_groups=mesh['z'=16,'x'=4,'y'=4,'c'=2] {'x','y'}, dimensions={0} | all-to-all | bytes 6422528 | tf_op jit(solution)/shard_map/all_to_all | solution.py:280
  82.7 8.7 %collective-permute-start = (bf16[16,784,128]{2,1,0:T(8,128)(2,1)S(1)}, bf16[16,784,128]{2,1,0:T(8,128)(2,1)}, u32[]{:S(2)}, u32[]{:S(2)}) collective-permute-start(bf16[16,784,128]{2,1,0:T(8,128)(2,1)S(1)} %all_to_all.21), channel_id=1, source_target_pairs={{0,1},{1,0},{2,3},{3,2},{4,5},{5,4},{6,7},{7,6},{8,9},{9,8},{10,11... | collective-permute-start | bytes 9633800 | tf_op jit(solution)/shard_map/ppermute | solution.py:50
  91.4 0.0 copy-done.4
  91.5 0.7 pad_maximum_fusion
  92.1 3.3 %all-to-all-start.2 = ((bf16[4,16,1024]{2,1,0:T(8,128)(2,1)}), bf16[4,16,1024]{2,1,0:T(8,128)(2,1)S(1)}, u32[]{:S(2)}, u32[]{:S(2)}) async-start(bf16[4,16,1024]{2,1,0:T(8,128)(2,1)} %pad_maximum_fusion), calls=%async_computation.2 | async-start | bytes 262144 | tf_op jit(solution)/shard_map/all_to_all | solution.py:64
  95.5 5.0 %all-to-all-done.2 = bf16[4,16,1024]{2,1,0:T(8,128)(2,1)S(1)} async-done(((bf16[4,16,1024]{2,1,0:T(8,128)(2,1)}), bf16[4,16,1024]{2,1,0:T(8,128)(2,1)S(1)}, u32[]{:S(2)}, u32[]{:S(2)}) %all-to-all-start.2) | async-done | bytes 131104 | tf_op jit(solution)/shard_map/all_to_all | solution.py:64
  100.5 9.4 %collective-permute-start.2 = (bf16[64,1024]{1,0:T(8,128)(2,1)S(1)}, bf16[64,1024]{1,0:T(8,128)(2,1)S(1)}, u32[]{:S(2)}, u32[]{:S(2)}) collective-permute-start(bf16[64,1024]{1,0:T(8,128)(2,1)S(1)} %bitcast.55), channel_id=1, source_target_pairs={{0,352},{32,384},{64,416},{96,448},{128,480},{160,0},{192,32},{224... | collective-permute-start | bytes 393224 | tf_op jit(solution)/shard_map/ppermute | solution.py:108
  109.9 2.4 %collective-permute-start.1 = (bf16[64,1024]{1,0:T(8,128)(2,1)S(1)}, bf16[64,1024]{1,0:T(8,128)(2,1)}, u32[]{:S(2)}, u32[]{:S(2)}) collective-permute-start(bf16[64,1024]{1,0:T(8,128)(2,1)S(1)} %bitcast.56), channel_id=1, source_target_pairs={{0,160},{32,192},{64,224},{96,256},{128,288},{160,320},{192,352},{... | collective-permute-start | bytes 393224 | tf_op jit(solution)/shard_map/ppermute | solution.py:108
  112.2 0.6 convert_multiply_fusion
  112.8 0.2 collective-permute-done.2.above_ref
  113.0 0.7 copy-done.5
  113.7 13.8 %collective-permute-done.1.below_ref = bf16[64,1024]{1,0:T(8,128)(2,1)} collective-permute-done((bf16[64,1024]{1,0:T(8,128)(2,1)S(1)}, bf16[64,1024]{1,0:T(8,128)(2,1)}, u32[]{:S(2)}, u32[]{:S(2)}) %collective-permute-start.1) | collective-permute-done | bytes 131104 | tf_op jit(solution)/shard_map/ppermute | solution.py:108
  127.5 1.9 joined.1
  129.3 4.7 %collective-permute-start.7 = (bf16[32,1024]{1,0:T(8,128)(2,1)}, bf16[32,1024]{1,0:T(8,128)(2,1)S(1)}, u32[]{:S(2)}, u32[]{:S(2)}) collective-permute-start(bf16[32,1024]{1,0:T(8,128)(2,1)} %get-tuple-element.9), channel_id=1, source_target_pairs={{0,416},{32,448},{64,480},{96,0},{128,32},{160,64},{192,96},{224,1... | collective-permute-start | bytes 196616 | tf_op jit(solution)/shard_map/ppermute | solution.py:108
  134.0 3.9 %collective-permute-start.8 = (bf16[32,1024]{1,0:T(8,128)(2,1)}, bf16[32,1024]{1,0:T(8,128)(2,1)S(1)}, u32[]{:S(2)}, u32[]{:S(2)}) collective-permute-start(bf16[32,1024]{1,0:T(8,128)(2,1)} %get-tuple-element.10), channel_id=1, source_target_pairs={{0,96},{32,128},{64,160},{96,192},{128,224},{160,256},{192,288},{2... | collective-permute-start | bytes 196616 | tf_op jit(solution)/shard_map/ppermute | solution.py:108
  137.9 0.6 pad_add_fusion.scalars_ref
  138.4 3.7 %collective-permute-start.6 = (bf16[192,1024]{1,0:T(8,128)(2,1)}, bf16[192,1024]{1,0:T(8,128)(2,1)}, u32[]{:S(2)}, u32[]{:S(2)}) collective-permute-start(bf16[192,1024]{1,0:T(8,128)(2,1)} %get-tuple-element.8.refs_0_), channel_id=1, source_target_pairs={{0,448},{32,480},{64,0},{96,32},{128,64},{160,96},{192,128},{224,1... | collective-permute-start | bytes 1179656 | tf_op jit(solution)/shard_map/ppermute | solution.py:108
  142.1 5.7 %collective-permute-start.5 = (bf16[192,1024]{1,0:T(8,128)(2,1)}, bf16[192,1024]{1,0:T(8,128)(2,1)}, u32[]{:S(2)}, u32[]{:S(2)}) collective-permute-start(bf16[192,1024]{1,0:T(8,128)(2,1)} %get-tuple-element.8.refs_0_), channel_id=1, source_target_pairs={{0,64},{32,96},{64,128},{96,160},{128,192},{160,224},{192,256},{22... | collective-permute-start | bytes 1179656 | tf_op jit(solution)/shard_map/ppermute | solution.py:108
  147.8 0.0 collective-permute-done.7.refs_5_
  147.8 0.0 copy-start.6
  147.8 3.4 %collective-permute-start.4 = (bf16[192,1024]{1,0:T(8,128)(2,1)}, bf16[192,1024]{1,0:T(8,128)(2,1)}, u32[]{:S(2)}, u32[]{:S(2)}) collective-permute-start(bf16[192,1024]{1,0:T(8,128)(2,1)} %get-tuple-element.8.refs_0_), channel_id=1, source_target_pairs={{0,480},{32,0},{64,32},{96,64},{128,96},{160,128},{192,160},{224,1... | collective-permute-start | bytes 1179656 | tf_op jit(solution)/shard_map/ppermute | solution.py:108
  151.2 0.0 collective-permute-done.8.refs_6_
  151.2 1.9 collective-permute-start.3
  153.2 0.1 and_select_fusion
  153.3 0.7 reshape_reshape.3.labels_ref
  154.0 9.7 %collective-permute-done.6.refs_4_ = bf16[192,1024]{1,0:T(8,128)(2,1)} collective-permute-done((bf16[192,1024]{1,0:T(8,128)(2,1)}, bf16[192,1024]{1,0:T(8,128)(2,1)}, u32[]{:S(2)}, u32[]{:S(2)}) %collective-permute-start.6) | collective-permute-done | bytes 393248 | tf_op jit(solution)/shard_map/ppermute | solution.py:108
  163.7 2.5 %collective-permute-done.5.refs_3_ = bf16[192,1024]{1,0:T(8,128)(2,1)} collective-permute-done((bf16[192,1024]{1,0:T(8,128)(2,1)}, bf16[192,1024]{1,0:T(8,128)(2,1)}, u32[]{:S(2)}, u32[]{:S(2)}) %collective-permute-start.5) | collective-permute-done | bytes 393248 | tf_op jit(solution)/shard_map/ppermute | solution.py:108
  166.2 4.0 %collective-permute-done.4.refs_2_ = bf16[192,1024]{1,0:T(8,128)(2,1)} collective-permute-done((bf16[192,1024]{1,0:T(8,128)(2,1)}, bf16[192,1024]{1,0:T(8,128)(2,1)}, u32[]{:S(2)}, u32[]{:S(2)}) %collective-permute-start.4) | collective-permute-done | bytes 393248 | tf_op jit(solution)/shard_map/ppermute | solution.py:108
  170.2 4.2 %collective-permute-done.3.refs_1_ = bf16[192,1024]{1,0:T(8,128)(2,1)} collective-permute-done((bf16[192,1024]{1,0:T(8,128)(2,1)}, bf16[192,1024]{1,0:T(8,128)(2,1)}, u32[]{:S(2)}, u32[]{:S(2)}) %collective-permute-start.3) | collective-permute-done | bytes 393248 | tf_op jit(solution)/shard_map/ppermute | solution.py:108
  174.5 0.0 collective-permute-done
  174.5 0.0 copy-done.6
  174.5 14.1 %row_stats.1 = f32[2,3072]{1,0:T(2,128)} custom-call(s32[3]{0:T(128)} %pad_add_fusion.scalars_ref, bf16[4,4,784,128]{3,2,1,0:T(8,128)(2,1)} %bitcast.53, bf16[4,4,784,128]{3,2,1,0:T(8,128)(2,1)} %bitcast.15.far_ref, f32[1,1024]{1,0:T(1,128)} %bitcast.62, s32[1,3072]{1,0:T(1,128)} %reshape_reshape.3.labels_ref, bf16[192,1024]{1,0:T(8,128)(2,1)} %get-tuple-element.8.refs_0_, ...), custom_call_target="tpu_custom_call" | custom-call | tf_op jit(solution)/shard_map/row_stats/pallas_call | solution.py:241
  188.6 1.1 reshape.216
  189.7 0.2 copy.52
  189.9 0.3 broadcast_in_dim.60
  190.2 0.7 broadcast_in_dim.61
  190.9 5.5 %all-to-all-start.3 = ((f32[32,2,768]{2,1,0:T(2,128)}), f32[32,2,768]{2,1,0:T(2,128)S(1)}, u32[]{:S(2)}, u32[]{:S(2)}) async-start(f32[32,2,768]{2,1,0:T(2,128)} %bitcast.24), calls=%async_computation.3 | async-start | bytes 393216 | tf_op jit(solution)/shard_map/all_to_all | solution.py:298
  196.4 0.1 copy.55
  196.5 0.1 copy.51
  196.6 0.1 ge.22
  196.7 8.0 %all-to-all-done.3 = f32[32,2,768]{2,1,0:T(2,128)S(1)} async-done(((f32[32,2,768]{2,1,0:T(2,128)}), f32[32,2,768]{2,1,0:T(2,128)S(1)}, u32[]{:S(2)}, u32[]{:S(2)}) %all-to-all-start.3) | async-done | bytes 196640 | tf_op jit(solution)/shard_map/all_to_all | solution.py:298
  204.8 0.2 slice_reduce_fusion.1
  205.0 0.6 subtract_select_fusion
  (28 shorter events, 0.3 us)
Async XLA Ops:
  0.0 4.8 %copy-start = (bf16[9,80,128]{2,1,0:T(8,128)(2,1)S(1)}, bf16[9,80,128]{2,1,0:T(8,128)(2,1)}, u32[]{:S(2)}) copy-start(bf16[9,80,128]{2,1,0:T(8,128)(2,1)} %param.9) | copy-start | bytes 552964
  34.1 0.7 copy-start.2
  41.4 50.1 %copy-start.4 = (bf16[4016,16]{0,1:T(8,128)(2,1)S(1)}, bf16[4016,16]{0,1:T(8,128)(2,1)}, u32[]{:S(2)}) copy-start(bf16[4016,16]{0,1:T(8,128)(2,1)} %param.11) | copy-start | bytes 385540
  41.4 70.9 %copy-start.8 = (bf16[1024]{0:T(1024)(128)(2,1)S(1)}, bf16[1024]{0:T(1024)(128)(2,1)}, u32[]{:S(2)}) copy-start(bf16[1024]{0:T(1024)(128)(2,1)} %param.10) | copy-start | bytes 6148
  82.7 91.8 %copy-start.1 = (bf16[16,784,128]{2,1,0:T(8,128)(2,1)}, bf16[16,784,128]{2,1,0:T(8,128)(2,1)S(1)}, u32[]{:S(2)}) copy-start(bf16[16,784,128]{2,1,0:T(8,128)(2,1)S(1)} %all_to_all.21) | copy-start | bytes 9633796
  82.7 91.8 %collective-permute-start = (bf16[16,784,128]{2,1,0:T(8,128)(2,1)S(1)}, bf16[16,784,128]{2,1,0:T(8,128)(2,1)}, u32[]{:S(2)}, u32[]{:S(2)}) collective-permute-start(bf16[16,784,128]{2,1,0:T(8,128)(2,1)S(1)} %all_to_all.21), channel_id=1, source_target_pairs={{0,1},{1,0},{2,3},{3,2},{4,5},{5,4},{6,7},{7,6},{8,9},{9,8},{10,11... | collective-permute-start | bytes 9633800 | tf_op jit(solution)/shard_map/ppermute | solution.py:50
  92.1 8.3 %all-to-all-start.2 = ((bf16[4,16,1024]{2,1,0:T(8,128)(2,1)}), bf16[4,16,1024]{2,1,0:T(8,128)(2,1)S(1)}, u32[]{:S(2)}, u32[]{:S(2)}) async-start(bf16[4,16,1024]{2,1,0:T(8,128)(2,1)} %pad_maximum_fusion), calls=%async_computation.2 | async-start | bytes 262144 | tf_op jit(solution)/shard_map/all_to_all | solution.py:64
  100.5 27.0 %copy-start.3 = (bf16[4,16,1024]{2,1,0:T(8,128)(2,1)}, bf16[4,16,1024]{2,1,0:T(8,128)(2,1)S(1)}, u32[]{:S(2)}) copy-start(bf16[4,16,1024]{2,1,0:T(8,128)(2,1)S(1)} %all-to-all-done.2) | copy-start | bytes 393220
  100.5 12.5 %collective-permute-start.2 = (bf16[64,1024]{1,0:T(8,128)(2,1)S(1)}, bf16[64,1024]{1,0:T(8,128)(2,1)S(1)}, u32[]{:S(2)}, u32[]{:S(2)}) collective-permute-start(bf16[64,1024]{1,0:T(8,128)(2,1)S(1)} %bitcast.55), channel_id=1, source_target_pairs={{0,352},{32,384},{64,416},{96,448},{128,480},{160,0},{192,32},{224... | collective-permute-start | bytes 393224 | tf_op jit(solution)/shard_map/ppermute | solution.py:108
  109.9 17.6 %collective-permute-start.1 = (bf16[64,1024]{1,0:T(8,128)(2,1)S(1)}, bf16[64,1024]{1,0:T(8,128)(2,1)}, u32[]{:S(2)}, u32[]{:S(2)}) collective-permute-start(bf16[64,1024]{1,0:T(8,128)(2,1)S(1)} %bitcast.56), channel_id=1, source_target_pairs={{0,160},{32,192},{64,224},{96,256},{128,288},{160,320},{192,352},{... | collective-permute-start | bytes 393224 | tf_op jit(solution)/shard_map/ppermute | solution.py:108
  113.0 0.7 copy-start.5
  129.3 18.5 %collective-permute-start.7 = (bf16[32,1024]{1,0:T(8,128)(2,1)}, bf16[32,1024]{1,0:T(8,128)(2,1)S(1)}, u32[]{:S(2)}, u32[]{:S(2)}) collective-permute-start(bf16[32,1024]{1,0:T(8,128)(2,1)} %get-tuple-element.9), channel_id=1, source_target_pairs={{0,416},{32,448},{64,480},{96,0},{128,32},{160,64},{192,96},{224,1... | collective-permute-start | bytes 196616 | tf_op jit(solution)/shard_map/ppermute | solution.py:108
  134.0 17.2 %collective-permute-start.8 = (bf16[32,1024]{1,0:T(8,128)(2,1)}, bf16[32,1024]{1,0:T(8,128)(2,1)S(1)}, u32[]{:S(2)}, u32[]{:S(2)}) collective-permute-start(bf16[32,1024]{1,0:T(8,128)(2,1)} %get-tuple-element.10), channel_id=1, source_target_pairs={{0,96},{32,128},{64,160},{96,192},{128,224},{160,256},{192,288},{2... | collective-permute-start | bytes 196616 | tf_op jit(solution)/shard_map/ppermute | solution.py:108
  138.4 25.3 %collective-permute-start.6 = (bf16[192,1024]{1,0:T(8,128)(2,1)}, bf16[192,1024]{1,0:T(8,128)(2,1)}, u32[]{:S(2)}, u32[]{:S(2)}) collective-permute-start(bf16[192,1024]{1,0:T(8,128)(2,1)} %get-tuple-element.8.refs_0_), channel_id=1, source_target_pairs={{0,448},{32,480},{64,0},{96,32},{128,64},{160,96},{192,128},{224,1... | collective-permute-start | bytes 1179656 | tf_op jit(solution)/shard_map/ppermute | solution.py:108
  142.1 24.1 %collective-permute-start.5 = (bf16[192,1024]{1,0:T(8,128)(2,1)}, bf16[192,1024]{1,0:T(8,128)(2,1)}, u32[]{:S(2)}, u32[]{:S(2)}) collective-permute-start(bf16[192,1024]{1,0:T(8,128)(2,1)} %get-tuple-element.8.refs_0_), channel_id=1, source_target_pairs={{0,64},{32,96},{64,128},{96,160},{128,192},{160,224},{192,256},{22... | collective-permute-start | bytes 1179656 | tf_op jit(solution)/shard_map/ppermute | solution.py:108
  147.8 26.7 %copy-start.6 = (bf16[32,1024]{1,0:T(8,128)(2,1)}, bf16[32,1024]{1,0:T(8,128)(2,1)S(1)}, u32[]{:S(2)}) copy-start(bf16[32,1024]{1,0:T(8,128)(2,1)S(1)} %collective-permute-done.7.refs_5_) | copy-start | bytes 196612
  147.8 22.4 %collective-permute-start.4 = (bf16[192,1024]{1,0:T(8,128)(2,1)}, bf16[192,1024]{1,0:T(8,128)(2,1)}, u32[]{:S(2)}, u32[]{:S(2)}) collective-permute-start(bf16[192,1024]{1,0:T(8,128)(2,1)} %get-tuple-element.8.refs_0_), channel_id=1, source_target_pairs={{0,480},{32,0},{64,32},{96,64},{128,96},{160,128},{192,160},{224,1... | collective-permute-start | bytes 1179656 | tf_op jit(solution)/shard_map/ppermute | solution.py:108
  151.2 1.9 copy-start.7
  151.2 23.2 %collective-permute-start.3 = (bf16[192,1024]{1,0:T(8,128)(2,1)}, bf16[192,1024]{1,0:T(8,128)(2,1)}, u32[]{:S(2)}, u32[]{:S(2)}) collective-permute-start(bf16[192,1024]{1,0:T(8,128)(2,1)} %get-tuple-element.8.refs_0_), channel_id=1, source_target_pairs={{0,32},{32,64},{64,96},{96,128},{128,160},{160,192},{192,224},{224... | collective-permute-start | bytes 1179656 | tf_op jit(solution)/shard_map/ppermute | solution.py:108
  190.9 13.9 %all-to-all-start.3 = ((f32[32,2,768]{2,1,0:T(2,128)}), f32[32,2,768]{2,1,0:T(2,128)S(1)}, u32[]{:S(2)}, u32[]{:S(2)}) async-start(f32[32,2,768]{2,1,0:T(2,128)} %bitcast.24), calls=%async_computation.3 | async-start | bytes 393216 | tf_op jit(solution)/shard_map/all_to_all | solution.py:298

commit v7 on v5

--- a/solution.py
+++ b/solution.py
@@ -254,15 +254,14 @@
     group = columns * capacity
     width = packed.shape[1]
     digits = jnp.stack([sent_labels // 256, sent_labels % 256]).astype(jnp.bfloat16)
-    digits = digits.reshape(2, planes, group).swapaxes(0, 1)
-    digits = jnp.pad(digits, ((0, 0), (0, 6), (0, width - group)))
+    digits = digits.reshape(2, planes, group).swapaxes(0, 1).reshape(planes, 1, 2 * group)
+    digits = jnp.pad(digits, ((0, 0), (0, 7), (0, width - 2 * group)))
     sent = jnp.concatenate([packed.reshape(planes, group, width), digits], axis=1)
     arrived = lax.all_to_all(sent, "z", split_axis=0, concat_axis=0, tiled=True)
     bundle = jnp.concatenate(
         [
             arrived[:, :group].reshape(OWN_ROWS, width),
             arrived[:, group],
-            arrived[:, group + 1],
         ],
         axis=0,
     )
@@ -270,9 +269,8 @@
     far = swap_cores(near)
     near = near.reshape(columns, -1, *bundle.shape)
     far = far.reshape(near.shape)
-    tags = near[:, 0, OWN_ROWS : OWN_ROWS + 2 * planes].astype(jnp.int32)
-    tags = tags.reshape(columns, 2, planes, width)[..., :group]
-    row_labels = tags[:, 0] * 256 + tags[:, 1] - 1
+    tags = near[:, 0, OWN_ROWS : OWN_ROWS + planes].astype(jnp.int32)
+    row_labels = tags[..., :group] * 256 + tags[..., group : 2 * group] - 1
     part = mixed.shape[1]
     assert columns * part - shard_rows < LANES
     here = lax.axis_index("x")

time: 200 us -> 200 us (level)
  waiting for transfers between devices: 36.4 us -> 47.5 us
  blocking collectives: 78 us -> 69.3 us
  starting transfers between devices: 56.5 us -> 52.4 us
    all_to_all x1 -> x0, blocking collectives: 8.09 us -> none  [exchanged_embedding(): mixed = lax.all_to_all(split, 'x', split_axis=0, concat_axis=0, tiled=True)]
    ppermute x8, starting transfers between devices: 42.6 us -> 34.9 us  [shifted(): lax.ppermute(value, 'z', [(k, (k + step) % planes) for k in range(planes)])]
    ppermute x8, waiting for transfers between devices: 28.4 us -> 34.5 us  [shifted(): lax.ppermute(value, 'z', [(k, (k + step) % planes) for k in range(planes)])]
    all_to_all x0 -> x1, waiting for transfers between devices: none -> 5 us  [exchanged_embedding(): mixed = lax.all_to_all(split, 'x', split_axis=0, concat_axis=0, tiled=True)]
    all_to_all x0 -> x1, starting transfers between devices: none -> 3.32 us  [exchanged_embedding(): mixed = lax.all_to_all(split, 'x', split_axis=0, concat_axis=0, tiled=True)]
  transfers between devices with their start and end apart: 10 -> 11, of which waited for: 5 -> 8; matrix products, arithmetic and copies ran while one was open for 1% -> 2% of each run, Pallas kernels for 1% -> 1%
where the time goes in v7:
time: 200 us; the launch traced here: 199 us
  blocking collectives  69.3 us (35%)
  starting transfers between devices  52.4 us (26%)
  waiting for transfers between devices  47.5 us (24%)
  Pallas kernels  16 us (8%)
  local copies, waits for them, and re-layouts  6.11 us (3%)
  other arithmetic  5.52 us (3%)
    all_to_all x1, blocking collectives, broadcast_all(): return lax.all_to_all(copies, axis, split_axis=0, concat_axis=0, tiled=True)  41.1 us
    ppermute x8, starting transfers between devices, shifted(): lax.ppermute(value, 'z', [(k, (k + step) % planes) for k in range(planes)])  34.9 us
    ppermute x8, waiting for transfers between devices, shifted(): lax.ppermute(value, 'z', [(k, (k + step) % planes) for k in range(planes)])  34.5 us
    all_to_all x1, blocking collectives, on_device_body(): arrived = lax.all_to_all(sent, 'z', split_axis=0, concat_axis=0, tiled=True)  28.2 us
    pallas_call x1, Pallas kernels, row_stats(): pl.pallas_call(functools.partial(stats_block, offsets=tuple((around for _...  14.1 us
    ppermute x1, starting transfers between devices, swap_cores(): return lax.ppermute(value, 'c', [(0, 1), (1, 0)])  8.7 us
    all_to_all x1, waiting for transfers between devices, on_device_body(): lax.all_to_all(copies, PLANE, split_axis=0, concat_axis=0, tiled=True)  8.04 us
    all_to_all x1, starting transfers between devices, on_device_body(): lax.all_to_all(copies, PLANE, split_axis=0, concat_axis=0, tiled=True)  5.46 us
  transfers between devices with their start and end apart: 11, of which 8 were waited for; matrix products, arithmetic and copies ran while one was open for 2% of the time, Pallas kernels for 1%

profile of v7, /device:TPU:1, one launch (start us, length us, event | category | flops | bytes accessed | tf_op | source)
XLA Modules:
  0.0 198.7 jit_solution(12121400248541704946)
XLA Ops:
  0.0 0.0 copy-start
  0.0 0.1 lt.42
  0.1 0.7 reduce.2
  0.8 0.1 reshape.209
  0.9 0.4 fusion.8
  1.3 0.8 fusion.25
  2.1 0.1 broadcast_in_dim.58
  2.2 0.1 reshape.212
  2.3 1.2 select_reduce_fusion.1
  3.5 0.1 add.92
  3.5 0.1 broadcast_in_dim.57
  3.6 0.2 sub.42
  3.9 0.7 select_reduce_fusion
  4.5 0.1 reduce_sum.50
  4.7 0.1 reshape.224
  4.8 0.0 copy-done
  4.8 1.0 fusion.4
  5.9 28.2 %all_to_all.20 = bf16[16,56,128]{2,1,0:T(8,128)(2,1)S(1)} all-to-all(bf16[16,56,128]{2,1,0:T(8,128)(2,1)S(1)} %fusion.12), channel_id=1, replica_groups=mesh['z'=16,'x'=4,'y'=4,'c'=2] {'z'}, dimensions={0} | all-to-all | bytes 458752 | tf_op jit(solution)/shard_map/all_to_all | solution.py:260
  34.2 0.4 broadcast_in_dim.63
  34.6 0.0 copy-start.3
  34.6 0.0 copy-start.7
  34.6 41.1 %all_to_all.21 = bf16[16,784,128]{2,1,0:T(8,128)(2,1)S(1)} all-to-all(bf16[16,784,128]{2,1,0:T(8,128)(2,1)S(1)} %broadcast_in_dim.63), channel_id=1, replica_groups=mesh['z'=16,'x'=4,'y'=4,'c'=2] {'x','y'}, dimensions={0} | all-to-all | bytes 6422528 | tf_op jit(solution)/shard_map/all_to_all | solution.py:28
  75.7 8.7 %collective-permute-start = (bf16[16,784,128]{2,1,0:T(8,128)(2,1)S(1)}, bf16[16,784,128]{2,1,0:T(8,128)(2,1)}, u32[]{:S(2)}, u32[]{:S(2)}) collective-permute-start(bf16[16,784,128]{2,1,0:T(8,128)(2,1)S(1)} %all_to_all.21), channel_id=1, source_target_pairs={{0,1},{1,0},{2,3},{3,2},{4,5},{5,4},{6,7},{7,6},{8,9},{9,8},{10,11... | collective-permute-start | bytes 9633800 | tf_op jit(solution)/shard_map/ppermute | solution.py:32
  84.5 0.0 copy-done.3
  84.5 0.7 pad_maximum_fusion.1
  85.1 3.3 %all-to-all-start.2 = ((bf16[4,16,1024]{2,1,0:T(8,128)(2,1)}), bf16[4,16,1024]{2,1,0:T(8,128)(2,1)S(1)}, u32[]{:S(2)}, u32[]{:S(2)}) async-start(bf16[4,16,1024]{2,1,0:T(8,128)(2,1)} %pad_maximum_fusion.1), calls=%async_computation.2 | async-start | bytes 262144 | tf_op jit(solution)/shard_map/all_to_all | solution.py:46
  88.5 5.0 %all-to-all-done.2 = bf16[4,16,1024]{2,1,0:T(8,128)(2,1)S(1)} async-done(((bf16[4,16,1024]{2,1,0:T(8,128)(2,1)}), bf16[4,16,1024]{2,1,0:T(8,128)(2,1)S(1)}, u32[]{:S(2)}, u32[]{:S(2)}) %all-to-all-start.2) | async-done | bytes 131104 | tf_op jit(solution)/shard_map/all_to_all | solution.py:46
  93.5 9.4 %collective-permute-start.2 = (bf16[64,1024]{1,0:T(8,128)(2,1)S(1)}, bf16[64,1024]{1,0:T(8,128)(2,1)S(1)}, u32[]{:S(2)}, u32[]{:S(2)}) collective-permute-start(bf16[64,1024]{1,0:T(8,128)(2,1)S(1)} %bitcast.57), channel_id=1, source_target_pairs={{0,352},{32,384},{64,416},{96,448},{128,480},{160,0},{192,32},{224... | collective-permute-start | bytes 393224 | tf_op jit(solution)/shard_map/ppermute | solution.py:90
  102.9 2.4 %collective-permute-start.1 = (bf16[64,1024]{1,0:T(8,128)(2,1)S(1)}, bf16[64,1024]{1,0:T(8,128)(2,1)}, u32[]{:S(2)}, u32[]{:S(2)}) collective-permute-start(bf16[64,1024]{1,0:T(8,128)(2,1)S(1)} %bitcast.58), channel_id=1, source_target_pairs={{0,160},{32,192},{64,224},{96,256},{128,288},{160,320},{192,352},{... | collective-permute-start | bytes 393224 | tf_op jit(solution)/shard_map/ppermute | solution.py:90
  105.2 0.0 copy-done.7
  105.2 0.6 convert_multiply_fusion
  105.8 0.2 collective-permute-done.2.above_ref
  106.0 0.7 copy-done.4
  106.7 13.8 %collective-permute-done.1.below_ref = bf16[64,1024]{1,0:T(8,128)(2,1)} collective-permute-done((bf16[64,1024]{1,0:T(8,128)(2,1)S(1)}, bf16[64,1024]{1,0:T(8,128)(2,1)}, u32[]{:S(2)}, u32[]{:S(2)}) %collective-permute-start.1) | collective-permute-done | bytes 131104 | tf_op jit(solution)/shard_map/ppermute | solution.py:90
  120.5 1.9 joined.1
  122.3 4.7 %collective-permute-start.7 = (bf16[32,1024]{1,0:T(8,128)(2,1)}, bf16[32,1024]{1,0:T(8,128)(2,1)S(1)}, u32[]{:S(2)}, u32[]{:S(2)}) collective-permute-start(bf16[32,1024]{1,0:T(8,128)(2,1)} %get-tuple-element.9), channel_id=1, source_target_pairs={{0,416},{32,448},{64,480},{96,0},{128,32},{160,64},{192,96},{224,1... | collective-permute-start | bytes 196616 | tf_op jit(solution)/shard_map/ppermute | solution.py:90
  127.0 3.9 %collective-permute-start.8 = (bf16[32,1024]{1,0:T(8,128)(2,1)}, bf16[32,1024]{1,0:T(8,128)(2,1)S(1)}, u32[]{:S(2)}, u32[]{:S(2)}) collective-permute-start(bf16[32,1024]{1,0:T(8,128)(2,1)} %get-tuple-element.10), channel_id=1, source_target_pairs={{0,96},{32,128},{64,160},{96,192},{128,224},{160,256},{192,288},{2... | collective-permute-start | bytes 196616 | tf_op jit(solution)/shard_map/ppermute | solution.py:90
  130.9 0.6 pad_add_fusion.scalars_ref
  131.5 3.7 %collective-permute-start.6 = (bf16[192,1024]{1,0:T(8,128)(2,1)}, bf16[192,1024]{1,0:T(8,128)(2,1)}, u32[]{:S(2)}, u32[]{:S(2)}) collective-permute-start(bf16[192,1024]{1,0:T(8,128)(2,1)} %get-tuple-element.8.refs_0_), channel_id=1, source_target_pairs={{0,448},{32,480},{64,0},{96,32},{128,64},{160,96},{192,128},{224,1... | collective-permute-start | bytes 1179656 | tf_op jit(solution)/shard_map/ppermute | solution.py:90
  135.2 5.7 %collective-permute-start.5 = (bf16[192,1024]{1,0:T(8,128)(2,1)}, bf16[192,1024]{1,0:T(8,128)(2,1)}, u32[]{:S(2)}, u32[]{:S(2)}) collective-permute-start(bf16[192,1024]{1,0:T(8,128)(2,1)} %get-tuple-element.8.refs_0_), channel_id=1, source_target_pairs={{0,64},{32,96},{64,128},{96,160},{128,192},{160,224},{192,256},{22... | collective-permute-start | bytes 1179656 | tf_op jit(solution)/shard_map/ppermute | solution.py:90
  140.8 0.0 collective-permute-done.7.refs_5_
  140.9 3.4 %collective-permute-start.4 = (bf16[192,1024]{1,0:T(8,128)(2,1)}, bf16[192,1024]{1,0:T(8,128)(2,1)}, u32[]{:S(2)}, u32[]{:S(2)}) collective-permute-start(bf16[192,1024]{1,0:T(8,128)(2,1)} %get-tuple-element.8.refs_0_), channel_id=1, source_target_pairs={{0,480},{32,0},{64,32},{96,64},{128,96},{160,128},{192,160},{224,1... | collective-permute-start | bytes 1179656 | tf_op jit(solution)/shard_map/ppermute | solution.py:90
  144.3 0.0 collective-permute-done.8.refs_6_
  144.3 1.9 collective-permute-start.3
  146.2 0.1 and_select_fusion
  146.3 0.7 reshape_reshape.3.labels_ref
  147.0 9.7 %collective-permute-done.6.refs_4_ = bf16[192,1024]{1,0:T(8,128)(2,1)} collective-permute-done((bf16[192,1024]{1,0:T(8,128)(2,1)}, bf16[192,1024]{1,0:T(8,128)(2,1)}, u32[]{:S(2)}, u32[]{:S(2)}) %collective-permute-start.6) | collective-permute-done | bytes 393248 | tf_op jit(solution)/shard_map/ppermute | solution.py:90
  156.8 2.5 %collective-permute-done.5.refs_3_ = bf16[192,1024]{1,0:T(8,128)(2,1)} collective-permute-done((bf16[192,1024]{1,0:T(8,128)(2,1)}, bf16[192,1024]{1,0:T(8,128)(2,1)}, u32[]{:S(2)}, u32[]{:S(2)}) %collective-permute-start.5) | collective-permute-done | bytes 393248 | tf_op jit(solution)/shard_map/ppermute | solution.py:90
  159.2 4.1 %collective-permute-done.4.refs_2_ = bf16[192,1024]{1,0:T(8,128)(2,1)} collective-permute-done((bf16[192,1024]{1,0:T(8,128)(2,1)}, bf16[192,1024]{1,0:T(8,128)(2,1)}, u32[]{:S(2)}, u32[]{:S(2)}) %collective-permute-start.4) | collective-permute-done | bytes 393248 | tf_op jit(solution)/shard_map/ppermute | solution.py:90
  163.3 4.2 %collective-permute-done.3.refs_1_ = bf16[192,1024]{1,0:T(8,128)(2,1)} collective-permute-done((bf16[192,1024]{1,0:T(8,128)(2,1)}, bf16[192,1024]{1,0:T(8,128)(2,1)}, u32[]{:S(2)}, u32[]{:S(2)}) %collective-permute-start.3) | collective-permute-done | bytes 393248 | tf_op jit(solution)/shard_map/ppermute | solution.py:90
  167.5 0.0 collective-permute-done
  167.5 0.0 copy-done.1
  167.6 14.1 %row_stats.1 = f32[2,3072]{1,0:T(2,128)} custom-call(s32[3]{0:T(128)} %pad_add_fusion.scalars_ref, bf16[4,4,784,128]{3,2,1,0:T(8,128)(2,1)} %bitcast.54, bf16[4,4,784,128]{3,2,1,0:T(8,128)(2,1)} %bitcast.15.far_ref, f32[1,1024]{1,0:T(1,128)} %bitcast.64, s32[1,3072]{1,0:T(1,128)} %reshape_reshape.3.labels_ref, bf16[192,1024]{1,0:T(8,128)(2,1)} %get-tuple-element.8.refs_0_, ...), custom_call_target="tpu_custom_call" | custom-call | tf_op jit(solution)/shard_map/row_stats/pallas_call | solution.py:223
  181.7 1.1 reshape.220
  182.8 0.2 copy.40
  183.0 0.3 broadcast_in_dim.64
  183.2 0.7 broadcast_in_dim.65
  184.0 5.5 %all-to-all-start.3 = ((f32[32,2,768]{2,1,0:T(2,128)}), f32[32,2,768]{2,1,0:T(2,128)S(1)}, u32[]{:S(2)}, u32[]{:S(2)}) async-start(f32[32,2,768]{2,1,0:T(2,128)} %bitcast.24), calls=%async_computation.3 | async-start | bytes 393216 | tf_op jit(solution)/shard_map/all_to_all | solution.py:286
  189.4 0.1 copy.43
  189.6 0.1 copy.39
  189.7 0.1 ge.22
  189.8 8.0 %all-to-all-done.3 = f32[32,2,768]{2,1,0:T(2,128)S(1)} async-done(((f32[32,2,768]{2,1,0:T(2,128)}), f32[32,2,768]{2,1,0:T(2,128)S(1)}, u32[]{:S(2)}, u32[]{:S(2)}) %all-to-all-start.3) | async-done | bytes 196640 | tf_op jit(solution)/shard_map/all_to_all | solution.py:286
  197.8 0.2 slice_reduce_fusion.1
  198.1 0.6 subtract_select_fusion
  (28 shorter events, 0.3 us)
Async XLA Ops:
  0.0 4.8 %copy-start = (bf16[9,80,128]{2,1,0:T(8,128)(2,1)S(1)}, bf16[9,80,128]{2,1,0:T(8,128)(2,1)}, u32[]{:S(2)}) copy-start(bf16[9,80,128]{2,1,0:T(8,128)(2,1)} %param.9) | copy-start | bytes 552964
  34.6 49.9 %copy-start.3 = (bf16[4016,16]{0,1:T(8,128)(2,1)S(1)}, bf16[4016,16]{0,1:T(8,128)(2,1)}, u32[]{:S(2)}) copy-start(bf16[4016,16]{0,1:T(8,128)(2,1)} %param.11) | copy-start | bytes 385540
  34.6 70.7 %copy-start.7 = (bf16[1024]{0:T(1024)(128)(2,1)S(1)}, bf16[1024]{0:T(1024)(128)(2,1)}, u32[]{:S(2)}) copy-start(bf16[1024]{0:T(1024)(128)(2,1)} %param.10) | copy-start | bytes 6148
  75.7 91.8 %copy-start.1 = (bf16[16,784,128]{2,1,0:T(8,128)(2,1)}, bf16[16,784,128]{2,1,0:T(8,128)(2,1)S(1)}, u32[]{:S(2)}) copy-start(bf16[16,784,128]{2,1,0:T(8,128)(2,1)S(1)} %all_to_all.21) | copy-start | bytes 9633796
  75.7 91.8 %collective-permute-start = (bf16[16,784,128]{2,1,0:T(8,128)(2,1)S(1)}, bf16[16,784,128]{2,1,0:T(8,128)(2,1)}, u32[]{:S(2)}, u32[]{:S(2)}) collective-permute-start(bf16[16,784,128]{2,1,0:T(8,128)(2,1)S(1)} %all_to_all.21), channel_id=1, source_target_pairs={{0,1},{1,0},{2,3},{3,2},{4,5},{5,4},{6,7},{7,6},{8,9},{9,8},{10,11... | collective-permute-start | bytes 9633800 | tf_op jit(solution)/shard_map/ppermute | solution.py:32
  85.1 8.3 %all-to-all-start.2 = ((bf16[4,16,1024]{2,1,0:T(8,128)(2,1)}), bf16[4,16,1024]{2,1,0:T(8,128)(2,1)S(1)}, u32[]{:S(2)}, u32[]{:S(2)}) async-start(bf16[4,16,1024]{2,1,0:T(8,128)(2,1)} %pad_maximum_fusion.1), calls=%async_computation.2 | async-start | bytes 262144 | tf_op jit(solution)/shard_map/all_to_all | solution.py:46
  93.5 27.0 %copy-start.2 = (bf16[4,16,1024]{2,1,0:T(8,128)(2,1)}, bf16[4,16,1024]{2,1,0:T(8,128)(2,1)S(1)}, u32[]{:S(2)}) copy-start(bf16[4,16,1024]{2,1,0:T(8,128)(2,1)S(1)} %all-to-all-done.2) | copy-start | bytes 393220
  93.5 12.5 %collective-permute-start.2 = (bf16[64,1024]{1,0:T(8,128)(2,1)S(1)}, bf16[64,1024]{1,0:T(8,128)(2,1)S(1)}, u32[]{:S(2)}, u32[]{:S(2)}) collective-permute-start(bf16[64,1024]{1,0:T(8,128)(2,1)S(1)} %bitcast.57), channel_id=1, source_target_pairs={{0,352},{32,384},{64,416},{96,448},{128,480},{160,0},{192,32},{224... | collective-permute-start | bytes 393224 | tf_op jit(solution)/shard_map/ppermute | solution.py:90
  102.9 17.6 %collective-permute-start.1 = (bf16[64,1024]{1,0:T(8,128)(2,1)S(1)}, bf16[64,1024]{1,0:T(8,128)(2,1)}, u32[]{:S(2)}, u32[]{:S(2)}) collective-permute-start(bf16[64,1024]{1,0:T(8,128)(2,1)S(1)} %bitcast.58), channel_id=1, source_target_pairs={{0,160},{32,192},{64,224},{96,256},{128,288},{160,320},{192,352},{... | collective-permute-start | bytes 393224 | tf_op jit(solution)/shard_map/ppermute | solution.py:90
  106.0 0.7 copy-start.4
  122.3 18.5 %collective-permute-start.7 = (bf16[32,1024]{1,0:T(8,128)(2,1)}, bf16[32,1024]{1,0:T(8,128)(2,1)S(1)}, u32[]{:S(2)}, u32[]{:S(2)}) collective-permute-start(bf16[32,1024]{1,0:T(8,128)(2,1)} %get-tuple-element.9), channel_id=1, source_target_pairs={{0,416},{32,448},{64,480},{96,0},{128,32},{160,64},{192,96},{224,1... | collective-permute-start | bytes 196616 | tf_op jit(solution)/shard_map/ppermute | solution.py:90
  127.0 17.3 %collective-permute-start.8 = (bf16[32,1024]{1,0:T(8,128)(2,1)}, bf16[32,1024]{1,0:T(8,128)(2,1)S(1)}, u32[]{:S(2)}, u32[]{:S(2)}) collective-permute-start(bf16[32,1024]{1,0:T(8,128)(2,1)} %get-tuple-element.10), channel_id=1, source_target_pairs={{0,96},{32,128},{64,160},{96,192},{128,224},{160,256},{192,288},{2... | collective-permute-start | bytes 196616 | tf_op jit(solution)/shard_map/ppermute | solution.py:90
  131.5 25.3 %collective-permute-start.6 = (bf16[192,1024]{1,0:T(8,128)(2,1)}, bf16[192,1024]{1,0:T(8,128)(2,1)}, u32[]{:S(2)}, u32[]{:S(2)}) collective-permute-start(bf16[192,1024]{1,0:T(8,128)(2,1)} %get-tuple-element.8.refs_0_), channel_id=1, source_target_pairs={{0,448},{32,480},{64,0},{96,32},{128,64},{160,96},{192,128},{224,1... | collective-permute-start | bytes 1179656 | tf_op jit(solution)/shard_map/ppermute | solution.py:90
  135.2 24.1 %collective-permute-start.5 = (bf16[192,1024]{1,0:T(8,128)(2,1)}, bf16[192,1024]{1,0:T(8,128)(2,1)}, u32[]{:S(2)}, u32[]{:S(2)}) collective-permute-start(bf16[192,1024]{1,0:T(8,128)(2,1)} %get-tuple-element.8.refs_0_), channel_id=1, source_target_pairs={{0,64},{32,96},{64,128},{96,160},{128,192},{160,224},{192,256},{22... | collective-permute-start | bytes 1179656 | tf_op jit(solution)/shard_map/ppermute | solution.py:90
  140.8 26.7 %copy-start.5 = (bf16[32,1024]{1,0:T(8,128)(2,1)}, bf16[32,1024]{1,0:T(8,128)(2,1)S(1)}, u32[]{:S(2)}) copy-start(bf16[32,1024]{1,0:T(8,128)(2,1)S(1)} %collective-permute-done.7.refs_5_) | copy-start | bytes 196612
  140.9 22.4 %collective-permute-start.4 = (bf16[192,1024]{1,0:T(8,128)(2,1)}, bf16[192,1024]{1,0:T(8,128)(2,1)}, u32[]{:S(2)}, u32[]{:S(2)}) collective-permute-start(bf16[192,1024]{1,0:T(8,128)(2,1)} %get-tuple-element.8.refs_0_), channel_id=1, source_target_pairs={{0,480},{32,0},{64,32},{96,64},{128,96},{160,128},{192,160},{224,1... | collective-permute-start | bytes 1179656 | tf_op jit(solution)/shard_map/ppermute | solution.py:90
  144.3 1.9 copy-start.6
  144.3 23.2 %collective-permute-start.3 = (bf16[192,1024]{1,0:T(8,128)(2,1)}, bf16[192,1024]{1,0:T(8,128)(2,1)}, u32[]{:S(2)}, u32[]{:S(2)}) collective-permute-start(bf16[192,1024]{1,0:T(8,128)(2,1)} %get-tuple-element.8.refs_0_), channel_id=1, source_target_pairs={{0,32},{32,64},{64,96},{96,128},{128,160},{160,192},{192,224},{224... | collective-permute-start | bytes 1179656 | tf_op jit(solution)/shard_map/ppermute | solution.py:90
  184.0 13.9 %all-to-all-start.3 = ((f32[32,2,768]{2,1,0:T(2,128)}), f32[32,2,768]{2,1,0:T(2,128)S(1)}, u32[]{:S(2)}, u32[]{:S(2)}) async-start(f32[32,2,768]{2,1,0:T(2,128)} %bitcast.24), calls=%async_computation.3 | async-start | bytes 393216 | tf_op jit(solution)/shard_map/all_to_all | solution.py:286
